TPU v7x, 128 devices: a whole 4x4x4 slice. The times are simulated.
128 devices in a mesh: facet: 8 (over z, core), chan: 16 (over x, y).
Axes of the slice: x: 4, y: 4, z: 4, core: 2. Of those that a mesh axis runs over, the one named last changes fastest.
Arguments:
- visibilities: bfloat16 [2, 16, 512, 128, 128], P(None, None, None, ('facet', 'chan')), may hold values from -12 to 12
- kernels: bfloat16 [32, 256, 512], replicated, may hold values from -0.25 to 0.25
- delays: float32 [16, 512, 128], P('facet'), may hold values from -4 to 4
- tile_of: int32 [16, 512], P('facet'), may hold values from 0 to 255
- plane_of: int32 [16, 512], P('facet'), may hold values from 0 to 31
- counts: int32 [16], P('facet'), may hold values from 128 to 512
- neighbours: int32 [16, 4], replicated, may hold values from 0 to 15, as said below
Outputs:
- joined_grids: float32 [256, 16, 16, 512], P('chan', 'facet')
Inputs may be any that keep to these rules, and one draw needn't show every extreme that they name: `neighbours`: each row names 4 different facets, none of them its own.
All inputs are finite; a program needn't handle non-finite values.
Results may differ from a plain program's by a relative error of at most 0.0043.
Values may be sent and summed in bfloat16 or wider, within the bound.
No kernel may reach another device: no remote copies, remote signals or barrier semaphores. Data moves between devices by JAX's collectives and lax.ppermute only.
A program may use at most 128 MiB of HBM per device.

v0:
```python
import math

import jax
import jax.numpy as jnp
from jax import lax
from jax.sharding import PartitionSpec as P

AVG = 8
TS = 16
NT_DEV = 16
GROUP = 8
EDGE = 4


HIGHEST = lax.Precision.HIGHEST


def in_blocks(x, dim, length):
    shape = x.shape
    parts = x.reshape(*shape[:dim], length, shape[dim] // length, *shape[dim + 1 :])
    return jnp.moveaxis(parts, dim, 0)


def sum_at_owner(x, axis, dim):
    parts = in_blocks(x, dim, lax.axis_size(axis))
    arrived = lax.all_to_all(parts, axis, split_axis=0, concat_axis=0, tiled=True)
    return arrived.astype(jnp.float32).sum(axis=0)


def copy_for_each(x, axis):
    copies = jnp.broadcast_to(x, (lax.axis_size(axis), *x.shape))
    return lax.all_to_all(copies, axis, split_axis=0, concat_axis=0, tiled=True)


def laid_out(parts, dim):
    shape = list(parts.shape[1:])
    shape[dim] *= parts.shape[0]
    return jnp.moveaxis(parts, 0, dim).reshape(shape)


def collect(x, axis, dim):
    parts = copy_for_each(x, axis)
    return laid_out(parts, dim)


def average_group(vis_piece, delay_piece, freq_turn, avg_matrix):
    vis_float = vis_piece.astype(jnp.float32)
    phase_angle = delay_piece[:, None, :] * freq_turn[None, :, None]
    cosine = jnp.cos(phase_angle)
    sine_part = jnp.sin(phase_angle)
    rot_real = vis_float[0] * cosine - vis_float[1] * sine_part
    rot_imag = vis_float[0] * sine_part + vis_float[1] * cosine
    avg_real = jnp.einsum("oc,gcv->gov", avg_matrix, rot_real, precision=HIGHEST)
    avg_imag = jnp.einsum("oc,gcv->gov", avg_matrix, rot_imag, precision=HIGHEST)
    return jnp.concatenate([avg_real, avg_imag], axis=-1).astype(jnp.bfloat16)


def project_rows(row_list, plane_list, kernels):
    products = []
    for row_item, plane_item in zip(row_list, plane_list):
        matrix = lax.dynamic_index_in_dim(kernels, plane_item, 0, keepdims=False)
        products.append(jnp.dot(row_item, matrix, preferred_element_type=jnp.float32))
    return jnp.stack(products, axis=0)


def add_tiles(grid_acc, contrib, tile_piece, weight, n_tiles):
    table = (tile_piece[None, :] == jnp.arange(n_tiles, dtype=jnp.int32)[:, None]).astype(
        jnp.float32
    ) * weight[None, :]
    return grid_acc + jnp.einsum("tg,gcx->tcx", table, contrib, precision=HIGHEST)


def grid_facet(
    vis_slot,
    delay_slot,
    tiles_slot,
    planes_slot,
    live_count,
    kernels,
    freq_turn,
    avg_matrix,
    n_tiles,
):
    group_size = GROUP
    out_chan = avg_matrix.shape[0]
    wide_cells = kernels.shape[2]

    def accumulate(step_index, grid_acc):
        begin_row = step_index * group_size
        vis_piece = lax.dynamic_slice_in_dim(vis_slot, begin_row, group_size, 1)
        delay_piece = lax.dynamic_slice_in_dim(delay_slot, begin_row, group_size, 0)
        avg_rows = average_group(vis_piece, delay_piece, freq_turn, avg_matrix)
        plane_piece = lax.dynamic_slice_in_dim(planes_slot, begin_row, group_size, 0)
        contrib = project_rows(
            [avg_rows[g] for g in range(group_size)],
            [plane_piece[g] for g in range(group_size)],
            kernels,
        )
        block_ids = begin_row + jnp.arange(group_size, dtype=jnp.int32)
        live_mask = (block_ids < live_count).astype(jnp.float32)
        tile_piece = lax.dynamic_slice_in_dim(tiles_slot, begin_row, group_size, 0)
        return add_tiles(grid_acc, contrib, tile_piece, live_mask, n_tiles)

    trip_count = (live_count + group_size - 1) // group_size
    start_grid = jnp.zeros((n_tiles, out_chan, wide_cells), jnp.float32)
    return lax.fori_loop(0, trip_count, accumulate, start_grid)


def local(visibilities, kernels, delays, tile_of, plane_of, counts, neighbours):
    n_facet = lax.axis_size("facet")
    n_chan = lax.axis_size("chan")
    facet_index = lax.axis_index("facet")
    chan_index = lax.axis_index("chan")
    halves, facets, blocks, ch_dev, block_vis = visibilities.shape
    fac_dev = facets // n_facet
    blk_dev = blocks // n_chan
    channels = ch_dev * n_facet * n_chan
    out_chan = channels // AVG
    tile_cells = kernels.shape[2] // 2
    n_tiles = NT_DEV * n_chan
    edge_cells = EDGE * TS
    reshaped = visibilities.reshape(halves, n_facet, fac_dev, blk_dev, n_chan, ch_dev, block_vis)
    arranged = jnp.transpose(reshaped, (0, 1, 4, 2, 3, 5, 6))
    my_delays = lax.dynamic_index_in_dim(
        delays.reshape(fac_dev, blk_dev, n_chan, block_vis), chan_index, 2, keepdims=False
    )
    my_tiles = lax.dynamic_index_in_dim(
        tile_of.reshape(fac_dev, blk_dev, n_chan), chan_index, 2, keepdims=False
    )
    my_planes = lax.dynamic_index_in_dim(
        plane_of.reshape(fac_dev, blk_dev, n_chan), chan_index, 2, keepdims=False
    )
    my_live = jnp.clip((counts - chan_index + n_chan - 1) // n_chan, 0, blk_dev)
    position = jnp.arange(channels, dtype=jnp.int32)
    flattened = arranged.reshape(halves, n_facet * n_chan, fac_dev, blk_dev, ch_dev, block_vis)
    received = lax.all_to_all(flattened, ("facet", "chan"), split_axis=1, concat_axis=4, tiled=True)
    local_vis = received.reshape(halves, fac_dev, blk_dev, channels, block_vis)
    freq_turn = 2.0 * math.pi * (1.0 + 0.5 * position.astype(jnp.float32) / channels)
    avg_matrix = (
        position[None, :] // AVG == jnp.arange(out_chan, dtype=jnp.int32)[:, None]
    ).astype(jnp.float32) / AVG
    facet_grids = []
    for facet_slot in range(fac_dev):
        facet_grids.append(
            grid_facet(
                local_vis[:, facet_slot],
                my_delays[facet_slot],
                my_tiles[facet_slot],
                my_planes[facet_slot],
                my_live[facet_slot],
                kernels,
                freq_turn,
                avg_matrix,
                n_tiles,
            )
        )
    stacked = jnp.stack(facet_grids, axis=1)
    summed = sum_at_owner(stacked.astype(jnp.bfloat16), "chan", 0)
    strips = jnp.concatenate(
        [summed[..., :edge_cells], summed[..., tile_cells : tile_cells + edge_cells]], axis=-1
    )
    gathered = collect(strips.astype(jnp.bfloat16), "facet", 1).astype(strips.dtype)
    my_neighbours = lax.dynamic_slice_in_dim(neighbours, facet_index * fac_dev, fac_dev, 0)
    adjacency = jnp.sum(
        (my_neighbours[:, :, None] == jnp.arange(facets, dtype=jnp.int32)[None, None, :]).astype(
            jnp.float32
        ),
        axis=1,
    )
    blended = 0.25 * jnp.einsum("fg,tgcx->tfcx", adjacency, gathered, precision=HIGHEST)
    joined = summed.at[..., tile_cells - edge_cells : tile_cells].add(blended[..., :edge_cells])
    joined = joined.at[..., 2 * tile_cells - edge_cells :].add(blended[..., edge_cells:])
    return joined


def solution(mesh):
    return jax.shard_map(
        local,
        mesh=mesh,
        in_specs=(
            P(None, None, None, ("facet", "chan"), None),
            P(),
            P("facet", None, None),
            P("facet", None),
            P("facet", None),
            P("facet"),
            P(),
        ),
        out_specs=P("chan", "facet", None, None),
        check_vma=False,
    )
```

profile of v0, /device:TPU:1, one launch (start us, length us, event | category | flops | bytes accessed | tf_op | source)
XLA Modules:
  0.0 625.6 jit_solution(14528997313077175508)
XLA Ops:
  0.0 5.4 copy.54
  5.4 11.9 %all-to-all-start = ((bf16[2,128,2,32,1,128]{5,3,0,2,4,1:T(8,128)(2,1)}), bf16[2,128,2,32,1,128]{5,3,0,2,4,1:T(8,128)(2,1)}, u32[]{:S(2)}, u32[]{:S(2)}) async-start(bf16[2,128,2,32,1,128]{5,3,0,2,4,1:T(8,128)(2,1)} %bitcast.427), calls=%async_computation | async-start | bytes 8388608 | tf_op jit(solution)/shard_map/all_to_all | solution.py:136
  20.7 49.0 %all-to-all-done = bf16[2,128,2,32,1,128]{5,3,0,2,4,1:T(8,128)(2,1)} async-done(((bf16[2,128,2,32,1,128]{5,3,0,2,4,1:T(8,128)(2,1)}), bf16[2,128,2,32,1,128]{5,3,0,2,4,1:T(8,128)(2,1)}, u32[]{:S(2)}, u32[]{:S(2)}) %all-to-all-start) | async-done | bytes 4194336 | tf_op jit(solution)/shard_map/all_to_all | solution.py:136
  69.7 4.6 slice_bitcast_fusion.13
  74.3 4.3 broadcast.125.clone.1
  78.5 85.1 %while.26 = (s32[]{:T(128)}, f32[256,16,512]{2,0,1:T(8,128)}, s32[]{:T(128)}, s32[32]{0:T(128)S(1)}, s32[]{:T(128)}, /*index=5*/bf16[2,32,128,128]{3,1,0,2:T(8,1...) while((s32[]{:T(128)}, f32[256,16,512]{2,0,1:T(8,128)}, ...), condition=%wide.region_1.2_spmd.clone.clone, body=%wide.region_0.1_spmd.clone.clone.sunk | while | flops 288797216 | bytes 24726812 | solution.py:106
  82.7 2.3 fusion.307
  85.0 2.3 fusion.308
  87.4 1.1 fusion.309
  90.2 1.1 fusion.310
  93.2 1.1 fusion.311
  96.3 1.1 fusion.312
  99.1 1.1 fusion.313
  109.6 11.4 %convolution_add_fusion.4 = f32[256,16,512]{2,0,1:T(8,128)} fusion(f32[256,16,512]{2,0,1:T(8,128)} %get-tuple-element.600, f32[8,16,512]{2,1,0:T(8,128)S(1)} %fusion.316, f32[8]{0:T(128)S(1)} %compare_convert_fusion.4, s32[8]{0:T(128)S(1)} %dynamic_slice.243), kind=kOutput, calls=%fused_computation.4.clone.1 | convolution fusion | flops 203427840 | bytes 17039424 | tf_op jit(solution)/shard_map/while/body/tg,gcx->tcx/dot_general | solution.py:70
  124.9 2.3 fusion.307
  127.2 2.3 fusion.308
  129.5 1.1 fusion.309
  132.3 1.1 fusion.310
  135.3 1.1 fusion.311
  141.3 1.1 fusion.313
  150.0 1.1 fusion.316
  151.8 11.4 %convolution_add_fusion.4 = f32[256,16,512]{2,0,1:T(8,128)} fusion(f32[256,16,512]{2,0,1:T(8,128)} %get-tuple-element.600, f32[8,16,512]{2,1,0:T(8,128)S(1)} %fusion.316, f32[8]{0:T(128)S(1)} %compare_convert_fusion.4, s32[8]{0:T(128)S(1)} %dynamic_slice.243), kind=kOutput, calls=%fused_computation.4.clone.1 | convolution fusion | flops 203427840 | bytes 17039424 | tf_op jit(solution)/shard_map/while/body/tg,gcx->tcx/dot_general | solution.py:70
  163.6 9.8 %copy.80 = bf16[256,16,512]{2,1,0:T(8,128)(2,1)} copy(f32[256,16,512]{2,0,1:T(8,128)} %get-tuple-element.151) | data formatting | bytes 12582912 | tf_op jit(solution)/shard_map/while | solution.py:106
  173.4 4.3 broadcast.125.clone
  177.7 83.7 %while.27 = (s32[]{:T(128)}, f32[256,16,512]{2,0,1:T(8,128)}, s32[]{:T(128)}, s32[32]{0:T(128)S(1)}, s32[]{:T(128)}, /*index=5*/bf16[2,32,128,128]{3,1,0,2:T(8,1...) while((s32[]{:T(128)}, f32[256,16,512]{2,0,1:T(8,128)}, ...), condition=%wide.region_3.4_spmd.clone.clone, body=%wide.region_2.3_spmd.clone.clone.sunk | while | flops 288797216 | bytes 24726812 | solution.py:106
  180.9 2.3 fusion.340
  183.2 2.3 fusion.341
  185.5 1.1 fusion.342
  191.3 1.1 fusion.344
  203.2 1.1 fusion.348
  208.2 11.4 %convolution_add_fusion.5 = f32[256,16,512]{2,0,1:T(8,128)} fusion(f32[256,16,512]{2,0,1:T(8,128)} %get-tuple-element.558, f32[8,16,512]{2,1,0:T(8,128)S(1)} %fusion.349, f32[8]{0:T(128)S(1)} %compare_convert_fusion.5, s32[8]{0:T(128)S(1)} %dynamic_slice.255), kind=kOutput, calls=%fused_computation.130.clone.1 | convolution fusion | flops 203427840 | bytes 17039424 | tf_op jit(solution)/shard_map/while/body/tg,gcx->tcx/dot_general | solution.py:70
  222.5 2.3 fusion.340
  224.9 2.3 fusion.341
  227.2 1.1 fusion.342
  232.9 1.1 fusion.344
  244.8 1.1 fusion.348
  249.9 11.4 %convolution_add_fusion.5 = f32[256,16,512]{2,0,1:T(8,128)} fusion(f32[256,16,512]{2,0,1:T(8,128)} %get-tuple-element.558, f32[8,16,512]{2,1,0:T(8,128)S(1)} %fusion.349, f32[8]{0:T(128)S(1)} %compare_convert_fusion.5, s32[8]{0:T(128)S(1)} %dynamic_slice.255), kind=kOutput, calls=%fused_computation.130.clone.1 | convolution fusion | flops 203427840 | bytes 17039424 | tf_op jit(solution)/shard_map/while/body/tg,gcx->tcx/dot_general | solution.py:70
  261.4 9.9 %copy.79 = bf16[256,16,512]{2,1,0:T(8,128)(2,1)} copy(f32[256,16,512]{2,0,1:T(8,128)} %get-tuple-element.152) | data formatting | bytes 12582912 | tf_op jit(solution)/shard_map/while | solution.py:106
  271.4 6.2 pad_maximum_fusion.2
  277.6 15.4 %copy.59 = bf16[16,16,2,16,512]{4,1,3,2,0:T(8,128)(2,1)} copy(bf16[16,16,2,16,512]{4,3,1,0,2:T(8,128)(2,1)} %pad_maximum_fusion.2) | data formatting | bytes 16777216 | tf_op jit(solution)/shard_map/stack | solution.py:157
  292.9 54.9 %all_to_all.25 = bf16[16,16,2,16,512]{4,1,3,2,0:T(8,128)(2,1)S(1)} all-to-all(bf16[16,16,2,16,512]{4,1,3,2,0:T(8,128)(2,1)} %copy.59), channel_id=1, replica_groups=mesh['facet'=8,'chan'=16] {'chan'}, dimensions={0} | all-to-all | bytes 16777216 | tf_op jit(solution)/shard_map/all_to_all | solution.py:26
  347.8 2.0 convert_reduce_fusion
  350.3 1.7 broadcast_in_dim.2
  351.9 169.7 %all-to-all-start.2 = ((bf16[8,16,2,16,128]{4,2,3,1,0:T(2,128)(2,1)}), bf16[8,16,2,16,128]{4,2,3,1,0:T(2,128)(2,1)S(1)}, u32[]{:S(2)}, u32[]{:S(2)}) async-start(bf16[8,16,2,16,128]{4,2,3,1,0:T(2,128)(2,1)} %broadcast_in_dim.2), calls=%async_computation.2 | async-start | bytes 2097152 | tf_op jit(solution)/shard_map/all_to_all | solution.py:32
  522.7 13.9 %all-to-all-done.2 = bf16[8,16,2,16,128]{4,2,3,1,0:T(2,128)(2,1)S(1)} async-done(((bf16[8,16,2,16,128]{4,2,3,1,0:T(2,128)(2,1)}), bf16[8,16,2,16,128]{4,2,3,1,0:T(2,128)(2,1)S(1)}, u32[]{:S(2)}, u32[]{:S(2)}) %all-to-all-start.2) | async-done | bytes 1048608 | tf_op jit(solution)/shard_map/all_to_all | solution.py:32
  538.4 42.6 %scatter-add.6 = f32[16,2,16,512]{3,1,2,0:T(2,128)S(1)} dynamic-update-slice(f32[16,2,16,512]{3,1,2,0:T(2,128)S(1)} %copy.65, f32[16,2,16,64]{3,1,2,0:T(2,128)S(1)} %slice_add_fusion.1, s32[]{:T(128)} %constant.188.clone.1, s32[]{:T(128)} %constant.188.clone.1, s32[]{:T(128)} %constant.188.clone.1, s32[]{:T(128)} %constant.207.clone.1) | dynamic-update-slice | bytes 262148 | tf_op jit(solution)/shard_map/scatter-add | solution.py:171
  581.7 42.3 %scatter-add.9 = f32[16,2,16,512]{3,1,2,0:T(2,128)S(1)} dynamic-update-slice(f32[16,2,16,512]{3,1,2,0:T(2,128)S(1)} %scatter-add.6, f32[16,2,16,64]{3,1,2,0:T(2,128)S(1)} %slice_add_fusion, s32[]{:T(128)} %constant.188.clone.1, s32[]{:T(128)} %constant.188.clone.1, s32[]{:T(128)} %constant.188.clone.1, s32[]{:T(128)} %constant.208.clone.1) | dynamic-update-slice | bytes 262148 | tf_op jit(solution)/shard_map/scatter-add | solution.py:172
  624.0 1.2 copy.66
  (77 shorter events, 32.3 us)
Async XLA Ops:
  0.0 521.6 %copy-start = (s32[16,4]{0,1:T(4,128)S(1)}, s32[16,4]{0,1:T(4,128)}, u32[]{:S(2)}) copy-start(s32[16,4]{0,1:T(4,128)} %param.21) | copy-start | bytes 772
  0.0 17.3 %copy-start.4 = (s32[2]{0:T(128)S(1)}, s32[2]{0:T(128)}, u32[]{:S(2)}) copy-start(s32[2]{0:T(128)} %param.20) | copy-start | bytes 28
  0.0 19.3 %copy-start.2 = (s32[2,512]{1,0:T(2,128)S(1)}, s32[2,512]{1,0:T(2,128)}, u32[]{:S(2)}) copy-start(s32[2,512]{1,0:T(2,128)} %param.18) | copy-start | bytes 12292
  0.0 19.4 %copy-start.3 = (s32[2,512]{1,0:T(2,128)S(1)}, s32[2,512]{1,0:T(2,128)}, u32[]{:S(2)}) copy-start(s32[2,512]{1,0:T(2,128)} %param.19) | copy-start | bytes 12292
  5.4 64.3 %all-to-all-start = ((bf16[2,128,2,32,1,128]{5,3,0,2,4,1:T(8,128)(2,1)}), bf16[2,128,2,32,1,128]{5,3,0,2,4,1:T(8,128)(2,1)}, u32[]{:S(2)}, u32[]{:S(2)}) async-start(bf16[2,128,2,32,1,128]{5,3,0,2,4,1:T(8,128)(2,1)} %bitcast.427), calls=%async_computation | async-start | bytes 8388608 | tf_op jit(solution)/shard_map/all_to_all | solution.py:136
  261.4 9.9 %copy-start.1 = (bf16[256,16,512]{2,1,0:T(8,128)(2,1)S(1)}, bf16[256,16,512]{2,1,0:T(8,128)(2,1)}, u32[]{:S(2)}) copy-start(bf16[256,16,512]{2,1,0:T(8,128)(2,1)} %copy.80) | copy-start | bytes 12582916
  351.9 184.6 %all-to-all-start.2 = ((bf16[8,16,2,16,128]{4,2,3,1,0:T(2,128)(2,1)}), bf16[8,16,2,16,128]{4,2,3,1,0:T(2,128)(2,1)S(1)}, u32[]{:S(2)}, u32[]{:S(2)}) async-start(bf16[8,16,2,16,128]{4,2,3,1,0:T(2,128)(2,1)} %broadcast_in_dim.2), calls=%async_computation.2 | async-start | bytes 2097152 | tf_op jit(solution)/shard_map/all_to_all | solution.py:32
where the time goes:
time: 613 us; the launch traced here: 626 us
  starting transfers between devices  182 us (30%)
  local copies, waits for them, and re-layouts  151 us (25%)
  matrix products  99.7 us (16%)
  waiting for transfers between devices  62.9 us (10%)
  loops' own time  60.8 us (10%)
  blocking collectives  54.9 us (9%)
  other arithmetic  12.4 us (2%)
    all_to_all x1, starting transfers between devices, copy_for_each(): return lax.all_to_all(copies, axis, split_axis=0, concat_axis=0, tiled=True)  170 us
    another operation x2, loops' own time, grid_facet(): return lax.fori_loop(0, trip_count, accumulate, start_grid)  60.8 us
    all_to_all x1, blocking collectives, sum_at_owner(): lax.all_to_all(parts, axis, split_axis=0, concat_axis=0, tiled=True)  54.9 us
    all_to_all x1, waiting for transfers between devices, local(): lax.all_to_all(flattened, ('facet', 'chan'), split_axis=1, concat_axis=4,...  49 us
    dot_general x4, matrix products, add_tiles(): jnp.einsum('tg,gcx->tcx', table, contrib, precision=HIGHEST)  45.5 us
    scatter-add x2, local copies, waits for them, and re-layouts, local(): joined.at[..., 2 * tile_cells - edge_cells:].add(blended[..., edge_cells:])  43.5 us
    scatter-add x1, local copies, waits for them, and re-layouts, local(): summed.at[..., tile_cells - edge_cells:tile_cells]  42.6 us
    dot_general x32, matrix products, project_rows(): jnp.dot(row_item, matrix, preferred_element_type=jnp.float32)  35 us
  transfers between devices with their start and end apart: 2, of which 2 were waited for; matrix products, arithmetic and copies ran while one was open for 0% of the time, Pallas kernels for 0%

commit v1 on v0

v1 whole, which is shorter than its diff:
```python
import functools
import math

import jax
import jax.numpy as jnp
from jax import lax
from jax.experimental import pallas as pl
from jax.experimental.pallas import tpu as pltpu
from jax.sharding import PartitionSpec as P

AVG = 8
TS = 16
EDGE = 4
STRIP = EDGE * TS
CHUNKS = ((0, 0, 256), (0, 256, 256), (1, 0, 256), (1, 256, 256))

SIN = (-1.0 / 6, 1.0 / 120, -1.0 / 5040, 1.0 / 362880, -1.0 / 39916800)
COS = (-1.0 / 2, 1.0 / 24, -1.0 / 720, 1.0 / 40320, -1.0 / 3628800, 1.0 / 479001600)


def series(turns):
    x = (2.0 * math.pi) * turns
    y = x * x
    s = jnp.full_like(x, SIN[-1])
    for k in SIN[-2::-1]:
        s = s * y + k
    c = jnp.full_like(x, COS[-1])
    for k in COS[-2::-1]:
        c = c * y + k
    return c * y + 1.0, (s * y + 1.0) * x


def turn_by(turns):
    half = jnp.round(2.0 * turns)
    c, s = series(turns - 0.5 * half)
    odd = (half - 2.0 * jnp.floor(0.5 * half)) > 0.5
    sign = jnp.where(odd, -1.0, 1.0)
    return c * sign, s * sign


def times(a, b):
    return a[0] * b[0] - a[1] * b[1], a[0] * b[1] + a[1] * b[0]


def average_kernel(vis_ref, delay_ref, out_ref):
    n_out = out_ref.shape[0]
    rows = out_ref.shape[2]
    for r in range(0, rows, 16):
        d = delay_ref[r : r + 16, :]
        c0, s0 = turn_by(d)
        outer = (c0 * (1.0 / AVG), s0 * (1.0 / AVG))
        step = series(d * (1.0 / 32.0))
        small = series(d * (1.0 / 256.0))
        table = [None, small]
        for j in range(2, AVG):
            table.append(times(table[j // 2], table[j - j // 2]))

        def one(o, turn, r=r, table=table, step=step):
            c = o * AVG
            re = vis_ref[c, 0, r : r + 16, :].astype(jnp.float32)
            im = vis_ref[c, 1, r : r + 16, :].astype(jnp.float32)
            for j in range(1, AVG):
                a = vis_ref[c + j, 0, r : r + 16, :].astype(jnp.float32)
                b = vis_ref[c + j, 1, r : r + 16, :].astype(jnp.float32)
                tc, ts = table[j]
                re += a * tc - b * ts
                im += a * ts + b * tc
            tc, ts = turn
            out_ref[o, 0, r : r + 16, :] = (re * tc - im * ts).astype(jnp.bfloat16)
            out_ref[o, 1, r : r + 16, :] = (re * ts + im * tc).astype(jnp.bfloat16)
            return times(turn, step)

        lax.fori_loop(0, n_out, one, outer)


def average(vis, delay):
    n_ch, halves, rows, bv = vis.shape
    return pl.pallas_call(
        average_kernel,
        out_shape=jax.ShapeDtypeStruct((n_ch // AVG, halves, rows, bv), jnp.bfloat16),
        in_specs=[pl.BlockSpec(memory_space=pltpu.VMEM)] * 2,
        out_specs=pl.BlockSpec(memory_space=pltpu.VMEM),
        name="average",
    )(vis, delay)


def grid_kernel(last, first, *refs):
    if first:
        rows_ref, plane_ref, tile_ref, k_ref, *outs = refs
        before_ref = None
    else:
        rows_ref, plane_ref, tile_ref, k_ref, before_ref, *outs = refs
    acc_ref = outs[-1]
    p = pl.program_id(0)
    n_blocks = acc_ref.shape[0]
    bv = rows_ref.shape[3]

    mine = plane_ref[...] == p.astype(jnp.float32)
    re = rows_ref[:, 0].reshape(n_blocks, bv).astype(jnp.float32)
    im = rows_ref[:, 1].reshape(n_blocks, bv).astype(jnp.float32)
    x = jnp.concatenate([jnp.where(mine, re, 0.0), jnp.where(mine, im, 0.0)], axis=1)
    part = jnp.dot(x.astype(jnp.bfloat16), k_ref[0], preferred_element_type=jnp.float32)

    @pl.when(p == 0)
    def _():
        acc_ref[...] = part

    @pl.when(p > 0)
    def _():
        acc_ref[...] += part

    @pl.when(p == pl.num_programs(0) - 1)
    def _():
        n_tiles = outs[0].shape[0] * outs[0].shape[1] if last else outs[0].shape[0]
        ids = lax.broadcasted_iota(jnp.int32, (n_tiles, n_blocks), 0)
        table = (ids == tile_ref[...]).astype(jnp.float32).astype(jnp.bfloat16)
        contrib = acc_ref[...]
        high = contrib.astype(jnp.bfloat16)
        low = (contrib - high.astype(jnp.float32)).astype(jnp.bfloat16)
        grid = jnp.dot(table, high, preferred_element_type=jnp.float32)
        grid += jnp.dot(table, low, preferred_element_type=jnp.float32)
        if before_ref is not None:
            grid += before_ref[...]
        if last:
            cells = grid.shape[1]
            value = grid.astype(jnp.bfloat16)
            outs[0][...] = value.reshape(outs[0].shape)
            strip = jnp.concatenate([grid[:, :STRIP], grid[:, cells // 2 : cells // 2 + STRIP]], axis=1)
            strip = strip.astype(jnp.bfloat16).reshape(outs[1].shape[1:])
            for k in range(outs[1].shape[0]):
                outs[1][k] = strip
        else:
            outs[0][...] = grid


def grid_piece(rows, planes, tiles, kernels, before, last, n_tiles, n_facet):
    n_src, halves, per, bv = rows.shape
    n_blocks = n_src * per
    planes_n, k_rows, cells = kernels.shape
    whole = lambda *shape: pl.BlockSpec(shape, lambda p: (0,) * len(shape))
    in_specs = [
        whole(*rows.shape),
        whole(n_blocks, bv),
        whole(1, n_blocks),
        pl.BlockSpec((1, k_rows, cells), lambda p: (p, 0, 0)),
    ]
    args = [
        rows,
        jnp.broadcast_to(planes.astype(jnp.float32)[:, None], (n_blocks, bv)),
        tiles[None, :],
        kernels,
    ]
    if before is not None:
        in_specs.append(whole(n_tiles, cells))
        args.append(before)
    if last:
        t_dev = n_tiles // n_src
        shapes = [(n_src, t_dev, cells), (n_facet, n_src, t_dev, 2 * STRIP)]
        out_shape = [jax.ShapeDtypeStruct(s, jnp.bfloat16) for s in shapes]
        out_specs = [whole(*s) for s in shapes]
    else:
        out_shape = [jax.ShapeDtypeStruct((n_tiles, cells), jnp.float32)]
        out_specs = [whole(n_tiles, cells)]
    return pl.pallas_call(
        functools.partial(grid_kernel, last, before is None),
        grid=(planes_n,),
        out_shape=out_shape,
        in_specs=in_specs,
        out_specs=out_specs,
        scratch_shapes=[pltpu.VMEM((n_blocks, cells), jnp.float32)],
        name="grid_last" if last else "grid_part",
    )(*args)


def join_kernel(nb_ref, main0_ref, main1_ref, strip0_ref, strip1_ref, out_ref):
    n_out, t_dev, cells = main0_ref.shape
    half = cells // 2
    n_rows = n_out * t_dev
    to = lax.broadcasted_iota(jnp.int32, (n_rows, n_rows), 0)
    source = lax.broadcasted_iota(jnp.int32, (n_rows, n_rows), 1)
    place = (source == (to % n_out) * t_dev + to // n_out).astype(jnp.float32)
    quarter = (0.25 * place).astype(jnp.bfloat16)
    place = place.astype(jnp.bfloat16)
    upper = lax.broadcasted_iota(jnp.int32, (n_rows, 2 * STRIP), 1) >= STRIP
    for slot, main_ref in enumerate((main0_ref, main1_ref)):
        blend = jnp.zeros((n_rows, 2 * STRIP), jnp.float32)
        for k in range(nb_ref.shape[1]):
            nb = nb_ref[slot, k]
            odd = nb % 2 == 1
            a = strip0_ref[nb // 2].reshape(n_rows, 2 * STRIP)
            b = strip1_ref[nb // 2].reshape(n_rows, 2 * STRIP)
            blend += jnp.dot(quarter, jnp.where(odd, b, a), preferred_element_type=jnp.float32)
        swapped = pltpu.roll(blend, STRIP, 1)
        main = main_ref[...].reshape(n_rows, cells)
        main = jnp.dot(place, main, preferred_element_type=jnp.float32)

        def put(lo, hi, value, slot=slot):
            out_ref[:, slot, :, lo:hi] = value.reshape(t_dev, n_out, hi - lo)

        put(0, half - 128, main[:, 0 : half - 128])
        put(half - 128, half, main[:, half - 128 : half] + jnp.where(upper, swapped, 0.0))
        put(half, cells - 128, main[:, half : cells - 128])
        put(cells - 128, cells, main[:, cells - 128 :] + jnp.where(upper, blend, 0.0))


def join(my_neighbours, mains, strips):
    n_out, t_dev, cells = mains[0].shape
    return pl.pallas_call(
        join_kernel,
        out_shape=jax.ShapeDtypeStruct((t_dev, 2, n_out, cells), jnp.float32),
        in_specs=[pl.BlockSpec(memory_space=pltpu.SMEM)] + [pl.BlockSpec(memory_space=pltpu.VMEM)] * 4,
        out_specs=pl.BlockSpec(memory_space=pltpu.VMEM),
        name="join",
    )(my_neighbours, *mains, *strips)


def exchange(x, axis):
    return lax.all_to_all(x, axis, split_axis=0, concat_axis=0, tiled=True)


def local(visibilities, kernels, delays, tile_of, plane_of, counts, neighbours):
    n_facet = lax.axis_size("facet")
    n_chan = lax.axis_size("chan")
    facet_index = lax.axis_index("facet")
    chan_index = lax.axis_index("chan")
    halves, facets, blocks, _, bv = visibilities.shape
    fac_dev = facets // n_facet
    n_tiles = 16 * n_chan
    cells = kernels.shape[2]
    vis = visibilities.reshape(halves, n_facet, fac_dev, blocks, bv)
    live = jnp.arange(blocks, dtype=jnp.int32)[None, :] < counts[:, None]
    planes = jnp.where(live, plane_of, -1)

    arrived = []
    for slot, begin, length in CHUNKS:
        per = length // n_chan
        piece = lax.slice_in_dim(vis[:, :, slot], begin, begin + length, axis=2)
        piece = piece.reshape(halves, n_facet, n_chan, per, bv)
        piece = jnp.transpose(piece, (1, 2, 0, 3, 4)).reshape(n_facet * n_chan, halves, per, bv)
        arrived.append(exchange(piece, ("facet", "chan")))

    mains, strips = [], []
    part = None
    for index, (slot, begin, length) in enumerate(CHUNKS):
        per = length // n_chan
        delay = lax.dynamic_slice(delays[slot], (begin + chan_index * per, 0), (per, bv))
        rows = exchange(average(arrived[index], delay), "chan")
        last = index + 1 == len(CHUNKS) or CHUNKS[index + 1][0] != slot
        result = grid_piece(
            rows,
            planes[slot, begin : begin + length],
            tile_of[slot, begin : begin + length],
            kernels,
            part,
            last,
            n_tiles,
            n_facet,
        )
        if last:
            part = None
            mains.append(exchange(result[0], "chan"))
            strip = result[1].reshape(n_facet * n_chan, n_tiles // n_chan, 2 * STRIP)
            strip = exchange(strip, ("facet", "chan"))
            strips.append(strip.reshape(n_facet, n_chan, n_tiles // n_chan, 2 * STRIP))
        else:
            part = result[0]
    my_neighbours = lax.dynamic_slice_in_dim(neighbours, facet_index * fac_dev, fac_dev, 0)
    return join(my_neighbours, mains, strips)


def solution(mesh):
    return jax.shard_map(
        local,
        mesh=mesh,
        in_specs=(
            P(None, None, None, ("facet", "chan"), None),
            P(),
            P("facet", None, None),
            P("facet", None),
            P("facet", None),
            P("facet"),
            P(),
        ),
        out_specs=P("chan", "facet", None, None),
        check_vma=False,
    )
```

time: 613 us -> 302 us (0.49); the launches traced: 626 us -> 299 us
  local copies, waits for them, and re-layouts: 151 us -> 17.5 us
  starting transfers between devices: 182 us -> 51.1 us
  Pallas kernels: 0 us -> 100 us
  matrix products: 99.7 us -> 0 us
  loops' own time: 60.8 us -> 0 us
  waiting for transfers between devices: 62.9 us -> 91.8 us
  blocking collectives: 54.9 us -> 38.1 us
  other arithmetic: 12.4 us -> 0.08 us
    all_to_all x2 -> x10, starting transfers between devices: 182 us -> 51.1 us  [exchange(): return lax.all_to_all(x, axis, split_axis=0, concat_axis=0, tiled=True)]
    pallas_call x0 -> x9, Pallas kernels: none -> 100 us  [the longest x4 87.6 us: grid_piece(): pl.pallas_call(functools.partial(grid_kernel, last, before is None), grid...]
    dot_general x45 -> x0, matrix products: 99.7 us -> none  [the longest x4 45.5 us: add_tiles(): jnp.einsum('tg,gcx->tcx', table, contrib, precision=HIGHEST)]
    scatter-add x3 -> x0, local copies, waits for them, and re-layouts: 86.1 us -> none  [the longest x2 43.5 us: local(): joined.at[..., 2 * tile_cells - edge_cells:].add(blended[..., edge_cells:])]
    another operation x2 -> x0, loops' own time: 60.8 us -> none  [grid_facet(): return lax.fori_loop(0, trip_count, accumulate, start_grid)]
    all_to_all x2 -> x10, waiting for transfers between devices: 62.9 us -> 91.8 us  [exchange(): return lax.all_to_all(x, axis, split_axis=0, concat_axis=0, tiled=True)]
    another operation x3 -> x0, local copies, waits for them, and re-layouts: 24 us -> none  [the longest x1 15.4 us: local(): stacked = jnp.stack(facet_grids, axis=1)]
    while x2 -> x0, local copies, waits for them, and re-layouts: 19.7 us -> none  [grid_facet(): return lax.fori_loop(0, trip_count, accumulate, start_grid)]
  transfers between devices with their start and end apart: 2 -> 10, of which waited for: 2 -> 8; matrix products, arithmetic and copies ran while one was open for 0% -> 4% of each run, Pallas kernels for 0% -> 32%
where the time goes in v1:
time: 302 us; the launch traced here: 299 us
  Pallas kernels  100 us (33%)
  waiting for transfers between devices  91.8 us (30%)
  starting transfers between devices  51.1 us (17%)
  blocking collectives  38.1 us (13%)
  local copies, waits for them, and re-layouts  17.5 us (6%)
    all_to_all x10, waiting for transfers between devices, exchange(): return lax.all_to_all(x, axis, split_axis=0, concat_axis=0, tiled=True)  91.8 us
    pallas_call x4, Pallas kernels, grid_piece(): pl.pallas_call(functools.partial(grid_kernel, last, before is None), grid...  87.6 us
    all_to_all x10, starting transfers between devices, exchange(): return lax.all_to_all(x, axis, split_axis=0, concat_axis=0, tiled=True)  51.1 us
    all_to_all x2, blocking collectives, exchange(): return lax.all_to_all(x, axis, split_axis=0, concat_axis=0, tiled=True)  38.1 us
    pallas_call x4, Pallas kernels, average(): pl.pallas_call(average_kernel, out_shape=jax.ShapeDtypeStruct((n_ch // AV...  9.41 us
  transfers between devices with their start and end apart: 10, of which 8 were waited for; matrix products, arithmetic and copies ran while one was open for 4% of the time, Pallas kernels for 32%

profile of v1, /device:TPU:1, one launch (start us, length us, event | category | flops | bytes accessed | tf_op | source)
XLA Modules:
  0.0 298.8 jit_solution(13222836197502455280)
XLA Ops:
  0.0 2.7 slice_bitcast_fusion
  2.7 1.4 fusion
  4.1 1.2 copy.15
  5.3 11.5 %all-to-all-start = ((bf16[128,2,16,128]{3,2,1,0:T(8,128)(2,1)}), bf16[128,2,16,128]{3,2,1,0:T(8,128)(2,1)S(1)}, u32[]{:S(2)}, u32[]{:S(2)}) async-start(bf16[128,2,16,128]{3,2,1,0:T(8,128)(2,1)} %bitcast.4), calls=%async_computation | async-start | bytes 2097152 | tf_op jit(solution)/shard_map/all_to_all | solution.py:218
  16.8 1.2 copy.16
  17.9 17.6 %all-to-all-done.vis_ref = bf16[128,2,16,128]{3,2,1,0:T(8,128)(2,1)S(1)} async-done(((bf16[128,2,16,128]{3,2,1,0:T(8,128)(2,1)}), bf16[128,2,16,128]{3,2,1,0:T(8,128)(2,1)S(1)}, u32[]{:S(2)}, u32[]{:S(2)}) %all-to-all-start) | async-done | bytes 1048608 | tf_op jit(solution)/shard_map/all_to_all | solution.py:218
  35.6 4.7 %all-to-all-start.2 = ((bf16[128,2,16,128]{3,2,1,0:T(8,128)(2,1)}), bf16[128,2,16,128]{3,2,1,0:T(8,128)(2,1)S(1)}, u32[]{:S(2)}, u32[]{:S(2)}) async-start(bf16[128,2,16,128]{3,2,1,0:T(8,128)(2,1)} %bitcast.9), calls=%async_computation.2 | async-start | bytes 2097152 | tf_op jit(solution)/shard_map/all_to_all | solution.py:218
  40.3 2.4 copy.17
  42.7 16.6 %all-to-all-done.2.vis_ref = bf16[128,2,16,128]{3,2,1,0:T(8,128)(2,1)S(1)} async-done(((bf16[128,2,16,128]{3,2,1,0:T(8,128)(2,1)}), bf16[128,2,16,128]{3,2,1,0:T(8,128)(2,1)S(1)}, u32[]{:S(2)}, u32[]{:S(2)}) %all-to-all-start.2) | async-done | bytes 1048608 | tf_op jit(solution)/shard_map/all_to_all | solution.py:218
  59.2 4.7 %all-to-all-start.5 = ((bf16[128,2,16,128]{3,2,1,0:T(8,128)(2,1)}), bf16[128,2,16,128]{3,2,1,0:T(8,128)(2,1)S(1)}, u32[]{:S(2)}, u32[]{:S(2)}) async-start(bf16[128,2,16,128]{3,2,1,0:T(8,128)(2,1)} %bitcast.15), calls=%async_computation.5 | async-start | bytes 2097152 | tf_op jit(solution)/shard_map/all_to_all | solution.py:218
  63.9 1.2 copy.18
  65.1 17.8 %all-to-all-done.5.vis_ref = bf16[128,2,16,128]{3,2,1,0:T(8,128)(2,1)S(1)} async-done(((bf16[128,2,16,128]{3,2,1,0:T(8,128)(2,1)}), bf16[128,2,16,128]{3,2,1,0:T(8,128)(2,1)S(1)}, u32[]{:S(2)}, u32[]{:S(2)}) %all-to-all-start.5) | async-done | bytes 1048608 | tf_op jit(solution)/shard_map/all_to_all | solution.py:218
  82.9 4.7 %all-to-all-start.7 = ((bf16[128,2,16,128]{3,2,1,0:T(8,128)(2,1)}), bf16[128,2,16,128]{3,2,1,0:T(8,128)(2,1)S(1)}, u32[]{:S(2)}, u32[]{:S(2)}) async-start(bf16[128,2,16,128]{3,2,1,0:T(8,128)(2,1)} %bitcast.20), calls=%async_computation.7 | async-start | bytes 2097152 | tf_op jit(solution)/shard_map/all_to_all | solution.py:218
  87.6 0.0 copy-start.14
  87.6 1.1 fusion.2
  88.7 0.6 dynamic-slice_bitcast_fusion.2
  89.3 2.4 average.4
  91.7 14.9 %all-to-all-done.7.vis_ref = bf16[128,2,16,128]{3,2,1,0:T(8,128)(2,1)S(1)} async-done(((bf16[128,2,16,128]{3,2,1,0:T(8,128)(2,1)}), bf16[128,2,16,128]{3,2,1,0:T(8,128)(2,1)S(1)}, u32[]{:S(2)}, u32[]{:S(2)}) %all-to-all-start.7) | async-done | bytes 1048608 | tf_op jit(solution)/shard_map/all_to_all | solution.py:218
  106.6 3.5 %all-to-all-start.1 = ((bf16[16,2,16,128]{3,2,1,0:T(8,128)(2,1)}), bf16[16,2,16,128]{3,2,1,0:T(8,128)(2,1)S(1)}, u32[]{:S(2)}, u32[]{:S(2)}) async-start(bf16[16,2,16,128]{3,2,1,0:T(8,128)(2,1)} %average.4), calls=%async_computation.1 | async-start | bytes 262144 | tf_op jit(solution)/shard_map/all_to_all | solution.py:218
  110.1 2.4 average.5
  112.5 4.3 %all-to-all-done.1.refs_0_ = bf16[16,2,16,128]{3,2,1,0:T(8,128)(2,1)S(1)} async-done(((bf16[16,2,16,128]{3,2,1,0:T(8,128)(2,1)}), bf16[16,2,16,128]{3,2,1,0:T(8,128)(2,1)S(1)}, u32[]{:S(2)}, u32[]{:S(2)}) %all-to-all-start.1) | async-done | bytes 131104 | tf_op jit(solution)/shard_map/all_to_all | solution.py:218
  116.7 3.6 %all-to-all-start.3 = ((bf16[16,2,16,128]{3,2,1,0:T(8,128)(2,1)}), bf16[16,2,16,128]{3,2,1,0:T(8,128)(2,1)S(1)}, u32[]{:S(2)}, u32[]{:S(2)}) async-start(bf16[16,2,16,128]{3,2,1,0:T(8,128)(2,1)} %average.5), calls=%async_computation.3 | async-start | bytes 262144 | tf_op jit(solution)/shard_map/all_to_all | solution.py:218
  120.4 0.1 compare_select_fusion
  120.5 0.6 dynamic-slice_bitcast_fusion
  121.1 2.4 average.6
  123.4 3.6 %all-to-all-done.3.refs_0_ = bf16[16,2,16,128]{3,2,1,0:T(8,128)(2,1)S(1)} async-done(((bf16[16,2,16,128]{3,2,1,0:T(8,128)(2,1)}), bf16[16,2,16,128]{3,2,1,0:T(8,128)(2,1)S(1)}, u32[]{:S(2)}, u32[]{:S(2)}) %all-to-all-start.3) | async-done | bytes 131104 | tf_op jit(solution)/shard_map/all_to_all | solution.py:218
  127.1 3.6 %all-to-all-start.6 = ((bf16[16,2,16,128]{3,2,1,0:T(8,128)(2,1)}), bf16[16,2,16,128]{3,2,1,0:T(8,128)(2,1)S(1)}, u32[]{:S(2)}, u32[]{:S(2)}) async-start(bf16[16,2,16,128]{3,2,1,0:T(8,128)(2,1)} %average.6), calls=%async_computation.6 | async-start | bytes 262144 | tf_op jit(solution)/shard_map/all_to_all | solution.py:218
  130.7 2.3 average.7
  133.1 4.3 %all-to-all-done.6.refs_0_ = bf16[16,2,16,128]{3,2,1,0:T(8,128)(2,1)S(1)} async-done(((bf16[16,2,16,128]{3,2,1,0:T(8,128)(2,1)}), bf16[16,2,16,128]{3,2,1,0:T(8,128)(2,1)S(1)}, u32[]{:S(2)}, u32[]{:S(2)}) %all-to-all-start.6) | async-done | bytes 131104 | tf_op jit(solution)/shard_map/all_to_all | solution.py:218
  137.4 3.5 %all-to-all-start.8 = ((bf16[16,2,16,128]{3,2,1,0:T(8,128)(2,1)}), bf16[16,2,16,128]{3,2,1,0:T(8,128)(2,1)S(1)}, u32[]{:S(2)}, u32[]{:S(2)}) async-start(bf16[16,2,16,128]{3,2,1,0:T(8,128)(2,1)} %average.7), calls=%async_computation.8 | async-start | bytes 262144 | tf_op jit(solution)/shard_map/all_to_all | solution.py:218
  140.9 0.6 fusion.3
  141.5 0.7 broadcast_in_dim.14.refs_1_
  142.2 21.6 %grid_part.2.refs_4_ = f32[256,512]{1,0:T(8,128)} custom-call(bf16[16,2,16,128]{3,2,1,0:T(8,128)(2,1)} %copy-done.9, f32[256,128]{1,0:T(8,128)} %broadcast_in_dim.14.refs_1_, s32[1,256]{1,0:T(1,128)} %get-tuple-element.26.refs_2_, bf16[32,256,512]{2,1,0:T(8,128)(2,1)} %refs_3_.7), custom_call_target="tpu_custom_call" | custom-call | tf_op jit(solution)/shard_map/grid_part/pallas_call | solution.py:164
  163.9 0.8 broadcast_in_dim.13.refs_1_
  164.6 22.1 %grid_last.2 = (bf16[16,16,512]{2,1,0:T(8,128)(2,1)}, bf16[8,16,16,128]{3,2,1,0:T(8,128)(2,1)}) custom-call(bf16[16,2,16,128]{3,2,1,0:T(8,128)(2,1)} %copy-done.7, f32[256,128]{1,0:T(8,128)} %broadcast_in_dim.13.refs_1_, s32[1,256]{1,0:T(1,128)} %get-tuple-element.27.refs_2_, bf16[32,256,512]{2,1,0:T(8,128)(2,1)} %refs_3_.7, f32[256,512]{1,0:T(8,128)} %grid_part.2.refs_4_), custom_call_target="tpu_custom_call" | custom-call | tf_op jit(solution)/shard_map/grid_last/pallas_call | solution.py:164
  186.8 6.6 %all-to-all-start.4 = ((bf16[16,16,512]{2,1,0:T(8,128)(2,1)}), bf16[16,16,512]{2,1,0:T(8,128)(2,1)S(1)}, u32[]{:S(2)}, u32[]{:S(2)}) async-start(bf16[16,16,512]{2,1,0:T(8,128)(2,1)} %get-tuple-element.9), calls=%async_computation.4 | async-start | bytes 524288 | tf_op jit(solution)/shard_map/all_to_all | solution.py:218
  193.4 0.7 broadcast_in_dim.16.refs_1_
  194.1 21.7 %grid_part.3.refs_4_ = f32[256,512]{1,0:T(8,128)} custom-call(bf16[16,2,16,128]{3,2,1,0:T(8,128)(2,1)} %copy-done.10, f32[256,128]{1,0:T(8,128)} %broadcast_in_dim.16.refs_1_, s32[1,256]{1,0:T(1,128)} %get-tuple-element.25.refs_2_, bf16[32,256,512]{2,1,0:T(8,128)(2,1)} %refs_3_.7), custom_call_target="tpu_custom_call" | custom-call | tf_op jit(solution)/shard_map/grid_part/pallas_call | solution.py:164
  215.8 0.7 broadcast_in_dim.15.refs_1_
  216.5 22.2 %grid_last.3 = (bf16[16,16,512]{2,1,0:T(8,128)(2,1)}, bf16[8,16,16,128]{3,2,1,0:T(8,128)(2,1)}) custom-call(bf16[16,2,16,128]{3,2,1,0:T(8,128)(2,1)} %copy-done.8, f32[256,128]{1,0:T(8,128)} %broadcast_in_dim.15.refs_1_, s32[1,256]{1,0:T(1,128)} %get-tuple-element.28.refs_2_, bf16[32,256,512]{2,1,0:T(8,128)(2,1)} %refs_3_.7, f32[256,512]{1,0:T(8,128)} %grid_part.3.refs_4_), custom_call_target="tpu_custom_call" | custom-call | tf_op jit(solution)/shard_map/grid_last/pallas_call | solution.py:164
  238.8 14.1 %all_to_all.60.main1_ref = bf16[16,16,512]{2,1,0:T(8,128)(2,1)} all-to-all(bf16[16,16,512]{2,1,0:T(8,128)(2,1)} %get-tuple-element.10), channel_id=1, replica_groups=mesh['facet'=8,'chan'=16] {'chan'}, dimensions={0} | all-to-all | bytes 524288 | tf_op jit(solution)/shard_map/all_to_all | solution.py:218
  252.9 24.0 %all_to_all.61 = bf16[128,16,128]{2,1,0:T(8,128)(2,1)} all-to-all(bf16[128,16,128]{2,1,0:T(8,128)(2,1)S(1)} %bitcast.45), channel_id=1, replica_groups=mesh['facet'=8,'chan'=16] {'facet','chan'}, dimensions={0} | all-to-all | bytes 1048576 | tf_op jit(solution)/shard_map/all_to_all | solution.py:218
  276.9 4.7 %all-to-all-start.11 = ((bf16[128,16,128]{2,1,0:T(8,128)(2,1)}), bf16[128,16,128]{2,1,0:T(8,128)(2,1)S(1)}, u32[]{:S(2)}, u32[]{:S(2)}) async-start(bf16[128,16,128]{2,1,0:T(8,128)(2,1)} %bitcast.44), calls=%async_computation.11 | async-start | bytes 1048576 | tf_op jit(solution)/shard_map/all_to_all | solution.py:218
  281.6 0.1 constant_dynamic-slice_fusion
  281.7 0.7 copy.19.nb_ref
  282.4 12.7 %all-to-all-done.11 = bf16[128,16,128]{2,1,0:T(8,128)(2,1)S(1)} async-done(((bf16[128,16,128]{2,1,0:T(8,128)(2,1)}), bf16[128,16,128]{2,1,0:T(8,128)(2,1)S(1)}, u32[]{:S(2)}, u32[]{:S(2)}) %all-to-all-start.11) | async-done | bytes 524320 | tf_op jit(solution)/shard_map/all_to_all | solution.py:218
  295.1 0.8 copy-done.5
  295.9 2.9 join.1
  (31 shorter events, 0.1 us)
Async XLA Ops:
  0.0 281.6 %copy-start = (s32[16,4]{0,1:T(4,128)S(1)}, s32[16,4]{0,1:T(4,128)}, u32[]{:S(2)}) copy-start(s32[16,4]{0,1:T(4,128)} %param.13) | copy-start | bytes 772
  5.3 30.3 %all-to-all-start = ((bf16[128,2,16,128]{3,2,1,0:T(8,128)(2,1)}), bf16[128,2,16,128]{3,2,1,0:T(8,128)(2,1)S(1)}, u32[]{:S(2)}, u32[]{:S(2)}) async-start(bf16[128,2,16,128]{3,2,1,0:T(8,128)(2,1)} %bitcast.4), calls=%async_computation | async-start | bytes 2097152 | tf_op jit(solution)/shard_map/all_to_all | solution.py:218
  35.6 7.1 %copy-start.4 = (bf16[128,2,16,128]{3,2,1,0:T(8,128)(2,1)}, bf16[128,2,16,128]{3,2,1,0:T(8,128)(2,1)S(1)}, u32[]{:S(2)}) copy-start(bf16[128,2,16,128]{3,2,1,0:T(8,128)(2,1)S(1)} %all-to-all-done.vis_ref) | copy-start | bytes 3145732
  35.6 23.7 %all-to-all-start.2 = ((bf16[128,2,16,128]{3,2,1,0:T(8,128)(2,1)}), bf16[128,2,16,128]{3,2,1,0:T(8,128)(2,1)S(1)}, u32[]{:S(2)}, u32[]{:S(2)}) async-start(bf16[128,2,16,128]{3,2,1,0:T(8,128)(2,1)} %bitcast.9), calls=%async_computation.2 | async-start | bytes 2097152 | tf_op jit(solution)/shard_map/all_to_all | solution.py:218
  59.2 5.9 %copy-start.3 = (bf16[128,2,16,128]{3,2,1,0:T(8,128)(2,1)}, bf16[128,2,16,128]{3,2,1,0:T(8,128)(2,1)S(1)}, u32[]{:S(2)}) copy-start(bf16[128,2,16,128]{3,2,1,0:T(8,128)(2,1)S(1)} %all-to-all-done.2.vis_ref) | copy-start | bytes 3145732
  59.2 23.7 %all-to-all-start.5 = ((bf16[128,2,16,128]{3,2,1,0:T(8,128)(2,1)}), bf16[128,2,16,128]{3,2,1,0:T(8,128)(2,1)S(1)}, u32[]{:S(2)}, u32[]{:S(2)}) async-start(bf16[128,2,16,128]{3,2,1,0:T(8,128)(2,1)} %bitcast.15), calls=%async_computation.5 | async-start | bytes 2097152 | tf_op jit(solution)/shard_map/all_to_all | solution.py:218
  82.9 8.8 %copy-start.2 = (bf16[128,2,16,128]{3,2,1,0:T(8,128)(2,1)}, bf16[128,2,16,128]{3,2,1,0:T(8,128)(2,1)S(1)}, u32[]{:S(2)}) copy-start(bf16[128,2,16,128]{3,2,1,0:T(8,128)(2,1)S(1)} %all-to-all-done.5.vis_ref) | copy-start | bytes 3145732
  82.9 23.7 %all-to-all-start.7 = ((bf16[128,2,16,128]{3,2,1,0:T(8,128)(2,1)}), bf16[128,2,16,128]{3,2,1,0:T(8,128)(2,1)S(1)}, u32[]{:S(2)}, u32[]{:S(2)}) async-start(bf16[128,2,16,128]{3,2,1,0:T(8,128)(2,1)} %bitcast.20), calls=%async_computation.7 | async-start | bytes 2097152 | tf_op jit(solution)/shard_map/all_to_all | solution.py:218
  87.6 32.8 %copy-start.12 = (s32[2,512]{1,0:T(2,128)S(1)}, s32[2,512]{1,0:T(2,128)}, u32[]{:S(2)}) copy-start(s32[2,512]{1,0:T(2,128)} %param.11) | copy-start | bytes 12292
  87.6 32.8 %copy-start.14 = (s32[2]{0:T(128)S(1)}, s32[2]{0:T(128)}, u32[]{:S(2)}) copy-start(s32[2]{0:T(128)} %param.12) | copy-start | bytes 28
  106.6 24.1 %copy-start.1 = (bf16[128,2,16,128]{3,2,1,0:T(8,128)(2,1)}, bf16[128,2,16,128]{3,2,1,0:T(8,128)(2,1)S(1)}, u32[]{:S(2)}) copy-start(bf16[128,2,16,128]{3,2,1,0:T(8,128)(2,1)S(1)} %all-to-all-done.7.vis_ref) | copy-start | bytes 3145732
  106.6 10.1 %all-to-all-start.1 = ((bf16[16,2,16,128]{3,2,1,0:T(8,128)(2,1)}), bf16[16,2,16,128]{3,2,1,0:T(8,128)(2,1)S(1)}, u32[]{:S(2)}, u32[]{:S(2)}) async-start(bf16[16,2,16,128]{3,2,1,0:T(8,128)(2,1)} %average.4), calls=%async_computation.1 | async-start | bytes 262144 | tf_op jit(solution)/shard_map/all_to_all | solution.py:218
  110.1 30.8 %copy-start.13 = (s32[2,512]{1,0:T(2,128)S(1)}, s32[2,512]{1,0:T(2,128)}, u32[]{:S(2)}) copy-start(s32[2,512]{1,0:T(2,128)} %param.10) | copy-start | bytes 12292
  116.7 47.1 %copy-start.7 = (bf16[16,2,16,128]{3,2,1,0:T(8,128)(2,1)}, bf16[16,2,16,128]{3,2,1,0:T(8,128)(2,1)S(1)}, u32[]{:S(2)}) copy-start(bf16[16,2,16,128]{3,2,1,0:T(8,128)(2,1)S(1)} %all-to-all-done.1.refs_0_) | copy-start | bytes 393220
  116.7 10.3 %all-to-all-start.3 = ((bf16[16,2,16,128]{3,2,1,0:T(8,128)(2,1)}), bf16[16,2,16,128]{3,2,1,0:T(8,128)(2,1)S(1)}, u32[]{:S(2)}, u32[]{:S(2)}) async-start(bf16[16,2,16,128]{3,2,1,0:T(8,128)(2,1)} %average.5), calls=%async_computation.3 | async-start | bytes 262144 | tf_op jit(solution)/shard_map/all_to_all | solution.py:218
  127.1 15.2 %copy-start.9 = (bf16[16,2,16,128]{3,2,1,0:T(8,128)(2,1)}, bf16[16,2,16,128]{3,2,1,0:T(8,128)(2,1)S(1)}, u32[]{:S(2)}) copy-start(bf16[16,2,16,128]{3,2,1,0:T(8,128)(2,1)S(1)} %all-to-all-done.3.refs_0_) | copy-start | bytes 393220
  127.1 10.3 %all-to-all-start.6 = ((bf16[16,2,16,128]{3,2,1,0:T(8,128)(2,1)}), bf16[16,2,16,128]{3,2,1,0:T(8,128)(2,1)S(1)}, u32[]{:S(2)}, u32[]{:S(2)}) async-start(bf16[16,2,16,128]{3,2,1,0:T(8,128)(2,1)} %average.6), calls=%async_computation.6 | async-start | bytes 262144 | tf_op jit(solution)/shard_map/all_to_all | solution.py:218
  137.4 26.5 %copy-start.8 = (bf16[16,2,16,128]{3,2,1,0:T(8,128)(2,1)}, bf16[16,2,16,128]{3,2,1,0:T(8,128)(2,1)S(1)}, u32[]{:S(2)}) copy-start(bf16[16,2,16,128]{3,2,1,0:T(8,128)(2,1)S(1)} %all-to-all-done.6.refs_0_) | copy-start | bytes 393220
  137.4 49.4 %all-to-all-start.8 = ((bf16[16,2,16,128]{3,2,1,0:T(8,128)(2,1)}), bf16[16,2,16,128]{3,2,1,0:T(8,128)(2,1)S(1)}, u32[]{:S(2)}, u32[]{:S(2)}) async-start(bf16[16,2,16,128]{3,2,1,0:T(8,128)(2,1)} %average.7), calls=%async_computation.8 | async-start | bytes 262144 | tf_op jit(solution)/shard_map/all_to_all | solution.py:218
  186.8 7.4 %copy-start.10 = (bf16[16,2,16,128]{3,2,1,0:T(8,128)(2,1)}, bf16[16,2,16,128]{3,2,1,0:T(8,128)(2,1)S(1)}, u32[]{:S(2)}) copy-start(bf16[16,2,16,128]{3,2,1,0:T(8,128)(2,1)S(1)} %all-to-all-done.8.refs_0_) | copy-start | bytes 393220
  186.8 52.0 %all-to-all-start.4 = ((bf16[16,16,512]{2,1,0:T(8,128)(2,1)}), bf16[16,16,512]{2,1,0:T(8,128)(2,1)S(1)}, u32[]{:S(2)}, u32[]{:S(2)}) async-start(bf16[16,16,512]{2,1,0:T(8,128)(2,1)} %get-tuple-element.9), calls=%async_computation.4 | async-start | bytes 524288 | tf_op jit(solution)/shard_map/all_to_all | solution.py:218
  216.5 36.3 %copy-start.11 = (bf16[8,16,16,128]{3,2,1,0:T(8,128)(2,1)S(1)}, bf16[8,16,16,128]{3,2,1,0:T(8,128)(2,1)}, u32[]{:S(2)}) copy-start(bf16[8,16,16,128]{3,2,1,0:T(8,128)(2,1)} %get-tuple-element.11) | copy-start | bytes 1572868
  238.8 56.3 %copy-start.6 = (bf16[16,16,512]{2,1,0:T(8,128)(2,1)}, bf16[16,16,512]{2,1,0:T(8,128)(2,1)S(1)}, u32[]{:S(2)}) copy-start(bf16[16,16,512]{2,1,0:T(8,128)(2,1)S(1)} %all-to-all-done.4.main0_ref) | copy-start | bytes 786436
  276.9 18.2 %all-to-all-start.11 = ((bf16[128,16,128]{2,1,0:T(8,128)(2,1)}), bf16[128,16,128]{2,1,0:T(8,128)(2,1)S(1)}, u32[]{:S(2)}, u32[]{:S(2)}) async-start(bf16[128,16,128]{2,1,0:T(8,128)(2,1)} %bitcast.44), calls=%async_computation.11 | async-start | bytes 1048576 | tf_op jit(solution)/shard_map/all_to_all | solution.py:218
  295.1 0.8 copy-start.5

commit v2 on v1

v2 whole, which is shorter than its diff:
```python
import functools
import math

import jax
import jax.numpy as jnp
from jax import lax
from jax.experimental import pallas as pl
from jax.experimental.pallas import tpu as pltpu
from jax.sharding import PartitionSpec as P

AVG = 8
TS = 16
EDGE = 4
STRIP = EDGE * TS
GROUP = 16
PIECE = 64
MIB = 1024 * 1024

SIN = (-1.0 / 6, 1.0 / 120, -1.0 / 5040, 1.0 / 362880, -1.0 / 39916800)
COS = (-1.0 / 2, 1.0 / 24, -1.0 / 720, 1.0 / 40320, -1.0 / 3628800, 1.0 / 479001600)


def series(turns):
    x = (2.0 * math.pi) * turns
    y = x * x
    s = jnp.full_like(x, SIN[-1])
    for k in SIN[-2::-1]:
        s = s * y + k
    c = jnp.full_like(x, COS[-1])
    for k in COS[-2::-1]:
        c = c * y + k
    return c * y + 1.0, (s * y + 1.0) * x


def turn_by(turns):
    half = jnp.round(2.0 * turns)
    c, s = series(turns - 0.5 * half)
    odd = (half - 2.0 * jnp.floor(0.5 * half)) > 0.5
    sign = jnp.where(odd, -1.0, 1.0)
    return c * sign, s * sign


def times(a, b):
    return a[0] * b[0] - a[1] * b[1], a[0] * b[1] + a[1] * b[0]


def vmem():
    return pl.BlockSpec(memory_space=pltpu.VMEM)


def send_kernel(vis_ref, out_ref, sem):
    copies = [
        pltpu.make_async_copy(vis_ref.at[h], out_ref.at[:, h], sem.at[h]) for h in range(vis_ref.shape[0])
    ]
    for copy in copies:
        copy.start()
    for copy in copies:
        copy.wait()


def send_order(vis):
    halves, dests, rows, bv = vis.shape
    return pl.pallas_call(
        send_kernel,
        out_shape=jax.ShapeDtypeStruct((dests, halves, rows, bv), vis.dtype),
        in_specs=[pl.BlockSpec(memory_space=pl.ANY)],
        out_specs=pl.BlockSpec(memory_space=pl.ANY),
        scratch_shapes=[pltpu.SemaphoreType.DMA((halves,))],
        compiler_params=pltpu.CompilerParams(vmem_limit_bytes=1 * MIB),
        name="send_order",
    )(vis)


def turns_kernel(delay_ref, inner_ref, outer_ref):
    d = delay_ref[...]
    small = series(d * (1.0 / 256.0))
    table = [None, small]
    for j in range(2, AVG):
        table.append(times(table[j // 2], table[j - j // 2]))
    for j in range(1, AVG):
        inner_ref[j - 1, 0] = table[j][0]
        inner_ref[j - 1, 1] = table[j][1]
    c, s = turn_by(d)
    turn = (c * (1.0 / AVG), s * (1.0 / AVG))
    step = series(d * (1.0 / 32.0))
    for o in range(outer_ref.shape[0]):
        outer_ref[o, 0] = turn[0]
        outer_ref[o, 1] = turn[1]
        turn = times(turn, step)


def turns(delay, n_out):
    rows, bv = delay.shape
    return pl.pallas_call(
        turns_kernel,
        out_shape=[
            jax.ShapeDtypeStruct((AVG - 1, 2, rows, bv), jnp.float32),
            jax.ShapeDtypeStruct((n_out, 2, rows, bv), jnp.float32),
        ],
        in_specs=[vmem()],
        out_specs=[vmem()] * 2,
        compiler_params=pltpu.CompilerParams(vmem_limit_bytes=8 * MIB),
        name="turns",
    )(delay)


def average_kernel(vis_ref, inner_ref, outer_ref, out_ref):
    n_out, _, rows, _ = out_ref.shape
    for r in range(0, rows, 16):
        at = slice(r, r + 16)
        table = [(inner_ref[j, 0, at], inner_ref[j, 1, at]) for j in range(AVG - 1)]

        def one(o, carry, at=at, table=table):
            c = o * AVG
            re = vis_ref[c, 0, at].astype(jnp.float32)
            im = vis_ref[c, 1, at].astype(jnp.float32)
            for j in range(1, AVG):
                a = vis_ref[c + j, 0, at].astype(jnp.float32)
                b = vis_ref[c + j, 1, at].astype(jnp.float32)
                tc, ts = table[j - 1]
                re += a * tc - b * ts
                im += a * ts + b * tc
            tc = outer_ref[o, 0, at]
            ts = outer_ref[o, 1, at]
            out_ref[o, 0, at] = (re * tc - im * ts).astype(jnp.bfloat16)
            out_ref[o, 1, at] = (re * ts + im * tc).astype(jnp.bfloat16)
            return carry

        lax.fori_loop(0, n_out, one, 0, unroll=4)


def average(vis, inner, outer):
    n_ch, halves, rows, bv = vis.shape
    return pl.pallas_call(
        average_kernel,
        out_shape=jax.ShapeDtypeStruct((n_ch // AVG, halves, rows, bv), jnp.bfloat16),
        in_specs=[vmem()] * 3,
        out_specs=vmem(),
        compiler_params=pltpu.CompilerParams(vmem_limit_bytes=12 * MIB),
        name="average",
    )(vis, inner, outer)


def to_bf16(mask):
    return mask.astype(jnp.float32).astype(jnp.bfloat16)


def tables_kernel(n_planes, n_tiles, t_dev, plane_ref, tile_ref, order_ref, tiles_ref, piece_ref):
    n_rows = plane_ref.shape[1]
    f32 = jnp.float32
    iota = lambda shape, dim: lax.broadcasted_iota(jnp.int32, shape, dim)
    plane = plane_ref[...]
    mine = plane == iota((n_planes, n_rows), 0)
    before = to_bf16(iota((n_rows, n_rows), 0) < iota((n_rows, n_rows), 1))
    rank = jnp.dot(to_bf16(mine), before, preferred_element_type=f32)
    count = jnp.sum(mine.astype(f32), axis=1, keepdims=True)
    groups = jnp.floor((count + (GROUP - 1)) * (1.0 / GROUP))
    pieces = jnp.floor((groups + (PIECE // GROUP - 1)) * (GROUP / PIECE))
    earlier = to_bf16(iota((n_planes, n_planes), 1) < iota((n_planes, n_planes), 0))
    both = jnp.concatenate(
        [jnp.broadcast_to(groups, (n_planes, 128)), jnp.broadcast_to(pieces, (n_planes, 128))], axis=1
    )
    both = jnp.dot(earlier, both.astype(jnp.bfloat16), preferred_element_type=f32)
    first_group = both[:, 0:1]
    first_piece = both[:, 128:129]
    place = jnp.sum(jnp.where(mine, rank + GROUP * first_group, 0.0), axis=0, keepdims=True)
    live = jnp.sum(mine.astype(f32), axis=0, keepdims=True)
    place = jnp.where(live > 0.5, place, -1.0).astype(jnp.int32)
    n_order = order_ref.shape[0]
    order = to_bf16(iota((n_order, n_rows), 0) == place)
    order_ref[...] = order

    row = iota((8, n_rows), 0)
    slot = (iota((8, n_rows), 1) >= n_rows // 2).astype(f32)
    values = jnp.where(row == 0, tile_ref[...].astype(f32) + 1.0, jnp.where(row == 1, slot, 0.0))
    n_used = tiles_ref.shape[1]
    ordered = lax.dot_general(
        values.astype(jnp.bfloat16), order[:n_used], (((1,), (1,)), ((), ())), preferred_element_type=f32
    )
    tile = ordered[0:1].astype(jnp.int32) - 1
    slot = ordered[1:2].astype(jnp.int32)
    code = (tile // t_dev) * (2 * t_dev) + slot * t_dev + tile % t_dev
    code = jnp.where(tile < 0, -1, code)
    tiles_ref[...] = to_bf16(iota((2 * n_tiles, n_used), 0) == code)

    total = jnp.sum(pieces)
    which = jnp.minimum(iota((n_planes, 128), 1).astype(f32), total - 1.0)
    taken = (which >= first_piece) & (which < first_piece + pieces)
    group = first_group + (PIECE // GROUP) * (which - first_piece)
    group = jnp.sum(jnp.where(taken, group, 0.0), axis=0, keepdims=True)
    owner = jnp.sum(jnp.where(taken, iota((n_planes, 128), 0).astype(f32), 0.0), axis=0, keepdims=True)
    row = iota((8, 128), 0)
    piece_ref[...] = jnp.where(row == 0, group, jnp.where(row == 1, owner, 0.0)).astype(jnp.int32)


def tables(planes, tiles, n_planes, n_tiles, t_dev):
    n_rows = planes.shape[1]
    used = n_rows + n_planes * (GROUP - 1)
    n_order = -(-(used - GROUP + PIECE) // 32) * 32
    n_used = -(-used // 256) * 256
    assert n_used <= n_order
    return pl.pallas_call(
        functools.partial(tables_kernel, n_planes, n_tiles, t_dev),
        out_shape=[
            jax.ShapeDtypeStruct((n_order, n_rows), jnp.bfloat16),
            jax.ShapeDtypeStruct((2 * n_tiles, n_used), jnp.bfloat16),
            jax.ShapeDtypeStruct((8, 128), jnp.int32),
        ],
        in_specs=[vmem()] * 2,
        out_specs=[vmem()] * 3,
        compiler_params=pltpu.CompilerParams(vmem_limit_bytes=40 * MIB),
        name="tables",
    )(planes, tiles)


def grid_kernel(n_pieces, piece_ref, rows_ref, order_ref, tiles_ref, k_ref, out_ref, x_ref, c_ref):
    n_src, _, per, bv = rows_ref.shape
    re = rows_ref[:, 0].reshape(n_src * per, bv)
    im = rows_ref[:, 1].reshape(n_src * per, bv)
    x = jnp.concatenate([re, im], axis=1)
    x_ref[...] = jnp.dot(order_ref[...], x, preferred_element_type=jnp.float32).astype(jnp.bfloat16)
    n_used = tiles_ref.shape[1]
    c_ref[...] = jnp.zeros_like(c_ref)
    for i in range(n_pieces):
        at = pl.ds(pl.multiple_of(piece_ref[0, i] * GROUP, GROUP), PIECE)
        product = jnp.dot(x_ref[at, :], k_ref[piece_ref[1, i]], preferred_element_type=jnp.float32)
        c_ref[at, :] = product.astype(jnp.bfloat16)
    grid = jnp.dot(tiles_ref[...], c_ref[:n_used, :], preferred_element_type=jnp.float32)
    out_ref[...] = grid.astype(jnp.bfloat16).reshape(out_ref.shape)


def grid_rows(piece, rows, order, tiles, kernels, n_chan):
    n_planes, k_rows, cells = kernels.shape
    n_order, n_rows = order.shape
    return pl.pallas_call(
        functools.partial(grid_kernel, n_rows // PIECE + n_planes),
        out_shape=jax.ShapeDtypeStruct((n_chan, tiles.shape[0] // n_chan, cells), jnp.bfloat16),
        in_specs=[pl.BlockSpec(memory_space=pltpu.SMEM)] + [vmem()] * 4,
        out_specs=vmem(),
        scratch_shapes=[
            pltpu.VMEM((n_order, k_rows), jnp.bfloat16),
            pltpu.VMEM((n_order, cells), jnp.bfloat16),
        ],
        compiler_params=pltpu.CompilerParams(vmem_limit_bytes=40 * MIB),
        name="grid_rows",
    )(piece, rows, order, tiles, kernels)


def strip_kernel(main_ref, out_ref):
    n_out, per, cells = main_ref.shape
    half = cells // 2
    low = main_ref[:, :, 0:128].reshape(n_out * per, 128).astype(jnp.float32)
    high = main_ref[:, :, half : half + 128].reshape(n_out * per, 128).astype(jnp.float32)
    lane = lax.broadcasted_iota(jnp.int32, low.shape, 1)
    strip = jnp.where(lane < STRIP, low, pltpu.roll(high, STRIP, 1)).astype(jnp.bfloat16)
    for k in range(out_ref.shape[0]):
        out_ref[k] = strip.reshape(out_ref.shape[1:])


def strips_for_each(main, n_facet):
    n_out, per, _ = main.shape
    return pl.pallas_call(
        strip_kernel,
        out_shape=jax.ShapeDtypeStruct((n_facet, n_out, per, 2 * STRIP), jnp.bfloat16),
        in_specs=[vmem()],
        out_specs=vmem(),
        compiler_params=pltpu.CompilerParams(vmem_limit_bytes=12 * MIB),
        name="strips",
    )(main)


def join_kernel(nb_ref, main_ref, strip_ref, out_ref):
    n_out, per, cells = main_ref.shape
    t_dev = per // 2
    half = cells // 2
    n_rows = n_out * t_dev
    iota = lambda shape, dim: lax.broadcasted_iota(jnp.int32, shape, dim)
    upper = iota((n_rows, 2 * STRIP), 1) >= STRIP
    to = iota((n_rows, n_rows), 0)
    place = (iota((n_rows, n_rows), 1) == (to % n_out) * t_dev + to // n_out).astype(jnp.float32)
    quarter = (0.25 * place).astype(jnp.bfloat16)
    place = place.astype(jnp.bfloat16)
    for slot in range(2):
        blend = jnp.zeros((n_rows, 2 * STRIP), jnp.float32)
        for k in range(nb_ref.shape[1]):
            nb = nb_ref[slot, k]
            strip = strip_ref[nb // 2, :, nb % 2].reshape(n_rows, 2 * STRIP)
            blend += jnp.dot(quarter, strip, preferred_element_type=jnp.float32)
        swapped = pltpu.roll(blend, STRIP, 1)
        main = main_ref[:, slot * t_dev : (slot + 1) * t_dev, :].reshape(n_rows, cells)
        main = jnp.dot(place, main, preferred_element_type=jnp.float32)

        def put(lo, hi, value, slot=slot):
            out_ref[:, slot, :, lo:hi] = value.reshape(t_dev, n_out, hi - lo)

        put(0, half - 128, main[:, 0 : half - 128])
        put(half - 128, half, main[:, half - 128 : half] + jnp.where(upper, swapped, 0.0))
        put(half, cells - 128, main[:, half : cells - 128])
        put(cells - 128, cells, main[:, cells - 128 :] + jnp.where(upper, blend, 0.0))


def join(my_neighbours, main, strips):
    n_out, per, cells = main.shape
    n_facet = strips.shape[0]
    strips = strips.reshape(n_facet, n_out, 2, per // 2, 2 * STRIP)
    return pl.pallas_call(
        join_kernel,
        out_shape=jax.ShapeDtypeStruct((per // 2, 2, n_out, cells), jnp.float32),
        in_specs=[pl.BlockSpec(memory_space=pltpu.SMEM)] + [vmem()] * 2,
        out_specs=vmem(),
        compiler_params=pltpu.CompilerParams(vmem_limit_bytes=16 * MIB),
        name="join",
    )(my_neighbours, main, strips)


def exchange(x, axis):
    return lax.all_to_all(x, axis, split_axis=0, concat_axis=0, tiled=True)


def local(visibilities, kernels, delays, tile_of, plane_of, counts, neighbours):
    n_facet = lax.axis_size("facet")
    n_chan = lax.axis_size("chan")
    facet_index = lax.axis_index("facet")
    chan_index = lax.axis_index("chan")
    halves, facets, blocks, _, bv = visibilities.shape
    fac_dev = facets // n_facet
    n_out = n_chan
    n_tiles = 16 * n_chan
    t_dev = n_tiles // n_chan
    n_rows = fac_dev * blocks
    per = n_rows // n_chan

    vis = send_order(visibilities.reshape(halves, n_facet * n_chan, per, bv))
    vis = exchange(vis, ("facet", "chan"))
    delay = lax.dynamic_index_in_dim(delays.reshape(n_chan, per, bv), chan_index, 0, keepdims=False)
    inner, outer = turns(delay, n_out)
    live = jnp.arange(blocks, dtype=jnp.int32)[None, :] < counts[:, None]
    planes = jnp.where(live, plane_of, -1).reshape(1, n_rows)
    order, tiles, piece = tables(planes, tile_of.reshape(1, n_rows), kernels.shape[0], n_tiles, t_dev)

    rows = exchange(average(vis, inner, outer), "chan")
    grids = grid_rows(piece, rows, order, tiles, kernels, n_chan)
    main = exchange(grids, "chan")
    strips = exchange(strips_for_each(main, n_facet), "facet")
    my_neighbours = lax.dynamic_slice_in_dim(neighbours, facet_index * fac_dev, fac_dev, 0)
    return join(my_neighbours, main, strips)


def solution(mesh):
    return jax.shard_map(
        local,
        mesh=mesh,
        in_specs=(
            P(None, None, None, ("facet", "chan"), None),
            P(),
            P("facet", None, None),
            P("facet", None),
            P("facet", None),
            P("facet"),
            P(),
        ),
        out_specs=P("chan", "facet", None, None),
        check_vma=False,
    )
```

time: 302 us -> 137 us (0.45)
  Pallas kernels: 100 us -> 17.7 us
  starting transfers between devices: 51.1 us -> 22.2 us
  blocking collectives: 38.1 us -> 12.4 us
  waiting for transfers between devices: 91.8 us -> 72.8 us
  local copies, waits for them, and re-layouts: 17.5 us -> 11.4 us
    pallas_call x5 -> x6, Pallas kernels: 90.6 us -> 13.3 us  [the longest x1 6.52 us: grid_rows(): pl.pallas_call(functools.partial(grid_kernel, n_rows // PIECE + n_planes)...]
    all_to_all x10 -> x3, starting transfers between devices: 51.1 us -> 22.2 us  [exchange(): return lax.all_to_all(x, axis, split_axis=0, concat_axis=0, tiled=True)]
    all_to_all x2 -> x1, blocking collectives: 38.1 us -> 12.4 us  [exchange(): return lax.all_to_all(x, axis, split_axis=0, concat_axis=0, tiled=True)]
    all_to_all x10 -> x3, waiting for transfers between devices: 91.8 us -> 72.8 us  [exchange(): return lax.all_to_all(x, axis, split_axis=0, concat_axis=0, tiled=True)]
    unnamed x31 -> x23, local copies, waits for them, and re-layouts: 1.54 us -> 11.3 us
    transpose x4 -> x0, local copies, waits for them, and re-layouts: 5.96 us -> none  [local(): jnp.transpose(piece, (1, 2, 0, 3, 4))]
    pallas_call x4 -> x1, Pallas kernels: 9.41 us -> 4.41 us  [average(): pl.pallas_call(average_kernel, out_shape=jax.ShapeDtypeStruct((n_ch // AV...]
    slice x3 -> x0, local copies, waits for them, and re-layouts: 3.07 us -> none  [the longest x1 1.41 us: local(): piece = lax.slice_in_dim(vis[:, :, slot], begin, begin + length, axis=2)]
  transfers between devices with their start and end apart: 10 -> 3, of which waited for: 8 -> 3; matrix products, arithmetic and copies ran while one was open for 4% -> 0% of each run, Pallas kernels for 32% -> 2%
where the time goes in v2:
time: 137 us
  waiting for transfers between devices  72.8 us (53%)
  starting transfers between devices  22.2 us (16%)
  Pallas kernels  17.7 us (13%)
  blocking collectives  12.4 us (9%)
  local copies, waits for them, and re-layouts  11.4 us (8%)
    all_to_all x3, waiting for transfers between devices, exchange(): return lax.all_to_all(x, axis, split_axis=0, concat_axis=0, tiled=True)  72.8 us
    all_to_all x3, starting transfers between devices, exchange(): return lax.all_to_all(x, axis, split_axis=0, concat_axis=0, tiled=True)  22.2 us
    all_to_all x1, blocking collectives, exchange(): return lax.all_to_all(x, axis, split_axis=0, concat_axis=0, tiled=True)  12.4 us
    unnamed x23, local copies, waits for them, and re-layouts  11.3 us
    pallas_call x1, Pallas kernels, grid_rows(): pl.pallas_call(functools.partial(grid_kernel, n_rows // PIECE + n_planes)...  6.52 us
    pallas_call x1, Pallas kernels, average(): pl.pallas_call(average_kernel, out_shape=jax.ShapeDtypeStruct((n_ch // AV...  4.41 us
  transfers between devices with their start and end apart: 3, of which 3 were waited for; matrix products, arithmetic and copies ran while one was open for 0% of the time, Pallas kernels for 2%

profile of v2, /device:TPU:1, one launch (start us, length us, event | category | flops | bytes accessed | tf_op | source)
XLA Modules:
  0.0 136.7 jit_solution(11981899781216297776)
XLA Ops:
  0.0 0.0 copy-start
  0.0 0.0 copy-start.3
  0.0 2.2 %copy-done.3 = bf16[2,16,512,1,128]{4,2,3,1,0:T(8,128)(2,1)S(1)} copy-done((bf16[2,16,512,1,128]{4,2,3,1,0:T(8,128)(2,1)S(1)}, bf16[2,16,512,1,128]{4,2,3,1,0:T(8,128)(2,1)}, u32[]{:S(2)}) %copy-start.3) | copy-done | bytes 4194328
  2.2 0.8 send_order.1
  3.1 0.0 copy-start.1
  3.1 2.0 %copy-done.1 = bf16[128,2,64,128]{3,2,1,0:T(8,128)(2,1)} copy-done((bf16[128,2,64,128]{3,2,1,0:T(8,128)(2,1)}, bf16[128,2,64,128]{3,2,1,0:T(8,128)(2,1)S(1)}, u32[]{:S(2)}) %copy-start.1) | copy-done | bytes 4194328
  5.0 11.9 %all-to-all-start = ((bf16[128,2,64,128]{3,2,1,0:T(8,128)(2,1)}), bf16[128,2,64,128]{3,2,1,0:T(8,128)(2,1)}, u32[]{:S(2)}, u32[]{:S(2)}) async-start(bf16[128,2,64,128]{3,2,1,0:T(8,128)(2,1)} %copy-done.1), calls=%async_computation | async-start | bytes 8388608 | tf_op jit(solution)/shard_map/all_to_all | solution.py:317
  17.0 0.0 copy-start.6
  17.0 0.0 copy-start.9
  17.0 0.0 copy-start.7
  17.0 0.0 copy-done
  17.1 0.3 turns.1
  17.3 52.0 %all-to-all-done.vis_ref = bf16[128,2,64,128]{3,2,1,0:T(8,128)(2,1)} async-done(((bf16[128,2,64,128]{3,2,1,0:T(8,128)(2,1)}), bf16[128,2,64,128]{3,2,1,0:T(8,128)(2,1)}, u32[]{:S(2)}, u32[]{:S(2)}) %all-to-all-start) | async-done | bytes 4194336 | tf_op jit(solution)/shard_map/all_to_all | solution.py:317
  69.3 4.4 %average.1 = bf16[16,2,64,128]{3,2,1,0:T(8,128)(2,1)} custom-call(bf16[128,2,64,128]{3,2,1,0:T(8,128)(2,1)} %all-to-all-done.vis_ref, f32[7,2,64,128]{3,2,1,0:T(8,128)S(1)} %get-tuple-element.11.inner_ref, f32[16,2,64,128]{3,2,1,0:T(8,128)S(1)} %get-tuple-element.12.outer_ref), custom_call_target="tpu_custom_call" | custom-call | tf_op jit(solution)/shard_map/average/pallas_call | solution.py:134
  73.7 3.6 %all-to-all-start.1 = ((bf16[16,2,64,128]{3,2,1,0:T(8,128)(2,1)}), bf16[16,2,64,128]{3,2,1,0:T(8,128)(2,1)S(1)}, u32[]{:S(2)}, u32[]{:S(2)}) async-start(bf16[16,2,64,128]{3,2,1,0:T(8,128)(2,1)} %average.1), calls=%async_computation.1 | async-start | bytes 1048576 | tf_op jit(solution)/shard_map/all_to_all | solution.py:317
  77.3 0.0 copy-done.6
  77.3 0.0 copy-done.9
  77.3 0.1 fusion
  77.4 0.0 copy-done.7
  77.4 2.5 %tables.1 = (bf16[1568,1024]{1,0:T(8,128)(2,1)S(1)}, bf16[512,1536]{1,0:T(8,128)(2,1)S(1)}, s32[8,128]{1,0:T(8,128)S(1)}) custom-call(s32[1,1024]{1,0:T(1,128)S(1)} %bitcast.15, s32[1,1024]{1,0:T(1,128)S(1)} %bitcast.16), custom_call_target="tpu_custom_call" | custom-call | tf_op jit(solution)/shard_map/tables/pallas_call | solution.py:202
  79.9 0.0 copy-start.4
  79.9 1.7 %copy-done.4 = bf16[1568,1024]{1,0:T(8,128)(2,1)} copy-done((bf16[1568,1024]{1,0:T(8,128)(2,1)}, bf16[1568,1024]{1,0:T(8,128)(2,1)S(1)}, u32[]{:S(2)}) %copy-start.4) | copy-done | bytes 3211288
  81.6 6.0 %all-to-all-done.1.rows_ref = bf16[16,2,64,128]{3,2,1,0:T(8,128)(2,1)S(1)} async-done(((bf16[16,2,64,128]{3,2,1,0:T(8,128)(2,1)}), bf16[16,2,64,128]{3,2,1,0:T(8,128)(2,1)S(1)}, u32[]{:S(2)}, u32[]{:S(2)}) %all-to-all-start.1) | async-done | bytes 524320 | tf_op jit(solution)/shard_map/all_to_all | solution.py:317
  87.5 0.0 copy-start.2
  87.5 3.4 %copy-done.2 = bf16[32,256,512]{2,1,0:T(8,128)(2,1)S(1)} copy-done((bf16[32,256,512]{2,1,0:T(8,128)(2,1)S(1)}, bf16[32,256,512]{2,1,0:T(8,128)(2,1)}, u32[]{:S(2)}) %copy-start.2) | copy-done | bytes 8388632
  90.9 0.0 copy-start.5
  90.9 1.9 %copy-done.5 = bf16[1568,1024]{1,0:T(8,128)(2,1)S(1)} copy-done((bf16[1568,1024]{1,0:T(8,128)(2,1)S(1)}, bf16[1568,1024]{1,0:T(8,128)(2,1)}, u32[]{:S(2)}) %copy-start.5) | copy-done | bytes 3211288
  92.8 6.5 %grid_rows.1 = bf16[16,32,512]{2,1,0:T(8,128)(2,1)S(1)} custom-call(s32[8,128]{1,0:T(8,128)S(1)} %get-tuple-element.10.piece_ref, bf16[16,2,64,128]{3,2,1,0:T(8,128)(2,1)S(1)} %all-to-all-done.1.rows_ref, bf16[1568,1024]{1,0:T(8,128)(2,1)S(1)} %copy-done.5, bf16[512,1536]{1,0:T(8,128)(2,1)S(1)} %get-tuple-element.14.tiles_ref, ...), custom_call_target="tpu_custom_call" | custom-call | tf_op jit(solution)/shard_map/grid_rows/pallas_call | solution.py:235
  99.3 0.0 copy-start.8
  99.4 12.4 %all_to_all.20.main_ref = bf16[16,32,512]{2,1,0:T(8,128)(2,1)S(1)} all-to-all(bf16[16,32,512]{2,1,0:T(8,128)(2,1)S(1)} %grid_rows.1), channel_id=1, replica_groups=mesh['facet'=8,'chan'=16] {'chan'}, dimensions={0} | all-to-all | bytes 1048576 | tf_op jit(solution)/shard_map/all_to_all | solution.py:317
  111.8 1.1 strips.1
  112.9 6.7 %all-to-all-start.3 = ((bf16[8,16,32,128]{3,2,1,0:T(8,128)(2,1)}), bf16[8,16,32,128]{3,2,1,0:T(8,128)(2,1)S(1)}, u32[]{:S(2)}, u32[]{:S(2)}) async-start(bf16[8,16,32,128]{3,2,1,0:T(8,128)(2,1)} %strips.1), calls=%async_computation.3 | async-start | bytes 2097152 | tf_op jit(solution)/shard_map/all_to_all | solution.py:317
  119.6 0.0 copy-done.8
  119.6 0.1 constant_dynamic-slice_fusion
  119.7 0.1 copy.9.nb_ref
  119.8 14.8 %all-to-all-done.3 = bf16[8,16,32,128]{3,2,1,0:T(8,128)(2,1)S(1)} async-done(((bf16[8,16,32,128]{3,2,1,0:T(8,128)(2,1)}), bf16[8,16,32,128]{3,2,1,0:T(8,128)(2,1)S(1)}, u32[]{:S(2)}, u32[]{:S(2)}) %all-to-all-start.3) | async-done | bytes 1048608 | tf_op jit(solution)/shard_map/all_to_all | solution.py:317
  134.6 2.1 %join.1 = f32[16,2,16,512]{3,2,1,0:T(8,128)} custom-call(s32[2,4]{1,0:T(2,128)S(1)} %copy.9.nb_ref, bf16[16,32,512]{2,1,0:T(8,128)(2,1)S(1)} %all_to_all.20.main_ref, bf16[8,16,2,16,128]{4,3,2,1,0:T(8,128)(2,1)S(1)} %bitcast.13), custom_call_target="tpu_custom_call" | custom-call | tf_op jit(solution)/shard_map/join/pallas_call | solution.py:306
  (3 shorter events, 0.0 us)
Async XLA Ops:
  0.0 17.0 %copy-start = (f32[2,512,128]{2,1,0:T(8,128)S(1)}, f32[2,512,128]{2,1,0:T(8,128)}, u32[]{:S(2)}) copy-start(f32[2,512,128]{2,1,0:T(8,128)} %param.9) | copy-start | bytes 1572868
  0.0 2.2 %copy-start.3 = (bf16[2,16,512,1,128]{4,2,3,1,0:T(8,128)(2,1)S(1)}, bf16[2,16,512,1,128]{4,2,3,1,0:T(8,128)(2,1)}, u32[]{:S(2)}) copy-start(bf16[2,16,512,1,128]{4,2,3,1,0:T(8,128)(2,1)} %param.7) | copy-start | bytes 12582916
  3.1 2.0 %copy-start.1 = (bf16[128,2,64,128]{3,2,1,0:T(8,128)(2,1)}, bf16[128,2,64,128]{3,2,1,0:T(8,128)(2,1)S(1)}, u32[]{:S(2)}) copy-start(bf16[128,2,64,128]{3,2,1,0:T(8,128)(2,1)S(1)} %send_order.1) | copy-start | bytes 12582916
  5.0 64.3 %all-to-all-start = ((bf16[128,2,64,128]{3,2,1,0:T(8,128)(2,1)}), bf16[128,2,64,128]{3,2,1,0:T(8,128)(2,1)}, u32[]{:S(2)}, u32[]{:S(2)}) async-start(bf16[128,2,64,128]{3,2,1,0:T(8,128)(2,1)} %copy-done.1), calls=%async_computation | async-start | bytes 8388608 | tf_op jit(solution)/shard_map/all_to_all | solution.py:317
  17.0 60.3 %copy-start.6 = (s32[2,512]{1,0:T(2,128)S(1)}, s32[2,512]{1,0:T(2,128)}, u32[]{:S(2)}) copy-start(s32[2,512]{1,0:T(2,128)} %param.11) | copy-start | bytes 12292
  17.0 60.3 %copy-start.9 = (s32[2]{0:T(128)S(1)}, s32[2]{0:T(128)}, u32[]{:S(2)}) copy-start(s32[2]{0:T(128)} %param.12) | copy-start | bytes 28
  17.0 60.4 %copy-start.7 = (s32[2,512]{1,0:T(2,128)S(1)}, s32[2,512]{1,0:T(2,128)}, u32[]{:S(2)}) copy-start(s32[2,512]{1,0:T(2,128)} %param.10) | copy-start | bytes 12292
  73.7 13.8 %all-to-all-start.1 = ((bf16[16,2,64,128]{3,2,1,0:T(8,128)(2,1)}), bf16[16,2,64,128]{3,2,1,0:T(8,128)(2,1)S(1)}, u32[]{:S(2)}, u32[]{:S(2)}) async-start(bf16[16,2,64,128]{3,2,1,0:T(8,128)(2,1)} %average.1), calls=%async_computation.1 | async-start | bytes 1048576 | tf_op jit(solution)/shard_map/all_to_all | solution.py:317
  79.9 1.7 %copy-start.4 = (bf16[1568,1024]{1,0:T(8,128)(2,1)}, bf16[1568,1024]{1,0:T(8,128)(2,1)S(1)}, u32[]{:S(2)}) copy-start(bf16[1568,1024]{1,0:T(8,128)(2,1)S(1)} %get-tuple-element.13.order_ref) | copy-start | bytes 9633796
  87.5 3.4 %copy-start.2 = (bf16[32,256,512]{2,1,0:T(8,128)(2,1)S(1)}, bf16[32,256,512]{2,1,0:T(8,128)(2,1)}, u32[]{:S(2)}) copy-start(bf16[32,256,512]{2,1,0:T(8,128)(2,1)} %k_ref.1) | copy-start | bytes 25165828
  90.9 1.9 %copy-start.5 = (bf16[1568,1024]{1,0:T(8,128)(2,1)S(1)}, bf16[1568,1024]{1,0:T(8,128)(2,1)}, u32[]{:S(2)}) copy-start(bf16[1568,1024]{1,0:T(8,128)(2,1)} %copy-done.4) | copy-start | bytes 9633796
  99.3 20.2 %copy-start.8 = (s32[16,4]{0,1:T(4,128)S(1)}, s32[16,4]{0,1:T(4,128)}, u32[]{:S(2)}) copy-start(s32[16,4]{0,1:T(4,128)} %param.13) | copy-start | bytes 772
  112.9 21.7 %all-to-all-start.3 = ((bf16[8,16,32,128]{3,2,1,0:T(8,128)(2,1)}), bf16[8,16,32,128]{3,2,1,0:T(8,128)(2,1)S(1)}, u32[]{:S(2)}, u32[]{:S(2)}) async-start(bf16[8,16,32,128]{3,2,1,0:T(8,128)(2,1)} %strips.1), calls=%async_computation.3 | async-start | bytes 2097152 | tf_op jit(solution)/shard_map/all_to_all | solution.py:317

commit v3 on v2

v3 whole, which is shorter than its diff:
```python
import functools
import math

import jax
import jax.numpy as jnp
from jax import lax
from jax.experimental import pallas as pl
from jax.experimental.pallas import tpu as pltpu
from jax.sharding import PartitionSpec as P

AVG = 8
TS = 16
EDGE = 4
STRIP = EDGE * TS
GROUP = 16
PIECE = 64
MIB = 1024 * 1024

SIN = (-1.0 / 6, 1.0 / 120, -1.0 / 5040, 1.0 / 362880, -1.0 / 39916800)
COS = (-1.0 / 2, 1.0 / 24, -1.0 / 720, 1.0 / 40320, -1.0 / 3628800, 1.0 / 479001600)


def series(turns):
    x = (2.0 * math.pi) * turns
    y = x * x
    s = jnp.full_like(x, SIN[-1])
    for k in SIN[-2::-1]:
        s = s * y + k
    c = jnp.full_like(x, COS[-1])
    for k in COS[-2::-1]:
        c = c * y + k
    return c * y + 1.0, (s * y + 1.0) * x


def turn_by(turns):
    half = jnp.round(2.0 * turns)
    c, s = series(turns - 0.5 * half)
    odd = (half - 2.0 * jnp.floor(0.5 * half)) > 0.5
    sign = jnp.where(odd, -1.0, 1.0)
    return c * sign, s * sign


def times(a, b):
    return a[0] * b[0] - a[1] * b[1], a[0] * b[1] + a[1] * b[0]


def vmem():
    return pl.BlockSpec(memory_space=pltpu.VMEM)


def send_kernel(vis_ref, out_ref, sem):
    halves, dests = vis_ref.shape[:2]
    n = sem.shape[1]
    copies = []
    for h in range(halves):
        for i in range(n):
            at = pl.ds(i * (dests // n), dests // n)
            copies.append(pltpu.make_async_copy(vis_ref.at[h, at], out_ref.at[at, h], sem.at[h, i]))
    for copy in copies:
        copy.start()
    for copy in copies:
        copy.wait()


def send_order(vis):
    halves, dests, rows, bv = vis.shape
    return pl.pallas_call(
        send_kernel,
        out_shape=pltpu.HBM((dests, halves, rows, bv), vis.dtype),
        in_specs=[pl.BlockSpec(memory_space=pltpu.HBM)],
        out_specs=pl.BlockSpec(memory_space=pltpu.HBM),
        scratch_shapes=[pltpu.SemaphoreType.DMA((halves, 4))],
        compiler_params=pltpu.CompilerParams(vmem_limit_bytes=1 * MIB),
        name="send_order",
    )(pltpu.with_memory_space_constraint(vis, pltpu.HBM))


def fill_turns(d, inner_ref, outer_ref):
    small = series(d * (1.0 / 256.0))
    table = [None, small]
    for j in range(2, AVG):
        table.append(times(table[j // 2], table[j - j // 2]))
    for j in range(1, AVG):
        inner_ref[j - 1, 0] = table[j][0]
        inner_ref[j - 1, 1] = table[j][1]
    c, s = turn_by(d)
    turn = (c * (1.0 / AVG), s * (1.0 / AVG))
    step = series(d * (1.0 / 32.0))
    for o in range(outer_ref.shape[0]):
        outer_ref[o, 0] = turn[0]
        outer_ref[o, 1] = turn[1]
        turn = times(turn, step)


def average_kernel(piece_ref, delay_ref, vis_hbm, out_ref, vis_ref, inner_ref, outer_ref, sem):
    n_out, _, rows, _ = out_ref.shape
    steps = sem.shape[0]
    size = vis_ref.shape[0] // steps
    copies = []
    for i in range(steps):
        at = pl.ds(i * size, size)
        copies.append(pltpu.make_async_copy(vis_hbm.at[at], vis_ref.at[at], sem.at[i]))
        copies[-1].start()
    fill_turns(delay_ref[...], inner_ref, outer_ref)
    for i in range(steps):
        copies[i].wait()
        for r in range(0, rows, 16):
            at = slice(r, r + 16)
            table = [(inner_ref[j, 0, at], inner_ref[j, 1, at]) for j in range(AVG - 1)]

            def one(o, carry, at=at, table=table):
                c = o * AVG
                re = vis_ref[c, 0, at].astype(jnp.float32)
                im = vis_ref[c, 1, at].astype(jnp.float32)
                for j in range(1, AVG):
                    a = vis_ref[c + j, 0, at].astype(jnp.float32)
                    b = vis_ref[c + j, 1, at].astype(jnp.float32)
                    tc, ts = table[j - 1]
                    re += a * tc - b * ts
                    im += a * ts + b * tc
                tc = outer_ref[o, 0, at]
                ts = outer_ref[o, 1, at]
                out_ref[o, 0, at] = (re * tc - im * ts).astype(jnp.bfloat16)
                out_ref[o, 1, at] = (re * ts + im * tc).astype(jnp.bfloat16)
                return carry

            n = n_out // steps
            lax.fori_loop(i * n, (i + 1) * n, one, 0, unroll=n)


def average(piece, vis, delay):
    n_ch, halves, rows, bv = vis.shape
    n_out = n_ch // AVG
    return pl.pallas_call(
        average_kernel,
        out_shape=jax.ShapeDtypeStruct((n_out, halves, rows, bv), jnp.bfloat16),
        in_specs=[vmem(), vmem(), pl.BlockSpec(memory_space=pltpu.HBM)],
        out_specs=vmem(),
        scratch_shapes=[
            pltpu.VMEM(vis.shape, vis.dtype),
            pltpu.VMEM((AVG - 1, 2, rows, bv), jnp.float32),
            pltpu.VMEM((n_out, 2, rows, bv), jnp.float32),
            pltpu.SemaphoreType.DMA((4,)),
        ],
        compiler_params=pltpu.CompilerParams(vmem_limit_bytes=12 * MIB),
        name="average",
    )(piece, delay, pltpu.with_memory_space_constraint(vis, pltpu.HBM))


def to_bf16(mask):
    return mask.astype(jnp.float32).astype(jnp.bfloat16)


def iota(shape, dim):
    return lax.broadcasted_iota(jnp.int32, shape, dim)


def tables_kernel(n_planes, n_order, t_dev, plane_ref, tile_ref, place_ref, code_ref, piece_ref):
    n_rows = plane_ref.shape[1]
    f32 = jnp.float32
    plane = plane_ref[...]
    mine = plane == iota((n_planes, n_rows), 0)
    before = to_bf16(iota((n_rows, n_rows), 0) < iota((n_rows, n_rows), 1))
    rank = jnp.dot(to_bf16(mine), before, preferred_element_type=f32)
    count = jnp.sum(mine.astype(f32), axis=1, keepdims=True)
    groups = jnp.floor((count + (GROUP - 1)) * (1.0 / GROUP))
    pieces = jnp.floor((groups + (PIECE // GROUP - 1)) * (GROUP / PIECE))
    earlier = to_bf16(iota((n_planes, n_planes), 1) < iota((n_planes, n_planes), 0))
    both = jnp.concatenate(
        [jnp.broadcast_to(groups, (n_planes, 128)), jnp.broadcast_to(pieces, (n_planes, 128))], axis=1
    )
    both = jnp.dot(earlier, both.astype(jnp.bfloat16), preferred_element_type=f32)
    first_group = both[:, 0:1]
    first_piece = both[:, 128:129]
    place = jnp.sum(jnp.where(mine, rank + GROUP * first_group, 0.0), axis=0, keepdims=True)
    live = jnp.sum(mine.astype(f32), axis=0, keepdims=True)
    place = jnp.where(live > 0.5, place, -1.0).astype(jnp.int32)
    place_ref[...] = place
    order = to_bf16(iota((n_order, n_rows), 0) == place)

    row = iota((8, n_rows), 0)
    slot = (iota((8, n_rows), 1) >= n_rows // 2).astype(f32)
    values = jnp.where(row == 0, tile_ref[...].astype(f32) + 1.0, jnp.where(row == 1, slot, 0.0))
    n_used = code_ref.shape[1]
    ordered = lax.dot_general(
        values.astype(jnp.bfloat16), order[:n_used], (((1,), (1,)), ((), ())), preferred_element_type=f32
    )
    tile = ordered[0:1].astype(jnp.int32) - 1
    slot = ordered[1:2].astype(jnp.int32)
    code = (tile // t_dev) * (2 * t_dev) + slot * t_dev + tile % t_dev
    code_ref[...] = jnp.where(tile < 0, -1, code)

    total = jnp.sum(pieces)
    which = jnp.minimum(iota((n_planes, 128), 1).astype(f32), total - 1.0)
    taken = (which >= first_piece) & (which < first_piece + pieces)
    group = first_group + (PIECE // GROUP) * (which - first_piece)
    group = jnp.sum(jnp.where(taken, group, 0.0), axis=0, keepdims=True)
    owner = jnp.sum(jnp.where(taken, iota((n_planes, 128), 0).astype(f32), 0.0), axis=0, keepdims=True)
    row = iota((8, 128), 0)
    piece_ref[...] = jnp.where(row == 0, group, jnp.where(row == 1, owner, 0.0)).astype(jnp.int32)


def sizes(n_rows, n_planes):
    used = n_rows + n_planes * (GROUP - 1)
    n_order = -(-(used - GROUP + PIECE) // 32) * 32
    n_used = -(-used // 256) * 256
    assert n_used <= n_order
    return n_order, n_used


def tables(planes, tiles, n_planes, t_dev):
    n_rows = planes.shape[1]
    n_order, n_used = sizes(n_rows, n_planes)
    return pl.pallas_call(
        functools.partial(tables_kernel, n_planes, n_order, t_dev),
        out_shape=[
            jax.ShapeDtypeStruct((1, n_rows), jnp.int32),
            jax.ShapeDtypeStruct((1, n_used), jnp.int32),
            jax.ShapeDtypeStruct((8, 128), jnp.int32),
        ],
        in_specs=[vmem()] * 2,
        out_specs=[vmem()] * 3,
        compiler_params=pltpu.CompilerParams(vmem_limit_bytes=40 * MIB),
        name="tables",
    )(planes, tiles)


def grid_kernel(n_pieces, piece_ref, place_ref, code_ref, rows_ref, k_hbm, out_ref, k_ref, x_ref, c_ref, sem):
    n_fetch = sem.shape[0]
    part = k_ref.shape[0] // n_fetch
    fetches = []
    for i in range(n_fetch):
        at = pl.ds(i * part, part)
        fetches.append(pltpu.make_async_copy(k_hbm.at[at], k_ref.at[at], sem.at[i]))
        fetches[-1].start()
    n_src, _, per, bv = rows_ref.shape
    n_order = x_ref.shape[0]
    re = rows_ref[:, 0].reshape(n_src * per, bv)
    im = rows_ref[:, 1].reshape(n_src * per, bv)
    x = jnp.concatenate([re, im], axis=1)
    order = to_bf16(iota((n_order, n_src * per), 0) == place_ref[...])
    x_ref[...] = jnp.dot(order, x, preferred_element_type=jnp.float32).astype(jnp.bfloat16)
    n_used = code_ref.shape[1]
    n_codes = out_ref.shape[0] * out_ref.shape[1]
    tiles = to_bf16(iota((n_codes, n_used), 0) == code_ref[...])
    c_ref[...] = jnp.zeros_like(c_ref)
    for fetch in fetches:
        fetch.wait()
    for i in range(n_pieces):
        at = pl.ds(pl.multiple_of(piece_ref[0, i] * GROUP, GROUP), PIECE)
        product = jnp.dot(x_ref[at, :], k_ref[piece_ref[1, i]], preferred_element_type=jnp.float32)
        c_ref[at, :] = product.astype(jnp.bfloat16)
    grid = jnp.dot(tiles, c_ref[:n_used, :], preferred_element_type=jnp.float32)
    out_ref[...] = grid.astype(jnp.bfloat16).reshape(out_ref.shape)


def grid_rows(piece, place, code, rows, kernels, n_codes):
    n_planes, k_rows, cells = kernels.shape
    n_rows = place.shape[1]
    n_chan = rows.shape[0]
    n_order, n_used = sizes(n_rows, n_planes)
    return pl.pallas_call(
        functools.partial(grid_kernel, n_rows // PIECE + n_planes),
        out_shape=jax.ShapeDtypeStruct((n_chan, n_codes // n_chan, cells), jnp.bfloat16),
        in_specs=[pl.BlockSpec(memory_space=pltpu.SMEM)] + [vmem()] * 3 + [pl.BlockSpec(memory_space=pltpu.HBM)],
        out_specs=vmem(),
        scratch_shapes=[
            pltpu.VMEM(kernels.shape, kernels.dtype),
            pltpu.VMEM((n_order, k_rows), jnp.bfloat16),
            pltpu.VMEM((n_order, cells), jnp.bfloat16),
            pltpu.SemaphoreType.DMA((8,)),
        ],
        compiler_params=pltpu.CompilerParams(vmem_limit_bytes=40 * MIB),
        name="grid_rows",
    )(piece, place, code, rows, pltpu.with_memory_space_constraint(kernels, pltpu.HBM))


def strip_kernel(main_ref, out_ref):
    n_out, per, cells = main_ref.shape
    half = cells // 2
    low = main_ref[:, :, 0:128].reshape(n_out * per, 128).astype(jnp.float32)
    high = main_ref[:, :, half : half + 128].reshape(n_out * per, 128).astype(jnp.float32)
    lane = lax.broadcasted_iota(jnp.int32, low.shape, 1)
    strip = jnp.where(lane < STRIP, low, pltpu.roll(high, STRIP, 1)).astype(jnp.bfloat16)
    out_ref[...] = strip.reshape(out_ref.shape)


def strips_of(main):
    n_out, per, _ = main.shape
    return pl.pallas_call(
        strip_kernel,
        out_shape=jax.ShapeDtypeStruct((n_out, per, 2 * STRIP), jnp.bfloat16),
        in_specs=[vmem()],
        out_specs=vmem(),
        compiler_params=pltpu.CompilerParams(vmem_limit_bytes=8 * MIB),
        name="strips",
    )(main)


def join_kernel(nb_ref, main_ref, *refs):
    strips, out_ref, strip_ref = refs[:-2], refs[-2], refs[-1]
    n_out, per, cells = main_ref.shape
    t_dev = per // 2
    half = cells // 2
    n_rows = n_out * t_dev
    for i, ref in enumerate(strips):
        strip_ref[i] = ref[...].reshape(strip_ref.shape[1:])
    upper = iota((n_rows, 2 * STRIP), 1) >= STRIP
    to = iota((n_rows, n_rows), 0)
    place = (iota((n_rows, n_rows), 1) == (to % n_out) * t_dev + to // n_out).astype(jnp.float32)
    quarter = (0.25 * place).astype(jnp.bfloat16)
    place = place.astype(jnp.bfloat16)
    n_nb = nb_ref.shape[1] // 2
    for slot in range(2):
        blend = jnp.zeros((n_rows, 2 * STRIP), jnp.float32)
        for k in range(n_nb):
            strip = strip_ref[nb_ref[slot, k], :, nb_ref[slot, n_nb + k]].reshape(n_rows, 2 * STRIP)
            blend += jnp.dot(quarter, strip, preferred_element_type=jnp.float32)
        swapped = pltpu.roll(blend, STRIP, 1)
        main = main_ref[:, slot * t_dev : (slot + 1) * t_dev, :].reshape(n_rows, cells)
        main = jnp.dot(place, main, preferred_element_type=jnp.float32)

        def put(lo, hi, value, slot=slot):
            out_ref[:, slot, :, lo:hi] = value.reshape(t_dev, n_out, hi - lo)

        put(0, half - 128, main[:, 0 : half - 128])
        put(half - 128, half, main[:, half - 128 : half] + jnp.where(upper, swapped, 0.0))
        put(half, cells - 128, main[:, half : cells - 128])
        put(cells - 128, cells, main[:, cells - 128 :] + jnp.where(upper, blend, 0.0))


def join(sources, main, strips):
    n_out, per, cells = main.shape
    return pl.pallas_call(
        join_kernel,
        out_shape=jax.ShapeDtypeStruct((per // 2, 2, n_out, cells), jnp.float32),
        in_specs=[pl.BlockSpec(memory_space=pltpu.SMEM)] + [vmem()] * (1 + len(strips)),
        out_specs=vmem(),
        scratch_shapes=[pltpu.VMEM((len(strips), n_out, 2, per // 2, 2 * STRIP), jnp.bfloat16)],
        compiler_params=pltpu.CompilerParams(vmem_limit_bytes=16 * MIB),
        name="join",
    )(sources, main, *strips)


def exchange(x, axis):
    return lax.all_to_all(x, axis, split_axis=0, concat_axis=0, tiled=True)


def local(visibilities, kernels, delays, tile_of, plane_of, counts, neighbours):
    n_facet = lax.axis_size("facet")
    n_chan = lax.axis_size("chan")
    facet_index = lax.axis_index("facet")
    chan_index = lax.axis_index("chan")
    halves, facets, blocks, _, bv = visibilities.shape
    fac_dev = facets // n_facet
    n_tiles = 16 * n_chan
    t_dev = n_tiles // n_chan
    n_rows = fac_dev * blocks
    per = n_rows // n_chan

    vis = send_order(visibilities.reshape(halves, n_facet * n_chan, per, bv))
    vis = exchange(vis, ("facet", "chan"))
    delay = lax.dynamic_index_in_dim(delays.reshape(n_chan, per, bv), chan_index, 0, keepdims=False)
    live = jnp.arange(blocks, dtype=jnp.int32)[None, :] < counts[:, None]
    planes = jnp.where(live, plane_of, -1).reshape(1, n_rows)
    place, code, piece = tables(planes, tile_of.reshape(1, n_rows), kernels.shape[0], t_dev)

    rows = exchange(average(piece, vis, delay), "chan")
    grids = grid_rows(piece, place, code, rows, kernels, fac_dev * n_tiles)
    main = exchange(grids, "chan")

    own = strips_of(main)
    chips = n_facet // 2
    strips = [own]
    for dz in range(1, chips):
        strips.append(lax.ppermute(own, "facet", [(f, (f + 2 * dz) % n_facet) for f in range(n_facet)]))
    strips += [lax.ppermute(s, "facet", [(f, f ^ 1) for f in range(n_facet)]) for s in strips]
    mine = lax.dynamic_slice_in_dim(neighbours, facet_index * fac_dev, fac_dev, 0)
    group = mine // fac_dev
    source = (facet_index // 2 - group // 2) % chips + chips * ((group + facet_index) % 2)
    sources = jnp.concatenate([source, mine % fac_dev], axis=1).astype(jnp.int32)
    return join(sources, main, strips)


def solution(mesh):
    return jax.shard_map(
        local,
        mesh=mesh,
        in_specs=(
            P(None, None, None, ("facet", "chan"), None),
            P(),
            P("facet", None, None),
            P("facet", None),
            P("facet", None),
            P("facet"),
            P(),
        ),
        out_specs=P("chan", "facet", None, None),
        check_vma=False,
    )
```

time: 137 us -> 246 us (1.80)
  Pallas kernels: 17.7 us -> 144 us
  waiting for transfers between devices: 72.8 us -> 51.7 us
  blocking collectives: 12.4 us -> 25.1 us
  local copies, waits for them, and re-layouts: 11.4 us -> 0.22 us
    pallas_call x5 -> x4, Pallas kernels: 9.05 us -> 132 us  [the longest x1 128 us: send_order(): pl.pallas_call(send_kernel, out_shape=pltpu.HBM((dests, halves, rows, bv)...]
    all_to_all x3 -> x1, waiting for transfers between devices: 72.8 us -> 50.8 us  [exchange(): return lax.all_to_all(x, axis, split_axis=0, concat_axis=0, tiled=True)]
    all_to_all x1 -> x2, blocking collectives: 12.4 us -> 25.1 us  [exchange(): return lax.all_to_all(x, axis, split_axis=0, concat_axis=0, tiled=True)]
    ppermute x0 -> x7, starting transfers between devices: none -> 12.3 us  [the longest x4 9.65 us: local(): lax.ppermute(s, 'facet', [(f, f ^ 1) for f in range(n_facet)])]
    unnamed x23 -> x13, local copies, waits for them, and re-layouts: 11.3 us -> 0.14 us
    all_to_all x3 -> x1, starting transfers between devices: 22.2 us -> 12 us  [exchange(): return lax.all_to_all(x, axis, split_axis=0, concat_axis=0, tiled=True)]
    pallas_call x1, Pallas kernels: 6.52 us -> 9.79 us  [grid_rows(): pl.pallas_call(functools.partial(grid_kernel, n_rows // PIECE + n_planes)...]
  transfers between devices with their start and end apart: 3 -> 8, of which waited for: 3 -> 2; matrix products, arithmetic and copies ran while one was open for 0% -> 0% of each run, Pallas kernels for 2% -> 1%
where the time goes in v3:
time: 246 us
  Pallas kernels  144 us (59%)
  waiting for transfers between devices  51.7 us (21%)
  blocking collectives  25.1 us (10%)
  starting transfers between devices  24.3 us (10%)
    pallas_call x1, Pallas kernels, send_order(): pl.pallas_call(send_kernel, out_shape=pltpu.HBM((dests, halves, rows, bv)...  128 us
    all_to_all x1, waiting for transfers between devices, exchange(): return lax.all_to_all(x, axis, split_axis=0, concat_axis=0, tiled=True)  50.8 us
    all_to_all x2, blocking collectives, exchange(): return lax.all_to_all(x, axis, split_axis=0, concat_axis=0, tiled=True)  25.1 us
    all_to_all x1, starting transfers between devices, exchange(): return lax.all_to_all(x, axis, split_axis=0, concat_axis=0, tiled=True)  12 us
    pallas_call x1, Pallas kernels, grid_rows(): pl.pallas_call(functools.partial(grid_kernel, n_rows // PIECE + n_planes)...  9.79 us
    ppermute x4, starting transfers between devices, local(): lax.ppermute(s, 'facet', [(f, f ^ 1) for f in range(n_facet)])  9.65 us
  transfers between devices with their start and end apart: 8, of which 2 were waited for; matrix products, arithmetic and copies ran while one was open for 0% of the time, Pallas kernels for 1%

profile of v3, /device:TPU:1, one launch (start us, length us, event | category | flops | bytes accessed | tf_op | source)
XLA Modules:
  0.0 245.9 jit_solution(5037512421141093845)
XLA Ops:
  0.0 0.0 copy-start
  0.0 128.2 %send_order.1 = bf16[128,2,64,128]{3,2,1,0:T(8,128)(2,1)} custom-call(bf16[2,128,64,128]{3,2,1,0:T(8,128)(2,1)} %bitcast.14), custom_call_target="tpu_custom_call" | custom-call | tf_op jit(solution)/shard_map/send_order/pallas_call | solution.py:67
  128.2 0.0 copy-start.1
  128.2 0.0 copy-start.2
  128.3 0.0 copy-start.4
  128.3 12.0 %all-to-all-start = ((bf16[128,2,64,128]{3,2,1,0:T(8,128)(2,1)}), bf16[128,2,64,128]{3,2,1,0:T(8,128)(2,1)}, u32[]{:S(2)}, u32[]{:S(2)}) async-start(bf16[128,2,64,128]{3,2,1,0:T(8,128)(2,1)} %send_order.1), calls=%async_computation | async-start | bytes 8388608 | tf_op jit(solution)/shard_map/all_to_all | solution.py:346
  140.2 0.0 copy-done.1
  140.3 0.0 copy-done.2
  140.3 0.0 copy-done.4
  140.3 0.1 fusion
  140.4 1.3 tables.1
  141.7 0.0 copy-done
  141.7 50.8 %all-to-all-done.vis_hbm = bf16[128,2,64,128]{3,2,1,0:T(8,128)(2,1)} async-done(((bf16[128,2,64,128]{3,2,1,0:T(8,128)(2,1)}), bf16[128,2,64,128]{3,2,1,0:T(8,128)(2,1)}, u32[]{:S(2)}, u32[]{:S(2)}) %all-to-all-start) | async-done | bytes 4194336 | tf_op jit(solution)/shard_map/all_to_all | solution.py:346
  192.6 2.7 %average.1 = bf16[16,2,64,128]{3,2,1,0:T(8,128)(2,1)S(1)} custom-call(s32[8,128]{1,0:T(8,128)S(1)} %get-tuple-element.8.piece_ref, f32[64,128]{1,0:T(8,128)S(1)} %dynamic-slice_bitcast_fusion.delay_ref, bf16[128,2,64,128]{3,2,1,0:T(8,128)(2,1)} %all-to-all-done.vis_hbm), custom_call_target="tpu_custom_call" | custom-call | tf_op jit(solution)/shard_map/average/pallas_call | solution.py:134
  195.2 11.9 %all_to_all.15.rows_ref = bf16[16,2,64,128]{3,2,1,0:T(8,128)(2,1)S(1)} all-to-all(bf16[16,2,64,128]{3,2,1,0:T(8,128)(2,1)S(1)} %average.1), channel_id=1, replica_groups=mesh['facet'=8,'chan'=16] {'chan'}, dimensions={0} | all-to-all | bytes 1048576 | tf_op jit(solution)/shard_map/all_to_all | solution.py:346
  207.1 0.0 copy-start.3
  207.1 9.8 %grid_rows.1 = bf16[16,32,512]{2,1,0:T(8,128)(2,1)S(1)} custom-call(s32[8,128]{1,0:T(8,128)S(1)} %get-tuple-element.8.piece_ref, s32[1,1024]{1,0:T(1,128)S(1)} %get-tuple-element.9.place_ref, s32[1,1536]{1,0:T(1,128)S(1)} %get-tuple-element.10.code_ref, bf16[16,2,64,128]{3,2,1,0:T(8,128)(2,1)S(1)} %all_to_all.15.rows_ref, bf16[32,256,512]{2,1,0:T(8,128)(2,1)} %k_hbm.1), custom_call_target="tpu_custom_call" | custom-call | tf_op jit(solution)/shard_map/grid_rows/pallas_call | solution.py:262
  216.9 13.2 %all_to_all.16.main_ref = bf16[16,32,512]{2,1,0:T(8,128)(2,1)S(1)} all-to-all(bf16[16,32,512]{2,1,0:T(8,128)(2,1)S(1)} %grid_rows.1), channel_id=1, replica_groups=mesh['facet'=8,'chan'=16] {'chan'}, dimensions={0} | all-to-all | bytes 1048576 | tf_op jit(solution)/shard_map/all_to_all | solution.py:346
  230.1 0.1 strips.1.refs_0_
  230.2 0.5 collective-permute-start.2
  230.7 2.1 collective-permute-start.1
  232.7 0.1 collective-permute-start
  232.9 0.0 copy-done.3
  232.9 0.1 constant_dynamic-slice_fusion
  233.0 0.1 copy.9
  233.1 4.0 %collective-permute-start.3 = (bf16[16,32,128]{2,1,0:T(8,128)(2,1)S(1)}, bf16[16,32,128]{2,1,0:T(8,128)(2,1)S(1)}, u32[]{:S(2)}, u32[]{:S(2)}) collective-permute-start(bf16[16,32,128]{2,1,0:T(8,128)(2,1)S(1)} %strips.1.refs_0_), channel_id=1, source_target_pairs={{0,16},{16,0},{32,48},{48,32},{64,80},{80,64},{96,112},{112,96},{1... | collective-permute-start | bytes 393224 | tf_op jit(solution)/shard_map/ppermute | solution.py:377
  237.1 0.0 collective-permute-done.2.refs_3_
  237.1 1.8 collective-permute-start.6
  238.9 0.0 collective-permute-done.1.refs_2_
  238.9 2.1 collective-permute-start.5
  241.0 0.0 collective-permute-done.refs_1_
  241.0 1.7 collective-permute-start.4
  242.8 0.1 pad_add_fusion.nb_ref
  242.8 0.0 collective-permute-done.3.refs_4_
  242.8 0.0 collective-permute-done.6.refs_7_
  242.8 0.0 collective-permute-done.5.refs_6_
  242.8 0.9 collective-permute-done.4.refs_5_
  243.7 2.2 join.1
  (4 shorter events, 0.1 us)
Async XLA Ops:
  0.0 141.7 %copy-start = (f32[2,512,128]{2,1,0:T(8,128)S(1)}, f32[2,512,128]{2,1,0:T(8,128)}, u32[]{:S(2)}) copy-start(f32[2,512,128]{2,1,0:T(8,128)} %param.9) | copy-start | bytes 1572868
  128.2 12.0 %copy-start.1 = (s32[2,512]{1,0:T(2,128)S(1)}, s32[2,512]{1,0:T(2,128)}, u32[]{:S(2)}) copy-start(s32[2,512]{1,0:T(2,128)} %param.10) | copy-start | bytes 12292
  128.2 12.0 %copy-start.2 = (s32[2,512]{1,0:T(2,128)S(1)}, s32[2,512]{1,0:T(2,128)}, u32[]{:S(2)}) copy-start(s32[2,512]{1,0:T(2,128)} %param.11) | copy-start | bytes 12292
  128.3 12.0 %copy-start.4 = (s32[2]{0:T(128)S(1)}, s32[2]{0:T(128)}, u32[]{:S(2)}) copy-start(s32[2]{0:T(128)} %param.12) | copy-start | bytes 28
  128.3 64.3 %all-to-all-start = ((bf16[128,2,64,128]{3,2,1,0:T(8,128)(2,1)}), bf16[128,2,64,128]{3,2,1,0:T(8,128)(2,1)}, u32[]{:S(2)}, u32[]{:S(2)}) async-start(bf16[128,2,64,128]{3,2,1,0:T(8,128)(2,1)} %send_order.1), calls=%async_computation | async-start | bytes 8388608 | tf_op jit(solution)/shard_map/all_to_all | solution.py:346
  207.1 25.8 %copy-start.3 = (s32[16,4]{0,1:T(4,128)S(1)}, s32[16,4]{0,1:T(4,128)}, u32[]{:S(2)}) copy-start(s32[16,4]{0,1:T(4,128)} %param.13) | copy-start | bytes 772
  230.2 6.9 %collective-permute-start.2 = (bf16[16,32,128]{2,1,0:T(8,128)(2,1)S(1)}, bf16[16,32,128]{2,1,0:T(8,128)(2,1)S(1)}, u32[]{:S(2)}, u32[]{:S(2)}) collective-permute-start(bf16[16,32,128]{2,1,0:T(8,128)(2,1)S(1)} %strips.1.refs_0_), channel_id=1, source_target_pairs={{0,96},{16,112},{32,0},{48,16},{64,32},{80,48},{96,64},{112,80},{1... | collective-permute-start | bytes 393224 | tf_op jit(solution)/shard_map/ppermute | solution.py:376
  230.7 8.2 %collective-permute-start.1 = (bf16[16,32,128]{2,1,0:T(8,128)(2,1)S(1)}, bf16[16,32,128]{2,1,0:T(8,128)(2,1)S(1)}, u32[]{:S(2)}, u32[]{:S(2)}) collective-permute-start(bf16[16,32,128]{2,1,0:T(8,128)(2,1)S(1)} %strips.1.refs_0_), channel_id=1, source_target_pairs={{0,64},{16,80},{32,96},{48,112},{64,0},{80,16},{96,32},{112,48},{1... | collective-permute-start | bytes 393224 | tf_op jit(solution)/shard_map/ppermute | solution.py:376
  232.7 8.3 %collective-permute-start = (bf16[16,32,128]{2,1,0:T(8,128)(2,1)S(1)}, bf16[16,32,128]{2,1,0:T(8,128)(2,1)S(1)}, u32[]{:S(2)}, u32[]{:S(2)}) collective-permute-start(bf16[16,32,128]{2,1,0:T(8,128)(2,1)S(1)} %strips.1.refs_0_), channel_id=1, source_target_pairs={{0,32},{16,48},{32,64},{48,80},{64,96},{80,112},{96,0},{112,16},{1... | collective-permute-start | bytes 393224 | tf_op jit(solution)/shard_map/ppermute | solution.py:376
  233.1 9.8 %collective-permute-start.3 = (bf16[16,32,128]{2,1,0:T(8,128)(2,1)S(1)}, bf16[16,32,128]{2,1,0:T(8,128)(2,1)S(1)}, u32[]{:S(2)}, u32[]{:S(2)}) collective-permute-start(bf16[16,32,128]{2,1,0:T(8,128)(2,1)S(1)} %strips.1.refs_0_), channel_id=1, source_target_pairs={{0,16},{16,0},{32,48},{48,32},{64,80},{80,64},{96,112},{112,96},{1... | collective-permute-start | bytes 393224 | tf_op jit(solution)/shard_map/ppermute | solution.py:377
  237.1 5.7 %collective-permute-start.6 = (bf16[16,32,128]{2,1,0:T(8,128)(2,1)S(1)}, bf16[16,32,128]{2,1,0:T(8,128)(2,1)S(1)}, u32[]{:S(2)}, u32[]{:S(2)}) collective-permute-start(bf16[16,32,128]{2,1,0:T(8,128)(2,1)S(1)} %collective-permute-done.2.refs_3_), channel_id=1, source_target_pairs={{0,16},{16,0},{32,48},{48,32},{64,80},{80,64},{96,112},{112,96},{1... | collective-permute-start | bytes 393224 | tf_op jit(solution)/shard_map/ppermute | solution.py:377
  238.9 3.9 %collective-permute-start.5 = (bf16[16,32,128]{2,1,0:T(8,128)(2,1)S(1)}, bf16[16,32,128]{2,1,0:T(8,128)(2,1)S(1)}, u32[]{:S(2)}, u32[]{:S(2)}) collective-permute-start(bf16[16,32,128]{2,1,0:T(8,128)(2,1)S(1)} %collective-permute-done.1.refs_2_), channel_id=1, source_target_pairs={{0,16},{16,0},{32,48},{48,32},{64,80},{80,64},{96,112},{112,96},{1... | collective-permute-start | bytes 393224 | tf_op jit(solution)/shard_map/ppermute | solution.py:377
  241.0 2.7 %collective-permute-start.4 = (bf16[16,32,128]{2,1,0:T(8,128)(2,1)S(1)}, bf16[16,32,128]{2,1,0:T(8,128)(2,1)S(1)}, u32[]{:S(2)}, u32[]{:S(2)}) collective-permute-start(bf16[16,32,128]{2,1,0:T(8,128)(2,1)S(1)} %collective-permute-done.refs_1_), channel_id=1, source_target_pairs={{0,16},{16,0},{32,48},{48,32},{64,80},{80,64},{96,112},{112,96},{1... | collective-permute-start | bytes 393224 | tf_op jit(solution)/shard_map/ppermute | solution.py:377

commit v4 on v3

--- a/solution.py
+++ b/solution.py
@@ -48,18 +48,21 @@
     return pl.BlockSpec(memory_space=pltpu.VMEM)
 
 
-def send_kernel(vis_ref, out_ref, sem):
+def send_kernel(vis_ref, out_ref, held_ref, in_sem, out_sem):
     halves, dests = vis_ref.shape[:2]
-    n = sem.shape[1]
-    copies = []
-    for h in range(halves):
-        for i in range(n):
-            at = pl.ds(i * (dests // n), dests // n)
-            copies.append(pltpu.make_async_copy(vis_ref.at[h, at], out_ref.at[at, h], sem.at[h, i]))
-    for copy in copies:
-        copy.start()
-    for copy in copies:
-        copy.wait()
+    n = in_sem.shape[1]
+    loads, stores = [], []
+    for i in range(n):
+        at = pl.ds(i * (dests // n), dests // n)
+        for h in range(halves):
+            loads.append(pltpu.make_async_copy(vis_ref.at[h, at], held_ref.at[h, at], in_sem.at[h, i]))
+            stores.append(pltpu.make_async_copy(held_ref.at[h, at], out_ref.at[at, h], out_sem.at[h, i]))
+            loads[-1].start()
+    for load, store in zip(loads, stores):
+        load.wait()
+        store.start()
+    for store in stores:
+        store.wait()
 
 
 def send_order(vis):
@@ -69,8 +72,12 @@
         out_shape=pltpu.HBM((dests, halves, rows, bv), vis.dtype),
         in_specs=[pl.BlockSpec(memory_space=pltpu.HBM)],
         out_specs=pl.BlockSpec(memory_space=pltpu.HBM),
-        scratch_shapes=[pltpu.SemaphoreType.DMA((halves, 4))],
-        compiler_params=pltpu.CompilerParams(vmem_limit_bytes=1 * MIB),
+        scratch_shapes=[
+            pltpu.VMEM(vis.shape, vis.dtype),
+            pltpu.SemaphoreType.DMA((halves, 8)),
+            pltpu.SemaphoreType.DMA((halves, 8)),
+        ],
+        compiler_params=pltpu.CompilerParams(vmem_limit_bytes=8 * MIB),
         name="send_order",
     )(pltpu.with_memory_space_constraint(vis, pltpu.HBM))
 

time: 246 us -> 122 us (0.50)
  Pallas kernels: 144 us -> 20 us
    pallas_call x1, Pallas kernels: 128 us -> 3.96 us  [send_order(): pl.pallas_call(send_kernel, out_shape=pltpu.HBM((dests, halves, rows, bv)...]
where the time goes in v4:
time: 122 us
  waiting for transfers between devices  51.7 us (42%)
  blocking collectives  25.1 us (21%)
  starting transfers between devices  24.3 us (20%)
  Pallas kernels  20 us (16%)
    all_to_all x1, waiting for transfers between devices, exchange(): return lax.all_to_all(x, axis, split_axis=0, concat_axis=0, tiled=True)  50.8 us
    all_to_all x2, blocking collectives, exchange(): return lax.all_to_all(x, axis, split_axis=0, concat_axis=0, tiled=True)  25.1 us
    all_to_all x1, starting transfers between devices, exchange(): return lax.all_to_all(x, axis, split_axis=0, concat_axis=0, tiled=True)  12 us
    pallas_call x1, Pallas kernels, grid_rows(): pl.pallas_call(functools.partial(grid_kernel, n_rows // PIECE + n_planes)...  9.79 us
    ppermute x4, starting transfers between devices, local(): lax.ppermute(s, 'facet', [(f, f ^ 1) for f in range(n_facet)])  9.65 us
    pallas_call x1, Pallas kernels, send_order(): pl.pallas_call(send_kernel, out_shape=pltpu.HBM((dests, halves, rows, bv)...  3.96 us
    ppermute x3, starting transfers between devices, local(): lax.ppermute(own, 'facet', [(f, (f + 2 * dz) % n_facet) for f in range(n_...  2.68 us
    pallas_call x1, Pallas kernels, average(): pl.pallas_call(average_kernel, out_shape=jax.ShapeDtypeStruct((n_out, hal...  2.65 us
  transfers between devices with their start and end apart: 8, of which 2 were waited for; matrix products, arithmetic and copies ran while one was open for 0% of the time, Pallas kernels for 1%

profile of v4, /device:TPU:1, one launch (start us, length us, event | category | flops | bytes accessed | tf_op | source)
XLA Modules:
  0.0 121.6 jit_solution(13979348068703294050)
XLA Ops:
  0.0 0.0 copy-start
  0.0 4.0 %send_order.1 = bf16[128,2,64,128]{3,2,1,0:T(8,128)(2,1)} custom-call(bf16[2,128,64,128]{3,2,1,0:T(8,128)(2,1)} %bitcast.14), custom_call_target="tpu_custom_call" | custom-call | tf_op jit(solution)/shard_map/send_order/pallas_call | solution.py:70
  4.0 0.0 copy-start.1
  4.0 0.0 copy-start.2
  4.0 0.0 copy-start.4
  4.0 12.0 %all-to-all-start = ((bf16[128,2,64,128]{3,2,1,0:T(8,128)(2,1)}), bf16[128,2,64,128]{3,2,1,0:T(8,128)(2,1)}, u32[]{:S(2)}, u32[]{:S(2)}) async-start(bf16[128,2,64,128]{3,2,1,0:T(8,128)(2,1)} %send_order.1), calls=%async_computation | async-start | bytes 8388608 | tf_op jit(solution)/shard_map/all_to_all | solution.py:353
  16.0 0.0 copy-done.1
  16.0 0.0 copy-done.2
  16.0 0.0 copy-done.4
  16.0 0.1 fusion
  16.1 1.3 %tables.1 = (s32[1,1024]{1,0:T(1,128)S(1)}, s32[1,1536]{1,0:T(1,128)S(1)}, s32[8,128]{1,0:T(8,128)S(1)}) custom-call(s32[1,1024]{1,0:T(1,128)S(1)} %bitcast.13, s32[1,1024]{1,0:T(1,128)S(1)} %bitcast.12), custom_call_target="tpu_custom_call" | custom-call | tf_op jit(solution)/shard_map/tables/pallas_call | solution.py:221
  17.4 0.0 copy-done
  17.5 50.8 %all-to-all-done.vis_hbm = bf16[128,2,64,128]{3,2,1,0:T(8,128)(2,1)} async-done(((bf16[128,2,64,128]{3,2,1,0:T(8,128)(2,1)}), bf16[128,2,64,128]{3,2,1,0:T(8,128)(2,1)}, u32[]{:S(2)}, u32[]{:S(2)}) %all-to-all-start) | async-done | bytes 4194336 | tf_op jit(solution)/shard_map/all_to_all | solution.py:353
  68.3 2.7 %average.1 = bf16[16,2,64,128]{3,2,1,0:T(8,128)(2,1)S(1)} custom-call(s32[8,128]{1,0:T(8,128)S(1)} %get-tuple-element.8.piece_ref, f32[64,128]{1,0:T(8,128)S(1)} %dynamic-slice_bitcast_fusion.delay_ref, bf16[128,2,64,128]{3,2,1,0:T(8,128)(2,1)} %all-to-all-done.vis_hbm), custom_call_target="tpu_custom_call" | custom-call | tf_op jit(solution)/shard_map/average/pallas_call | solution.py:141
  71.0 11.9 %all_to_all.15.rows_ref = bf16[16,2,64,128]{3,2,1,0:T(8,128)(2,1)S(1)} all-to-all(bf16[16,2,64,128]{3,2,1,0:T(8,128)(2,1)S(1)} %average.1), channel_id=1, replica_groups=mesh['facet'=8,'chan'=16] {'chan'}, dimensions={0} | all-to-all | bytes 1048576 | tf_op jit(solution)/shard_map/all_to_all | solution.py:353
  82.9 0.0 copy-start.3
  82.9 9.8 %grid_rows.1 = bf16[16,32,512]{2,1,0:T(8,128)(2,1)S(1)} custom-call(s32[8,128]{1,0:T(8,128)S(1)} %get-tuple-element.8.piece_ref, s32[1,1024]{1,0:T(1,128)S(1)} %get-tuple-element.9.place_ref, s32[1,1536]{1,0:T(1,128)S(1)} %get-tuple-element.10.code_ref, bf16[16,2,64,128]{3,2,1,0:T(8,128)(2,1)S(1)} %all_to_all.15.rows_ref, bf16[32,256,512]{2,1,0:T(8,128)(2,1)} %k_hbm.1), custom_call_target="tpu_custom_call" | custom-call | tf_op jit(solution)/shard_map/grid_rows/pallas_call | solution.py:269
  92.7 13.2 %all_to_all.16.main_ref = bf16[16,32,512]{2,1,0:T(8,128)(2,1)S(1)} all-to-all(bf16[16,32,512]{2,1,0:T(8,128)(2,1)S(1)} %grid_rows.1), channel_id=1, replica_groups=mesh['facet'=8,'chan'=16] {'chan'}, dimensions={0} | all-to-all | bytes 1048576 | tf_op jit(solution)/shard_map/all_to_all | solution.py:353
  105.8 0.1 strips.1.refs_0_
  106.0 0.5 collective-permute-start.2
  106.4 2.1 %collective-permute-start.1 = (bf16[16,32,128]{2,1,0:T(8,128)(2,1)S(1)}, bf16[16,32,128]{2,1,0:T(8,128)(2,1)S(1)}, u32[]{:S(2)}, u32[]{:S(2)}) collective-permute-start(bf16[16,32,128]{2,1,0:T(8,128)(2,1)S(1)} %strips.1.refs_0_), channel_id=1, source_target_pairs={{0,64},{16,80},{32,96},{48,112},{64,0},{80,16},{96,32},{112,48},{1... | collective-permute-start | bytes 393224 | tf_op jit(solution)/shard_map/ppermute | solution.py:383
  108.5 0.2 collective-permute-start
  108.6 0.0 copy-done.3
  108.6 0.1 constant_dynamic-slice_fusion
  108.7 0.1 copy.9
  108.8 4.0 %collective-permute-start.3 = (bf16[16,32,128]{2,1,0:T(8,128)(2,1)S(1)}, bf16[16,32,128]{2,1,0:T(8,128)(2,1)S(1)}, u32[]{:S(2)}, u32[]{:S(2)}) collective-permute-start(bf16[16,32,128]{2,1,0:T(8,128)(2,1)S(1)} %strips.1.refs_0_), channel_id=1, source_target_pairs={{0,16},{16,0},{32,48},{48,32},{64,80},{80,64},{96,112},{112,96},{1... | collective-permute-start | bytes 393224 | tf_op jit(solution)/shard_map/ppermute | solution.py:384
  112.8 0.0 collective-permute-done.2.refs_3_
  112.8 1.8 %collective-permute-start.6 = (bf16[16,32,128]{2,1,0:T(8,128)(2,1)S(1)}, bf16[16,32,128]{2,1,0:T(8,128)(2,1)S(1)}, u32[]{:S(2)}, u32[]{:S(2)}) collective-permute-start(bf16[16,32,128]{2,1,0:T(8,128)(2,1)S(1)} %collective-permute-done.2.refs_3_), channel_id=1, source_target_pairs={{0,16},{16,0},{32,48},{48,32},{64,80},{80,64},{96,112},{112,96},{1... | collective-permute-start | bytes 393224 | tf_op jit(solution)/shard_map/ppermute | solution.py:384
  114.6 0.0 collective-permute-done.1.refs_2_
  114.6 2.1 %collective-permute-start.5 = (bf16[16,32,128]{2,1,0:T(8,128)(2,1)S(1)}, bf16[16,32,128]{2,1,0:T(8,128)(2,1)S(1)}, u32[]{:S(2)}, u32[]{:S(2)}) collective-permute-start(bf16[16,32,128]{2,1,0:T(8,128)(2,1)S(1)} %collective-permute-done.1.refs_2_), channel_id=1, source_target_pairs={{0,16},{16,0},{32,48},{48,32},{64,80},{80,64},{96,112},{112,96},{1... | collective-permute-start | bytes 393224 | tf_op jit(solution)/shard_map/ppermute | solution.py:384
  116.8 0.0 collective-permute-done.refs_1_
  116.8 1.7 %collective-permute-start.4 = (bf16[16,32,128]{2,1,0:T(8,128)(2,1)S(1)}, bf16[16,32,128]{2,1,0:T(8,128)(2,1)S(1)}, u32[]{:S(2)}, u32[]{:S(2)}) collective-permute-start(bf16[16,32,128]{2,1,0:T(8,128)(2,1)S(1)} %collective-permute-done.refs_1_), channel_id=1, source_target_pairs={{0,16},{16,0},{32,48},{48,32},{64,80},{80,64},{96,112},{112,96},{1... | collective-permute-start | bytes 393224 | tf_op jit(solution)/shard_map/ppermute | solution.py:384
  118.5 0.1 pad_add_fusion.nb_ref
  118.6 0.0 collective-permute-done.3.refs_4_
  118.6 0.0 collective-permute-done.6.refs_7_
  118.6 0.0 collective-permute-done.5.refs_6_
  118.6 0.9 collective-permute-done.4.refs_5_
  119.5 2.2 %join.1 = f32[16,2,16,512]{3,2,1,0:T(8,128)} custom-call(s32[2,8]{1,0:T(2,128)S(1)} %pad_add_fusion.nb_ref, bf16[16,32,512]{2,1,0:T(8,128)(2,1)S(1)} %all_to_all.16.main_ref, bf16[16,32,128]{2,1,0:T(8,128)(2,1)S(1)} %strips.1.refs_0_, bf16[16,32,128]{2,1,0:T(8,128)(2,1)S(1)} %collective-permute-done.refs_1_, ...), custom_call_target="tpu_custom_call" | custom-call | tf_op jit(solution)/shard_map/join/pallas_call | solution.py:341
  (4 shorter events, 0.1 us)
Async XLA Ops:
  0.0 17.4 %copy-start = (f32[2,512,128]{2,1,0:T(8,128)S(1)}, f32[2,512,128]{2,1,0:T(8,128)}, u32[]{:S(2)}) copy-start(f32[2,512,128]{2,1,0:T(8,128)} %param.9) | copy-start | bytes 1572868
  4.0 12.0 %copy-start.1 = (s32[2,512]{1,0:T(2,128)S(1)}, s32[2,512]{1,0:T(2,128)}, u32[]{:S(2)}) copy-start(s32[2,512]{1,0:T(2,128)} %param.10) | copy-start | bytes 12292
  4.0 12.0 %copy-start.2 = (s32[2,512]{1,0:T(2,128)S(1)}, s32[2,512]{1,0:T(2,128)}, u32[]{:S(2)}) copy-start(s32[2,512]{1,0:T(2,128)} %param.11) | copy-start | bytes 12292
  4.0 12.0 %copy-start.4 = (s32[2]{0:T(128)S(1)}, s32[2]{0:T(128)}, u32[]{:S(2)}) copy-start(s32[2]{0:T(128)} %param.12) | copy-start | bytes 28
  4.0 64.3 %all-to-all-start = ((bf16[128,2,64,128]{3,2,1,0:T(8,128)(2,1)}), bf16[128,2,64,128]{3,2,1,0:T(8,128)(2,1)}, u32[]{:S(2)}, u32[]{:S(2)}) async-start(bf16[128,2,64,128]{3,2,1,0:T(8,128)(2,1)} %send_order.1), calls=%async_computation | async-start | bytes 8388608 | tf_op jit(solution)/shard_map/all_to_all | solution.py:353
  82.9 25.8 %copy-start.3 = (s32[16,4]{0,1:T(4,128)S(1)}, s32[16,4]{0,1:T(4,128)}, u32[]{:S(2)}) copy-start(s32[16,4]{0,1:T(4,128)} %param.13) | copy-start | bytes 772
  106.0 6.9 %collective-permute-start.2 = (bf16[16,32,128]{2,1,0:T(8,128)(2,1)S(1)}, bf16[16,32,128]{2,1,0:T(8,128)(2,1)S(1)}, u32[]{:S(2)}, u32[]{:S(2)}) collective-permute-start(bf16[16,32,128]{2,1,0:T(8,128)(2,1)S(1)} %strips.1.refs_0_), channel_id=1, source_target_pairs={{0,96},{16,112},{32,0},{48,16},{64,32},{80,48},{96,64},{112,80},{1... | collective-permute-start | bytes 393224 | tf_op jit(solution)/shard_map/ppermute | solution.py:383
  106.4 8.2 %collective-permute-start.1 = (bf16[16,32,128]{2,1,0:T(8,128)(2,1)S(1)}, bf16[16,32,128]{2,1,0:T(8,128)(2,1)S(1)}, u32[]{:S(2)}, u32[]{:S(2)}) collective-permute-start(bf16[16,32,128]{2,1,0:T(8,128)(2,1)S(1)} %strips.1.refs_0_), channel_id=1, source_target_pairs={{0,64},{16,80},{32,96},{48,112},{64,0},{80,16},{96,32},{112,48},{1... | collective-permute-start | bytes 393224 | tf_op jit(solution)/shard_map/ppermute | solution.py:383
  108.5 8.3 %collective-permute-start = (bf16[16,32,128]{2,1,0:T(8,128)(2,1)S(1)}, bf16[16,32,128]{2,1,0:T(8,128)(2,1)S(1)}, u32[]{:S(2)}, u32[]{:S(2)}) collective-permute-start(bf16[16,32,128]{2,1,0:T(8,128)(2,1)S(1)} %strips.1.refs_0_), channel_id=1, source_target_pairs={{0,32},{16,48},{32,64},{48,80},{64,96},{80,112},{96,0},{112,16},{1... | collective-permute-start | bytes 393224 | tf_op jit(solution)/shard_map/ppermute | solution.py:383
  108.8 9.8 %collective-permute-start.3 = (bf16[16,32,128]{2,1,0:T(8,128)(2,1)S(1)}, bf16[16,32,128]{2,1,0:T(8,128)(2,1)S(1)}, u32[]{:S(2)}, u32[]{:S(2)}) collective-permute-start(bf16[16,32,128]{2,1,0:T(8,128)(2,1)S(1)} %strips.1.refs_0_), channel_id=1, source_target_pairs={{0,16},{16,0},{32,48},{48,32},{64,80},{80,64},{96,112},{112,96},{1... | collective-permute-start | bytes 393224 | tf_op jit(solution)/shard_map/ppermute | solution.py:384
  112.8 5.7 %collective-permute-start.6 = (bf16[16,32,128]{2,1,0:T(8,128)(2,1)S(1)}, bf16[16,32,128]{2,1,0:T(8,128)(2,1)S(1)}, u32[]{:S(2)}, u32[]{:S(2)}) collective-permute-start(bf16[16,32,128]{2,1,0:T(8,128)(2,1)S(1)} %collective-permute-done.2.refs_3_), channel_id=1, source_target_pairs={{0,16},{16,0},{32,48},{48,32},{64,80},{80,64},{96,112},{112,96},{1... | collective-permute-start | bytes 393224 | tf_op jit(solution)/shard_map/ppermute | solution.py:384
  114.6 3.9 %collective-permute-start.5 = (bf16[16,32,128]{2,1,0:T(8,128)(2,1)S(1)}, bf16[16,32,128]{2,1,0:T(8,128)(2,1)S(1)}, u32[]{:S(2)}, u32[]{:S(2)}) collective-permute-start(bf16[16,32,128]{2,1,0:T(8,128)(2,1)S(1)} %collective-permute-done.1.refs_2_), channel_id=1, source_target_pairs={{0,16},{16,0},{32,48},{48,32},{64,80},{80,64},{96,112},{112,96},{1... | collective-permute-start | bytes 393224 | tf_op jit(solution)/shard_map/ppermute | solution.py:384
  116.8 2.7 %collective-permute-start.4 = (bf16[16,32,128]{2,1,0:T(8,128)(2,1)S(1)}, bf16[16,32,128]{2,1,0:T(8,128)(2,1)S(1)}, u32[]{:S(2)}, u32[]{:S(2)}) collective-permute-start(bf16[16,32,128]{2,1,0:T(8,128)(2,1)S(1)} %collective-permute-done.refs_1_), channel_id=1, source_target_pairs={{0,16},{16,0},{32,48},{48,32},{64,80},{80,64},{96,112},{112,96},{1... | collective-permute-start | bytes 393224 | tf_op jit(solution)/shard_map/ppermute | solution.py:384

commit v5 on v3

--- a/solution.py
+++ b/solution.py
@@ -14,6 +14,7 @@
 STRIP = EDGE * TS
 GROUP = 16
 PIECE = 64
+STRETCH = 12
 MIB = 1024 * 1024
 
 SIN = (-1.0 / 6, 1.0 / 120, -1.0 / 5040, 1.0 / 362880, -1.0 / 39916800)
@@ -48,105 +49,6 @@
     return pl.BlockSpec(memory_space=pltpu.VMEM)
 
 
-def send_kernel(vis_ref, out_ref, sem):
-    halves, dests = vis_ref.shape[:2]
-    n = sem.shape[1]
-    copies = []
-    for h in range(halves):
-        for i in range(n):
-            at = pl.ds(i * (dests // n), dests // n)
-            copies.append(pltpu.make_async_copy(vis_ref.at[h, at], out_ref.at[at, h], sem.at[h, i]))
-    for copy in copies:
-        copy.start()
-    for copy in copies:
-        copy.wait()
-
-
-def send_order(vis):
-    halves, dests, rows, bv = vis.shape
-    return pl.pallas_call(
-        send_kernel,
-        out_shape=pltpu.HBM((dests, halves, rows, bv), vis.dtype),
-        in_specs=[pl.BlockSpec(memory_space=pltpu.HBM)],
-        out_specs=pl.BlockSpec(memory_space=pltpu.HBM),
-        scratch_shapes=[pltpu.SemaphoreType.DMA((halves, 4))],
-        compiler_params=pltpu.CompilerParams(vmem_limit_bytes=1 * MIB),
-        name="send_order",
-    )(pltpu.with_memory_space_constraint(vis, pltpu.HBM))
-
-
-def fill_turns(d, inner_ref, outer_ref):
-    small = series(d * (1.0 / 256.0))
-    table = [None, small]
-    for j in range(2, AVG):
-        table.append(times(table[j // 2], table[j - j // 2]))
-    for j in range(1, AVG):
-        inner_ref[j - 1, 0] = table[j][0]
-        inner_ref[j - 1, 1] = table[j][1]
-    c, s = turn_by(d)
-    turn = (c * (1.0 / AVG), s * (1.0 / AVG))
-    step = series(d * (1.0 / 32.0))
-    for o in range(outer_ref.shape[0]):
-        outer_ref[o, 0] = turn[0]
-        outer_ref[o, 1] = turn[1]
-        turn = times(turn, step)
-
-
-def average_kernel(piece_ref, delay_ref, vis_hbm, out_ref, vis_ref, inner_ref, outer_ref, sem):
-    n_out, _, rows, _ = out_ref.shape
-    steps = sem.shape[0]
-    size = vis_ref.shape[0] // steps
-    copies = []
-    for i in range(steps):
-        at = pl.ds(i * size, size)
-        copies.append(pltpu.make_async_copy(vis_hbm.at[at], vis_ref.at[at], sem.at[i]))
-        copies[-1].start()
-    fill_turns(delay_ref[...], inner_ref, outer_ref)
-    for i in range(steps):
-        copies[i].wait()
-        for r in range(0, rows, 16):
-            at = slice(r, r + 16)
-            table = [(inner_ref[j, 0, at], inner_ref[j, 1, at]) for j in range(AVG - 1)]
-
-            def one(o, carry, at=at, table=table):
-                c = o * AVG
-                re = vis_ref[c, 0, at].astype(jnp.float32)
-                im = vis_ref[c, 1, at].astype(jnp.float32)
-                for j in range(1, AVG):
-                    a = vis_ref[c + j, 0, at].astype(jnp.float32)
-                    b = vis_ref[c + j, 1, at].astype(jnp.float32)
-                    tc, ts = table[j - 1]
-                    re += a * tc - b * ts
-                    im += a * ts + b * tc
-                tc = outer_ref[o, 0, at]
-                ts = outer_ref[o, 1, at]
-                out_ref[o, 0, at] = (re * tc - im * ts).astype(jnp.bfloat16)
-                out_ref[o, 1, at] = (re * ts + im * tc).astype(jnp.bfloat16)
-                return carry
-
-            n = n_out // steps
-            lax.fori_loop(i * n, (i + 1) * n, one, 0, unroll=n)
-
-
-def average(piece, vis, delay):
-    n_ch, halves, rows, bv = vis.shape
-    n_out = n_ch // AVG
-    return pl.pallas_call(
-        average_kernel,
-        out_shape=jax.ShapeDtypeStruct((n_out, halves, rows, bv), jnp.bfloat16),
-        in_specs=[vmem(), vmem(), pl.BlockSpec(memory_space=pltpu.HBM)],
-        out_specs=vmem(),
-        scratch_shapes=[
-            pltpu.VMEM(vis.shape, vis.dtype),
-            pltpu.VMEM((AVG - 1, 2, rows, bv), jnp.float32),
-            pltpu.VMEM((n_out, 2, rows, bv), jnp.float32),
-            pltpu.SemaphoreType.DMA((4,)),
-        ],
-        compiler_params=pltpu.CompilerParams(vmem_limit_bytes=12 * MIB),
-        name="average",
-    )(piece, delay, pltpu.with_memory_space_constraint(vis, pltpu.HBM))
-
-
 def to_bf16(mask):
     return mask.astype(jnp.float32).astype(jnp.bfloat16)
 
@@ -155,10 +57,17 @@
     return lax.broadcasted_iota(jnp.int32, shape, dim)
 
 
-def tables_kernel(n_planes, n_order, t_dev, plane_ref, tile_ref, place_ref, code_ref, piece_ref):
-    n_rows = plane_ref.shape[1]
+def fill_tables(n_planes, n_order, t_dev, count_ref, plane_ref, tile_ref, place_ref, code_ref, piece_ref):
     f32 = jnp.float32
-    plane = plane_ref[...]
+    slots, blocks = plane_ref.shape
+    n_rows = slots * blocks
+    planes, tiles = [], []
+    for slot in range(slots):
+        alive = iota((1, blocks), 1) < count_ref[slot]
+        planes.append(jnp.where(alive, plane_ref[slot : slot + 1, :], -1))
+        tiles.append(tile_ref[slot : slot + 1, :])
+    plane = jnp.concatenate(planes, axis=1)
+    tile = jnp.concatenate(tiles, axis=1)
     mine = plane == iota((n_planes, n_rows), 0)
     before = to_bf16(iota((n_rows, n_rows), 0) < iota((n_rows, n_rows), 1))
     rank = jnp.dot(to_bf16(mine), before, preferred_element_type=f32)
@@ -180,7 +89,7 @@
 
     row = iota((8, n_rows), 0)
     slot = (iota((8, n_rows), 1) >= n_rows // 2).astype(f32)
-    values = jnp.where(row == 0, tile_ref[...].astype(f32) + 1.0, jnp.where(row == 1, slot, 0.0))
+    values = jnp.where(row == 0, tile.astype(f32) + 1.0, jnp.where(row == 1, slot, 0.0))
     n_used = code_ref.shape[1]
     ordered = lax.dot_general(
         values.astype(jnp.bfloat16), order[:n_used], (((1,), (1,)), ((), ())), preferred_element_type=f32
@@ -208,21 +117,109 @@
     return n_order, n_used
 
 
-def tables(planes, tiles, n_planes, t_dev):
-    n_rows = planes.shape[1]
+def send_kernel(n_planes, n_order, t_dev, count_ref, plane_ref, tile_ref, vis_ref, out_ref, *rest):
+    tables, sem = rest[:-1], rest[-1]
+    halves, dests = vis_ref.shape[:2]
+    n = sem.shape[1]
+    copies = []
+    for i in range(n):
+        at = pl.ds(i * (dests // n), dests // n)
+        for h in range(halves):
+            copies.append(pltpu.make_async_copy(vis_ref.at[h, at], out_ref.at[at, h], sem.at[h, i]))
+            copies[-1].start()
+    fill_tables(n_planes, n_order, t_dev, count_ref, plane_ref, tile_ref, *tables)
+    for copy in copies:
+        copy.wait()
+
+
+def send_order(counts, planes, tiles, vis, n_planes, t_dev):
+    halves, dests, rows, bv = vis.shape
+    n_rows = planes.shape[0] * planes.shape[1]
     n_order, n_used = sizes(n_rows, n_planes)
     return pl.pallas_call(
-        functools.partial(tables_kernel, n_planes, n_order, t_dev),
+        functools.partial(send_kernel, n_planes, n_order, t_dev),
         out_shape=[
+            jax.ShapeDtypeStruct((dests, halves, rows, bv), vis.dtype),
             jax.ShapeDtypeStruct((1, n_rows), jnp.int32),
             jax.ShapeDtypeStruct((1, n_used), jnp.int32),
             jax.ShapeDtypeStruct((8, 128), jnp.int32),
         ],
-        in_specs=[vmem()] * 2,
-        out_specs=[vmem()] * 3,
-        compiler_params=pltpu.CompilerParams(vmem_limit_bytes=40 * MIB),
-        name="tables",
-    )(planes, tiles)
+        in_specs=[
+            pl.BlockSpec(memory_space=pltpu.SMEM),
+            vmem(),
+            vmem(),
+            pl.BlockSpec(memory_space=pltpu.HBM),
+        ],
+        out_specs=[vmem()] * 4,
+        scratch_shapes=[pltpu.SemaphoreType.DMA((halves, 4))],
+        compiler_params=pltpu.CompilerParams(vmem_limit_bytes=32 * MIB),
+        name="send_order",
+    )(counts, planes, tiles, pltpu.with_memory_space_constraint(vis, pltpu.HBM))
+
+
+def fill_turns(d, inner_ref, outer_ref):
+    small = series(d * (1.0 / 256.0))
+    table = [None, small]
+    for j in range(2, AVG):
+        table.append(times(table[j // 2], table[j - j // 2]))
+    for j in range(1, AVG):
+        inner_ref[j - 1, 0] = table[j][0]
+        inner_ref[j - 1, 1] = table[j][1]
+    c, s = turn_by(d)
+    turn = (c * (1.0 / AVG), s * (1.0 / AVG))
+    step = series(d * (1.0 / 32.0))
+    for o in range(outer_ref.shape[0]):
+        outer_ref[o, 0] = turn[0]
+        outer_ref[o, 1] = turn[1]
+        turn = times(turn, step)
+
+
+def average_kernel(delay_hbm, vis_ref, out_ref, delay_ref, inner_ref, outer_ref, sem):
+    fetch = pltpu.make_async_copy(delay_hbm.at[lax.axis_index("chan")], delay_ref, sem.at[0])
+    fetch.start()
+    fetch.wait()
+    fill_turns(delay_ref[...], inner_ref, outer_ref)
+    n_out, _, rows, _ = out_ref.shape
+    for r in range(0, rows, 16):
+        at = slice(r, r + 16)
+        table = [(inner_ref[j, 0, at], inner_ref[j, 1, at]) for j in range(AVG - 1)]
+
+        def one(o, carry, at=at, table=table):
+            c = o * AVG
+            re = vis_ref[c, 0, at].astype(jnp.float32)
+            im = vis_ref[c, 1, at].astype(jnp.float32)
+            for j in range(1, AVG):
+                a = vis_ref[c + j, 0, at].astype(jnp.float32)
+                b = vis_ref[c + j, 1, at].astype(jnp.float32)
+                tc, ts = table[j - 1]
+                re += a * tc - b * ts
+                im += a * ts + b * tc
+            tc = outer_ref[o, 0, at]
+            ts = outer_ref[o, 1, at]
+            out_ref[o, 0, at] = (re * tc - im * ts).astype(jnp.bfloat16)
+            out_ref[o, 1, at] = (re * ts + im * tc).astype(jnp.bfloat16)
+            return carry
+
+        lax.fori_loop(0, n_out, one, 0, unroll=4)
+
+
+def average(delays, vis):
+    n_ch, halves, rows, bv = vis.shape
+    n_out = n_ch // AVG
+    return pl.pallas_call(
+        average_kernel,
+        out_shape=jax.ShapeDtypeStruct((n_out, halves, rows, bv), jnp.bfloat16),
+        in_specs=[pl.BlockSpec(memory_space=pltpu.HBM), vmem()],
+        out_specs=vmem(),
+        scratch_shapes=[
+            pltpu.VMEM((rows, bv), jnp.float32),
+            pltpu.VMEM((AVG - 1, 2, rows, bv), jnp.float32),
+            pltpu.VMEM((n_out, 2, rows, bv), jnp.float32),
+            pltpu.SemaphoreType.DMA((1,)),
+        ],
+        compiler_params=pltpu.CompilerParams(vmem_limit_bytes=12 * MIB),
+        name="average",
+    )(pltpu.with_memory_space_constraint(delays, pltpu.HBM), vis)
 
 
 def grid_kernel(n_pieces, piece_ref, place_ref, code_ref, rows_ref, k_hbm, out_ref, k_ref, x_ref, c_ref, sem):
@@ -244,9 +241,17 @@
     n_codes = out_ref.shape[0] * out_ref.shape[1]
     tiles = to_bf16(iota((n_codes, n_used), 0) == code_ref[...])
     c_ref[...] = jnp.zeros_like(c_ref)
-    for fetch in fetches:
-        fetch.wait()
+    had = jnp.int32(0)
     for i in range(n_pieces):
+        if i % STRETCH == 0:
+            need = n_fetch if i + STRETCH >= n_pieces else piece_ref[1, i + STRETCH - 1] // part + 1
+            for k, fetch in enumerate(fetches):
+
+                @pl.when((k >= had) & (k < need))
+                def _(fetch=fetch):
+                    fetch.wait()
+
+            had = jnp.maximum(had, need)
         at = pl.ds(pl.multiple_of(piece_ref[0, i] * GROUP, GROUP), PIECE)
         product = jnp.dot(x_ref[at, :], k_ref[piece_ref[1, i]], preferred_element_type=jnp.float32)
         c_ref[at, :] = product.astype(jnp.bfloat16)
@@ -350,7 +355,6 @@
     n_facet = lax.axis_size("facet")
     n_chan = lax.axis_size("chan")
     facet_index = lax.axis_index("facet")
-    chan_index = lax.axis_index("chan")
     halves, facets, blocks, _, bv = visibilities.shape
     fac_dev = facets // n_facet
     n_tiles = 16 * n_chan
@@ -358,14 +362,11 @@
     n_rows = fac_dev * blocks
     per = n_rows // n_chan
 
-    vis = send_order(visibilities.reshape(halves, n_facet * n_chan, per, bv))
+    vis = visibilities.reshape(halves, n_facet * n_chan, per, bv)
+    vis, place, code, piece = send_order(counts, plane_of, tile_of, vis, kernels.shape[0], t_dev)
     vis = exchange(vis, ("facet", "chan"))
-    delay = lax.dynamic_index_in_dim(delays.reshape(n_chan, per, bv), chan_index, 0, keepdims=False)
-    live = jnp.arange(blocks, dtype=jnp.int32)[None, :] < counts[:, None]
-    planes = jnp.where(live, plane_of, -1).reshape(1, n_rows)
-    place, code, piece = tables(planes, tile_of.reshape(1, n_rows), kernels.shape[0], t_dev)
-
-    rows = exchange(average(piece, vis, delay), "chan")
+
+    rows = exchange(average(delays.reshape(n_chan, per, bv), vis), "chan")
     grids = grid_rows(piece, place, code, rows, kernels, fac_dev * n_tiles)
     main = exchange(grids, "chan")
 

time: 246 us -> 121 us (0.49)
  Pallas kernels: 144 us -> 15.9 us
  blocking collectives: 25.1 us -> 89.1 us
  waiting for transfers between devices: 51.7 us -> 0.89 us
  starting transfers between devices: 24.3 us -> 12.3 us
    pallas_call x2 -> x1, Pallas kernels: 130 us -> 3.13 us  [send_order(): pl.pallas_call(functools.partial(send_kernel, n_planes, n_order, t_dev),...]
    all_to_all x2 -> x3, blocking collectives: 25.1 us -> 89.1 us  [exchange(): return lax.all_to_all(x, axis, split_axis=0, concat_axis=0, tiled=True)]
    all_to_all x1 -> x0, waiting for transfers between devices: 50.8 us -> none  [exchange(): return lax.all_to_all(x, axis, split_axis=0, concat_axis=0, tiled=True)]
    all_to_all x1 -> x0, starting transfers between devices: 12 us -> none  [exchange(): return lax.all_to_all(x, axis, split_axis=0, concat_axis=0, tiled=True)]
  transfers between devices with their start and end apart: 8 -> 7, of which waited for: 2 -> 1; matrix products, arithmetic and copies ran while one was open for 0% -> 0% of each run, Pallas kernels for 1% -> 0%
where the time goes in v5:
time: 121 us
  blocking collectives  89.1 us (74%)
  Pallas kernels  15.9 us (13%)
  starting transfers between devices  12.3 us (10%)
  local copies, waits for them, and re-layouts  2.21 us (2%)
    all_to_all x3, blocking collectives, exchange(): return lax.all_to_all(x, axis, split_axis=0, concat_axis=0, tiled=True)  89.1 us
    ppermute x4, starting transfers between devices, local(): lax.ppermute(s, 'facet', [(f, f ^ 1) for f in range(n_facet)])  9.64 us
    pallas_call x1, Pallas kernels, grid_rows(): pl.pallas_call(functools.partial(grid_kernel, n_rows // PIECE + n_planes)...  8.05 us
    pallas_call x1, Pallas kernels, send_order(): pl.pallas_call(functools.partial(send_kernel, n_planes, n_order, t_dev),...  3.13 us
    ppermute x3, starting transfers between devices, local(): lax.ppermute(own, 'facet', [(f, (f + 2 * dz) % n_facet) for f in range(n_...  2.68 us
    pallas_call x1, Pallas kernels, average(): pl.pallas_call(average_kernel, out_shape=jax.ShapeDtypeStruct((n_out, hal...  2.46 us
  transfers between devices with their start and end apart: 7, of which 1 were waited for; matrix products, arithmetic and copies ran while one was open for 0% of the time, Pallas kernels for 0%

profile of v5, /device:TPU:1, one launch (start us, length us, event | category | flops | bytes accessed | tf_op | source)
XLA Modules:
  0.0 120.5 jit_solution(16058242211605293167)
XLA Ops:
  0.0 0.0 copy-start
  0.0 0.0 copy-start.1
  0.0 0.7 copy-done.1
  0.7 0.0 copy-start.2
  0.7 0.7 copy-done.2
  1.4 0.0 copy-start.3
  1.4 0.7 copy-done.3
  2.0 3.1 %send_order.1 = (bf16[128,2,64,128]{3,2,1,0:T(8,128)(2,1)S(1)}, s32[1,1024]{1,0:T(1,128)S(1)}, s32[1,1536]{1,0:T(1,128)S(1)}, s32[8,128]{1,0:T(8,128)S(1)}) custom-call(s32[2]{0:T(128)S(1)} %copy-done.3, s32[2,512]{1,0:T(2,128)S(1)} %copy-done.1, s32[2,512]{1,0:T(2,128)S(1)} %copy-done.2, bf16[2,128,64,128]{3,2,1,0:T(8,128)(2,1)} %bitcast.2), custom_call_target="tpu_custom_call" | custom-call | tf_op jit(solution)/shard_map/send_order/pallas_call | solution.py:139
  5.2 64.0 %all_to_all.15.vis_ref = bf16[128,2,64,128]{3,2,1,0:T(8,128)(2,1)S(1)} all-to-all(bf16[128,2,64,128]{3,2,1,0:T(8,128)(2,1)S(1)} %get-tuple-element.12), channel_id=1, replica_groups=mesh['facet'=8,'chan'=16] {'facet','chan'}, dimensions={0} | all-to-all | bytes 8388608 | tf_op jit(solution)/shard_map/all_to_all | solution.py:351
  69.2 2.5 %average.1 = bf16[16,2,64,128]{3,2,1,0:T(8,128)(2,1)S(1)} custom-call(f32[16,64,128]{2,1,0:T(8,128)} %bitcast.3, bf16[128,2,64,128]{3,2,1,0:T(8,128)(2,1)S(1)} %all_to_all.15.vis_ref), custom_call_target="tpu_custom_call" | custom-call | tf_op jit(solution)/shard_map/average/pallas_call | solution.py:209
  71.6 11.9 %all_to_all.16.rows_ref = bf16[16,2,64,128]{3,2,1,0:T(8,128)(2,1)S(1)} all-to-all(bf16[16,2,64,128]{3,2,1,0:T(8,128)(2,1)S(1)} %average.1), channel_id=1, replica_groups=mesh['facet'=8,'chan'=16] {'chan'}, dimensions={0} | all-to-all | bytes 1048576 | tf_op jit(solution)/shard_map/all_to_all | solution.py:351
  83.5 8.0 %grid_rows.1 = bf16[16,32,512]{2,1,0:T(8,128)(2,1)S(1)} custom-call(s32[8,128]{1,0:T(8,128)S(1)} %get-tuple-element.9.piece_ref, s32[1,1024]{1,0:T(1,128)S(1)} %get-tuple-element.10.place_ref, s32[1,1536]{1,0:T(1,128)S(1)} %get-tuple-element.11.code_ref, bf16[16,2,64,128]{3,2,1,0:T(8,128)(2,1)S(1)} %all_to_all.16.rows_ref, bf16[32,256,512]{2,1,0:T(8,128)(2,1)} %k_hbm.1), custom_call_target="tpu_custom_call" | custom-call | tf_op jit(solution)/shard_map/grid_rows/pallas_call | solution.py:267
  91.6 13.2 %all_to_all.17.main_ref = bf16[16,32,512]{2,1,0:T(8,128)(2,1)S(1)} all-to-all(bf16[16,32,512]{2,1,0:T(8,128)(2,1)S(1)} %grid_rows.1), channel_id=1, replica_groups=mesh['facet'=8,'chan'=16] {'chan'}, dimensions={0} | all-to-all | bytes 1048576 | tf_op jit(solution)/shard_map/all_to_all | solution.py:351
  104.8 0.1 strips.1.refs_0_
  104.9 0.5 collective-permute-start.2
  105.4 2.0 %collective-permute-start.1 = (bf16[16,32,128]{2,1,0:T(8,128)(2,1)S(1)}, bf16[16,32,128]{2,1,0:T(8,128)(2,1)S(1)}, u32[]{:S(2)}, u32[]{:S(2)}) collective-permute-start(bf16[16,32,128]{2,1,0:T(8,128)(2,1)S(1)} %strips.1.refs_0_), channel_id=1, source_target_pairs={{0,64},{16,80},{32,96},{48,112},{64,0},{80,16},{96,32},{112,48},{1... | collective-permute-start | bytes 393224 | tf_op jit(solution)/shard_map/ppermute | solution.py:377
  107.4 0.2 collective-permute-start
  107.6 0.0 copy-done
  107.6 0.1 constant_dynamic-slice_fusion
  107.6 0.1 copy.9
  107.7 4.0 %collective-permute-start.3 = (bf16[16,32,128]{2,1,0:T(8,128)(2,1)S(1)}, bf16[16,32,128]{2,1,0:T(8,128)(2,1)S(1)}, u32[]{:S(2)}, u32[]{:S(2)}) collective-permute-start(bf16[16,32,128]{2,1,0:T(8,128)(2,1)S(1)} %strips.1.refs_0_), channel_id=1, source_target_pairs={{0,16},{16,0},{32,48},{48,32},{64,80},{80,64},{96,112},{112,96},{1... | collective-permute-start | bytes 393224 | tf_op jit(solution)/shard_map/ppermute | solution.py:378
  111.8 0.0 collective-permute-done.2.refs_3_
  111.8 1.8 %collective-permute-start.6 = (bf16[16,32,128]{2,1,0:T(8,128)(2,1)S(1)}, bf16[16,32,128]{2,1,0:T(8,128)(2,1)S(1)}, u32[]{:S(2)}, u32[]{:S(2)}) collective-permute-start(bf16[16,32,128]{2,1,0:T(8,128)(2,1)S(1)} %collective-permute-done.2.refs_3_), channel_id=1, source_target_pairs={{0,16},{16,0},{32,48},{48,32},{64,80},{80,64},{96,112},{112,96},{1... | collective-permute-start | bytes 393224 | tf_op jit(solution)/shard_map/ppermute | solution.py:378
  113.6 0.0 collective-permute-done.1.refs_2_
  113.6 2.1 %collective-permute-start.5 = (bf16[16,32,128]{2,1,0:T(8,128)(2,1)S(1)}, bf16[16,32,128]{2,1,0:T(8,128)(2,1)S(1)}, u32[]{:S(2)}, u32[]{:S(2)}) collective-permute-start(bf16[16,32,128]{2,1,0:T(8,128)(2,1)S(1)} %collective-permute-done.1.refs_2_), channel_id=1, source_target_pairs={{0,16},{16,0},{32,48},{48,32},{64,80},{80,64},{96,112},{112,96},{1... | collective-permute-start | bytes 393224 | tf_op jit(solution)/shard_map/ppermute | solution.py:378
  115.7 0.0 collective-permute-done.refs_1_
  115.7 1.7 %collective-permute-start.4 = (bf16[16,32,128]{2,1,0:T(8,128)(2,1)S(1)}, bf16[16,32,128]{2,1,0:T(8,128)(2,1)S(1)}, u32[]{:S(2)}, u32[]{:S(2)}) collective-permute-start(bf16[16,32,128]{2,1,0:T(8,128)(2,1)S(1)} %collective-permute-done.refs_1_), channel_id=1, source_target_pairs={{0,16},{16,0},{32,48},{48,32},{64,80},{80,64},{96,112},{112,96},{1... | collective-permute-start | bytes 393224 | tf_op jit(solution)/shard_map/ppermute | solution.py:378
  117.4 0.1 pad_add_fusion.nb_ref
  117.5 0.0 collective-permute-done.3.refs_4_
  117.5 0.0 collective-permute-done.6.refs_7_
  117.5 0.0 collective-permute-done.5.refs_6_
  117.5 0.9 collective-permute-done.4.refs_5_
  118.4 2.2 %join.1 = f32[16,2,16,512]{3,2,1,0:T(8,128)} custom-call(s32[2,8]{1,0:T(2,128)S(1)} %pad_add_fusion.nb_ref, bf16[16,32,512]{2,1,0:T(8,128)(2,1)S(1)} %all_to_all.17.main_ref, bf16[16,32,128]{2,1,0:T(8,128)(2,1)S(1)} %strips.1.refs_0_, bf16[16,32,128]{2,1,0:T(8,128)(2,1)S(1)} %collective-permute-done.refs_1_, ...), custom_call_target="tpu_custom_call" | custom-call | tf_op jit(solution)/shard_map/join/pallas_call | solution.py:339
  (1 shorter events, 0.0 us)
Async XLA Ops:
  0.0 107.6 %copy-start = (s32[16,4]{0,1:T(4,128)S(1)}, s32[16,4]{0,1:T(4,128)}, u32[]{:S(2)}) copy-start(s32[16,4]{0,1:T(4,128)} %param.13) | copy-start | bytes 772
  0.0 0.7 copy-start.1
  0.7 0.7 copy-start.2
  1.4 0.7 copy-start.3
  104.9 6.9 %collective-permute-start.2 = (bf16[16,32,128]{2,1,0:T(8,128)(2,1)S(1)}, bf16[16,32,128]{2,1,0:T(8,128)(2,1)S(1)}, u32[]{:S(2)}, u32[]{:S(2)}) collective-permute-start(bf16[16,32,128]{2,1,0:T(8,128)(2,1)S(1)} %strips.1.refs_0_), channel_id=1, source_target_pairs={{0,96},{16,112},{32,0},{48,16},{64,32},{80,48},{96,64},{112,80},{1... | collective-permute-start | bytes 393224 | tf_op jit(solution)/shard_map/ppermute | solution.py:377
  105.4 8.2 %collective-permute-start.1 = (bf16[16,32,128]{2,1,0:T(8,128)(2,1)S(1)}, bf16[16,32,128]{2,1,0:T(8,128)(2,1)S(1)}, u32[]{:S(2)}, u32[]{:S(2)}) collective-permute-start(bf16[16,32,128]{2,1,0:T(8,128)(2,1)S(1)} %strips.1.refs_0_), channel_id=1, source_target_pairs={{0,64},{16,80},{32,96},{48,112},{64,0},{80,16},{96,32},{112,48},{1... | collective-permute-start | bytes 393224 | tf_op jit(solution)/shard_map/ppermute | solution.py:377
  107.4 8.3 %collective-permute-start = (bf16[16,32,128]{2,1,0:T(8,128)(2,1)S(1)}, bf16[16,32,128]{2,1,0:T(8,128)(2,1)S(1)}, u32[]{:S(2)}, u32[]{:S(2)}) collective-permute-start(bf16[16,32,128]{2,1,0:T(8,128)(2,1)S(1)} %strips.1.refs_0_), channel_id=1, source_target_pairs={{0,32},{16,48},{32,64},{48,80},{64,96},{80,112},{96,0},{112,16},{1... | collective-permute-start | bytes 393224 | tf_op jit(solution)/shard_map/ppermute | solution.py:377
  107.7 9.8 %collective-permute-start.3 = (bf16[16,32,128]{2,1,0:T(8,128)(2,1)S(1)}, bf16[16,32,128]{2,1,0:T(8,128)(2,1)S(1)}, u32[]{:S(2)}, u32[]{:S(2)}) collective-permute-start(bf16[16,32,128]{2,1,0:T(8,128)(2,1)S(1)} %strips.1.refs_0_), channel_id=1, source_target_pairs={{0,16},{16,0},{32,48},{48,32},{64,80},{80,64},{96,112},{112,96},{1... | collective-permute-start | bytes 393224 | tf_op jit(solution)/shard_map/ppermute | solution.py:378
  111.8 5.7 %collective-permute-start.6 = (bf16[16,32,128]{2,1,0:T(8,128)(2,1)S(1)}, bf16[16,32,128]{2,1,0:T(8,128)(2,1)S(1)}, u32[]{:S(2)}, u32[]{:S(2)}) collective-permute-start(bf16[16,32,128]{2,1,0:T(8,128)(2,1)S(1)} %collective-permute-done.2.refs_3_), channel_id=1, source_target_pairs={{0,16},{16,0},{32,48},{48,32},{64,80},{80,64},{96,112},{112,96},{1... | collective-permute-start | bytes 393224 | tf_op jit(solution)/shard_map/ppermute | solution.py:378
  113.6 3.9 %collective-permute-start.5 = (bf16[16,32,128]{2,1,0:T(8,128)(2,1)S(1)}, bf16[16,32,128]{2,1,0:T(8,128)(2,1)S(1)}, u32[]{:S(2)}, u32[]{:S(2)}) collective-permute-start(bf16[16,32,128]{2,1,0:T(8,128)(2,1)S(1)} %collective-permute-done.1.refs_2_), channel_id=1, source_target_pairs={{0,16},{16,0},{32,48},{48,32},{64,80},{80,64},{96,112},{112,96},{1... | collective-permute-start | bytes 393224 | tf_op jit(solution)/shard_map/ppermute | solution.py:378
  115.7 2.7 %collective-permute-start.4 = (bf16[16,32,128]{2,1,0:T(8,128)(2,1)S(1)}, bf16[16,32,128]{2,1,0:T(8,128)(2,1)S(1)}, u32[]{:S(2)}, u32[]{:S(2)}) collective-permute-start(bf16[16,32,128]{2,1,0:T(8,128)(2,1)S(1)} %collective-permute-done.refs_1_), channel_id=1, source_target_pairs={{0,16},{16,0},{32,48},{48,32},{64,80},{80,64},{96,112},{112,96},{1... | collective-permute-start | bytes 393224 | tf_op jit(solution)/shard_map/ppermute | solution.py:378

commit v6 on v5

--- a/solution.py
+++ b/solution.py
@@ -117,44 +117,58 @@
     return n_order, n_used
 
 
-def send_kernel(n_planes, n_order, t_dev, count_ref, plane_ref, tile_ref, vis_ref, out_ref, *rest):
-    tables, sem = rest[:-1], rest[-1]
-    halves, dests = vis_ref.shape[:2]
+def send_kernel(n_planes, n_order, t_dev, *refs):
+    (count_hbm, plane_hbm, tile_hbm, delay_hbm, vis_hbm), refs = refs[:5], refs[5:]
+    (out_ref, delay_ref, *tables), (count_ref, plane_ref, tile_ref, small_sem, sem) = refs[:-5], refs[-5:]
+    smalls = [
+        pltpu.make_async_copy(count_hbm, count_ref, small_sem.at[0]),
+        pltpu.make_async_copy(plane_hbm, plane_ref, small_sem.at[1]),
+        pltpu.make_async_copy(tile_hbm, tile_ref, small_sem.at[2]),
+        pltpu.make_async_copy(delay_hbm.at[lax.axis_index("chan")], delay_ref, small_sem.at[3]),
+    ]
+    for copy in smalls:
+        copy.start()
+    halves, dests = vis_hbm.shape[:2]
     n = sem.shape[1]
     copies = []
     for i in range(n):
         at = pl.ds(i * (dests // n), dests // n)
         for h in range(halves):
-            copies.append(pltpu.make_async_copy(vis_ref.at[h, at], out_ref.at[at, h], sem.at[h, i]))
+            copies.append(pltpu.make_async_copy(vis_hbm.at[h, at], out_ref.at[at, h], sem.at[h, i]))
             copies[-1].start()
+    for copy in smalls:
+        copy.wait()
     fill_tables(n_planes, n_order, t_dev, count_ref, plane_ref, tile_ref, *tables)
     for copy in copies:
         copy.wait()
 
 
-def send_order(counts, planes, tiles, vis, n_planes, t_dev):
+def send_order(counts, planes, tiles, delays, vis, n_planes, t_dev):
     halves, dests, rows, bv = vis.shape
     n_rows = planes.shape[0] * planes.shape[1]
     n_order, n_used = sizes(n_rows, n_planes)
+    args = [pltpu.with_memory_space_constraint(x, pltpu.HBM) for x in (counts, planes, tiles, delays, vis)]
     return pl.pallas_call(
         functools.partial(send_kernel, n_planes, n_order, t_dev),
         out_shape=[
             jax.ShapeDtypeStruct((dests, halves, rows, bv), vis.dtype),
+            jax.ShapeDtypeStruct(delays.shape[1:], delays.dtype),
             jax.ShapeDtypeStruct((1, n_rows), jnp.int32),
             jax.ShapeDtypeStruct((1, n_used), jnp.int32),
             jax.ShapeDtypeStruct((8, 128), jnp.int32),
         ],
-        in_specs=[
-            pl.BlockSpec(memory_space=pltpu.SMEM),
-            vmem(),
-            vmem(),
-            pl.BlockSpec(memory_space=pltpu.HBM),
+        in_specs=[pl.BlockSpec(memory_space=pltpu.HBM)] * len(args),
+        out_specs=[vmem()] * 5,
+        scratch_shapes=[
+            pltpu.SMEM(counts.shape, jnp.int32),
+            pltpu.VMEM(planes.shape, jnp.int32),
+            pltpu.VMEM(tiles.shape, jnp.int32),
+            pltpu.SemaphoreType.DMA((4,)),
+            pltpu.SemaphoreType.DMA((halves, 8)),
         ],
-        out_specs=[vmem()] * 4,
-        scratch_shapes=[pltpu.SemaphoreType.DMA((halves, 4))],
         compiler_params=pltpu.CompilerParams(vmem_limit_bytes=32 * MIB),
         name="send_order",
-    )(counts, planes, tiles, pltpu.with_memory_space_constraint(vis, pltpu.HBM))
+    )(*args)
 
 
 def fill_turns(d, inner_ref, outer_ref):
@@ -174,10 +188,7 @@
         turn = times(turn, step)
 
 
-def average_kernel(delay_hbm, vis_ref, out_ref, delay_ref, inner_ref, outer_ref, sem):
-    fetch = pltpu.make_async_copy(delay_hbm.at[lax.axis_index("chan")], delay_ref, sem.at[0])
-    fetch.start()
-    fetch.wait()
+def average_kernel(delay_ref, vis_ref, out_ref, inner_ref, outer_ref):
     fill_turns(delay_ref[...], inner_ref, outer_ref)
     n_out, _, rows, _ = out_ref.shape
     for r in range(0, rows, 16):
@@ -203,88 +214,137 @@
         lax.fori_loop(0, n_out, one, 0, unroll=4)
 
 
-def average(delays, vis):
+def average(delay, vis):
     n_ch, halves, rows, bv = vis.shape
     n_out = n_ch // AVG
     return pl.pallas_call(
         average_kernel,
         out_shape=jax.ShapeDtypeStruct((n_out, halves, rows, bv), jnp.bfloat16),
-        in_specs=[pl.BlockSpec(memory_space=pltpu.HBM), vmem()],
+        in_specs=[vmem()] * 2,
         out_specs=vmem(),
         scratch_shapes=[
-            pltpu.VMEM((rows, bv), jnp.float32),
             pltpu.VMEM((AVG - 1, 2, rows, bv), jnp.float32),
             pltpu.VMEM((n_out, 2, rows, bv), jnp.float32),
-            pltpu.SemaphoreType.DMA((1,)),
         ],
         compiler_params=pltpu.CompilerParams(vmem_limit_bytes=12 * MIB),
         name="average",
-    )(pltpu.with_memory_space_constraint(delays, pltpu.HBM), vis)
-
-
-def grid_kernel(n_pieces, piece_ref, place_ref, code_ref, rows_ref, k_hbm, out_ref, k_ref, x_ref, c_ref, sem):
-    n_fetch = sem.shape[0]
-    part = k_ref.shape[0] // n_fetch
+    )(delay, vis)
+
+
+def products(n_pieces, column, piece_ref, k_hbm, k_ref, x_ref, c_ref, sem, before):
+    n_fetch = sem.shape[1]
+    planes, _, width = k_ref.shape
+    part = planes // n_fetch
+    run = width // 2
+    half = k_hbm.shape[2] // 2
     fetches = []
     for i in range(n_fetch):
         at = pl.ds(i * part, part)
-        fetches.append(pltpu.make_async_copy(k_hbm.at[at], k_ref.at[at], sem.at[i]))
-        fetches[-1].start()
-    n_src, _, per, bv = rows_ref.shape
-    n_order = x_ref.shape[0]
-    re = rows_ref[:, 0].reshape(n_src * per, bv)
-    im = rows_ref[:, 1].reshape(n_src * per, bv)
-    x = jnp.concatenate([re, im], axis=1)
-    order = to_bf16(iota((n_order, n_src * per), 0) == place_ref[...])
-    x_ref[...] = jnp.dot(order, x, preferred_element_type=jnp.float32).astype(jnp.bfloat16)
-    n_used = code_ref.shape[1]
-    n_codes = out_ref.shape[0] * out_ref.shape[1]
-    tiles = to_bf16(iota((n_codes, n_used), 0) == code_ref[...])
+        for j in range(2):
+            source = k_hbm.at[at, :, pl.ds(j * half + column * run, run)]
+            fetches.append(pltpu.make_async_copy(source, k_ref.at[at, :, pl.ds(j * run, run)], sem.at[j, i]))
+            fetches[-1].start()
+    before()
     c_ref[...] = jnp.zeros_like(c_ref)
     had = jnp.int32(0)
     for i in range(n_pieces):
         if i % STRETCH == 0:
             need = n_fetch if i + STRETCH >= n_pieces else piece_ref[1, i + STRETCH - 1] // part + 1
-            for k, fetch in enumerate(fetches):
+            for k in range(n_fetch):
 
                 @pl.when((k >= had) & (k < need))
-                def _(fetch=fetch):
-                    fetch.wait()
+                def _(k=k):
+                    fetches[2 * k].wait()
+                    fetches[2 * k + 1].wait()
 
             had = jnp.maximum(had, need)
         at = pl.ds(pl.multiple_of(piece_ref[0, i] * GROUP, GROUP), PIECE)
         product = jnp.dot(x_ref[at, :], k_ref[piece_ref[1, i]], preferred_element_type=jnp.float32)
         c_ref[at, :] = product.astype(jnp.bfloat16)
+
+
+def sum_tiles(code_ref, c_ref, out_ref):
+    n_used = code_ref.shape[1]
+    n_codes = out_ref.shape[0] * out_ref.shape[1]
+    tiles = to_bf16(iota((n_codes, n_used), 0) == code_ref[...])
     grid = jnp.dot(tiles, c_ref[:n_used, :], preferred_element_type=jnp.float32)
     out_ref[...] = grid.astype(jnp.bfloat16).reshape(out_ref.shape)
 
 
-def grid_rows(piece, place, code, rows, kernels, n_codes):
+def grid_first_kernel(n_pieces, *refs):
+    piece_vmem, place_ref, code_ref, rows_ref, k_hbm, out_ref, x_ref, piece_ref, k_ref, c_ref, sem, piece_sem = refs
+    fetch = pltpu.make_async_copy(piece_vmem, piece_ref, piece_sem.at[0])
+    fetch.start()
+
+    def before():
+        n_src, _, per, bv = rows_ref.shape
+        re = rows_ref[:, 0].reshape(n_src * per, bv)
+        im = rows_ref[:, 1].reshape(n_src * per, bv)
+        x = jnp.concatenate([re, im], axis=1)
+        order = to_bf16(iota((x_ref.shape[0], n_src * per), 0) == place_ref[...])
+        x_ref[...] = jnp.dot(order, x, preferred_element_type=jnp.float32).astype(jnp.bfloat16)
+        fetch.wait()
+
+    products(n_pieces, 0, piece_ref, k_hbm, k_ref, x_ref, c_ref, sem, before)
+    sum_tiles(code_ref, c_ref, out_ref)
+
+
+def grid_second_kernel(n_pieces, *refs):
+    piece_vmem, code_ref, x_ref, k_hbm, out_ref, piece_ref, k_ref, c_ref, sem, piece_sem = refs
+    fetch = pltpu.make_async_copy(piece_vmem, piece_ref, piece_sem.at[0])
+    fetch.start()
+    products(n_pieces, 1, piece_ref, k_hbm, k_ref, x_ref, c_ref, sem, fetch.wait)
+    sum_tiles(code_ref, c_ref, out_ref)
+
+
+def grid_scratch(piece, n_order, kernels):
+    n_planes, k_rows, cells = kernels.shape
+    return [
+        pltpu.SMEM(piece.shape, jnp.int32),
+        pltpu.VMEM((n_planes, k_rows, cells // 2), jnp.bfloat16),
+        pltpu.VMEM((n_order, cells // 2), jnp.bfloat16),
+        pltpu.SemaphoreType.DMA((2, 4)),
+        pltpu.SemaphoreType.DMA((1,)),
+    ]
+
+
+def grid_first(piece, place, code, rows, kernels, n_codes):
     n_planes, k_rows, cells = kernels.shape
     n_rows = place.shape[1]
     n_chan = rows.shape[0]
     n_order, n_used = sizes(n_rows, n_planes)
     return pl.pallas_call(
-        functools.partial(grid_kernel, n_rows // PIECE + n_planes),
-        out_shape=jax.ShapeDtypeStruct((n_chan, n_codes // n_chan, cells), jnp.bfloat16),
-        in_specs=[pl.BlockSpec(memory_space=pltpu.SMEM)] + [vmem()] * 3 + [pl.BlockSpec(memory_space=pltpu.HBM)],
+        functools.partial(grid_first_kernel, n_rows // PIECE + n_planes),
+        out_shape=[
+            jax.ShapeDtypeStruct((n_chan, n_codes // n_chan, cells // 2), jnp.bfloat16),
+            jax.ShapeDtypeStruct((n_order, k_rows), jnp.bfloat16),
+        ],
+        in_specs=[vmem()] * 4 + [pl.BlockSpec(memory_space=pltpu.HBM)],
+        out_specs=[vmem()] * 2,
+        scratch_shapes=grid_scratch(piece, n_order, kernels),
+        compiler_params=pltpu.CompilerParams(vmem_limit_bytes=32 * MIB),
+        name="grid_first",
+    )(piece, place, code, rows, pltpu.with_memory_space_constraint(kernels, pltpu.HBM))
+
+
+def grid_second(piece, code, ordered, kernels, n_rows, n_chan, n_codes):
+    n_planes, k_rows, cells = kernels.shape
+    n_order, n_used = sizes(n_rows, n_planes)
+    return pl.pallas_call(
+        functools.partial(grid_second_kernel, n_rows // PIECE + n_planes),
+        out_shape=jax.ShapeDtypeStruct((n_chan, n_codes // n_chan, cells // 2), jnp.bfloat16),
+        in_specs=[vmem()] * 3 + [pl.BlockSpec(memory_space=pltpu.HBM)],
         out_specs=vmem(),
-        scratch_shapes=[
-            pltpu.VMEM(kernels.shape, kernels.dtype),
-            pltpu.VMEM((n_order, k_rows), jnp.bfloat16),
-            pltpu.VMEM((n_order, cells), jnp.bfloat16),
-            pltpu.SemaphoreType.DMA((8,)),
-        ],
-        compiler_params=pltpu.CompilerParams(vmem_limit_bytes=40 * MIB),
-        name="grid_rows",
-    )(piece, place, code, rows, pltpu.with_memory_space_constraint(kernels, pltpu.HBM))
+        scratch_shapes=grid_scratch(piece, n_order, kernels),
+        compiler_params=pltpu.CompilerParams(vmem_limit_bytes=32 * MIB),
+        name="grid_second",
+    )(piece, code, ordered, pltpu.with_memory_space_constraint(kernels, pltpu.HBM))
 
 
 def strip_kernel(main_ref, out_ref):
-    n_out, per, cells = main_ref.shape
-    half = cells // 2
-    low = main_ref[:, :, 0:128].reshape(n_out * per, 128).astype(jnp.float32)
-    high = main_ref[:, :, half : half + 128].reshape(n_out * per, 128).astype(jnp.float32)
+    n_out, per, width = main_ref.shape
+    low = main_ref[:, :, :128].reshape(n_out * per, 128).astype(jnp.float32)
+    high = main_ref[:, :, 128:].reshape(n_out * per, 128).astype(jnp.float32)
     lane = lax.broadcasted_iota(jnp.int32, low.shape, 1)
     strip = jnp.where(lane < STRIP, low, pltpu.roll(high, STRIP, 1)).astype(jnp.bfloat16)
     out_ref[...] = strip.reshape(out_ref.shape)
@@ -302,11 +362,11 @@
     )(main)
 
 
-def join_kernel(nb_ref, main_ref, *refs):
+def join_kernel(nb_ref, first_ref, second_ref, *refs):
     strips, out_ref, strip_ref = refs[:-2], refs[-2], refs[-1]
-    n_out, per, cells = main_ref.shape
+    n_out, per, width = first_ref.shape
     t_dev = per // 2
-    half = cells // 2
+    run = width // 2
     n_rows = n_out * t_dev
     for i, ref in enumerate(strips):
         strip_ref[i] = ref[...].reshape(strip_ref.shape[1:])
@@ -322,29 +382,33 @@
             strip = strip_ref[nb_ref[slot, k], :, nb_ref[slot, n_nb + k]].reshape(n_rows, 2 * STRIP)
             blend += jnp.dot(quarter, strip, preferred_element_type=jnp.float32)
         swapped = pltpu.roll(blend, STRIP, 1)
-        main = main_ref[:, slot * t_dev : (slot + 1) * t_dev, :].reshape(n_rows, cells)
-        main = jnp.dot(place, main, preferred_element_type=jnp.float32)
-
-        def put(lo, hi, value, slot=slot):
-            out_ref[:, slot, :, lo:hi] = value.reshape(t_dev, n_out, hi - lo)
-
-        put(0, half - 128, main[:, 0 : half - 128])
-        put(half - 128, half, main[:, half - 128 : half] + jnp.where(upper, swapped, 0.0))
-        put(half, cells - 128, main[:, half : cells - 128])
-        put(cells - 128, cells, main[:, cells - 128 :] + jnp.where(upper, blend, 0.0))
-
-
-def join(sources, main, strips):
-    n_out, per, cells = main.shape
+        rows = slice(slot * t_dev, (slot + 1) * t_dev)
+        first = first_ref[:, rows, :].reshape(n_rows, width)
+        first = jnp.dot(place, first, preferred_element_type=jnp.float32)
+        second = second_ref[:, rows, :].reshape(n_rows, width)
+        second = jnp.dot(place, second, preferred_element_type=jnp.float32)
+        parts = [
+            first[:, :run],
+            second[:, :run] + jnp.where(upper, swapped, 0.0),
+            first[:, run:],
+            second[:, run:] + jnp.where(upper, blend, 0.0),
+        ]
+        for i, part in enumerate(parts):
+            out_ref[:, slot, :, i * run : (i + 1) * run] = part.reshape(t_dev, n_out, run)
+
+
+def join(sources, first, second, strips):
+    n_out, per, width = first.shape
+    assert width == 4 * STRIP
     return pl.pallas_call(
         join_kernel,
-        out_shape=jax.ShapeDtypeStruct((per // 2, 2, n_out, cells), jnp.float32),
-        in_specs=[pl.BlockSpec(memory_space=pltpu.SMEM)] + [vmem()] * (1 + len(strips)),
+        out_shape=jax.ShapeDtypeStruct((per // 2, 2, n_out, 2 * width), jnp.float32),
+        in_specs=[pl.BlockSpec(memory_space=pltpu.SMEM)] + [vmem()] * (2 + len(strips)),
         out_specs=vmem(),
         scratch_shapes=[pltpu.VMEM((len(strips), n_out, 2, per // 2, 2 * STRIP), jnp.bfloat16)],
         compiler_params=pltpu.CompilerParams(vmem_limit_bytes=16 * MIB),
         name="join",
-    )(sources, main, *strips)
+    )(sources, first, second, *strips)
 
 
 def exchange(x, axis):
@@ -363,14 +427,20 @@
     per = n_rows // n_chan
 
     vis = visibilities.reshape(halves, n_facet * n_chan, per, bv)
-    vis, place, code, piece = send_order(counts, plane_of, tile_of, vis, kernels.shape[0], t_dev)
+    vis, delay, place, code, piece = send_order(
+        counts, plane_of, tile_of, delays.reshape(n_chan, per, bv), vis, kernels.shape[0], t_dev
+    )
     vis = exchange(vis, ("facet", "chan"))
 
-    rows = exchange(average(delays.reshape(n_chan, per, bv), vis), "chan")
-    grids = grid_rows(piece, place, code, rows, kernels, fac_dev * n_tiles)
-    main = exchange(grids, "chan")
-
-    own = strips_of(main)
+    rows = exchange(average(delay, vis), "chan")
+    n_codes = fac_dev * n_tiles
+    grids, ordered = grid_first(piece, place, code, rows, kernels, n_codes)
+    first = exchange(grids, "chan")
+    grids = grid_second(piece, code, ordered, kernels, n_rows, n_chan, n_codes)
+
+    own = strips_of(first)
+    own, grids = lax.optimization_barrier((own, grids))
+    second = exchange(grids, "chan")
     chips = n_facet // 2
     strips = [own]
     for dz in range(1, chips):
@@ -380,7 +450,7 @@
     group = mine // fac_dev
     source = (facet_index // 2 - group // 2) % chips + chips * ((group + facet_index) % 2)
     sources = jnp.concatenate([source, mine % fac_dev], axis=1).astype(jnp.int32)
-    return join(sources, main, strips)
+    return join(sources, first, second, strips)
 
 
 def solution(mesh):

time: 121 us -> 121 us (level)
  blocking collectives: 89.1 us -> 75.9 us
  waiting for transfers between devices: 0.89 us -> 8.22 us
  starting transfers between devices: 12.3 us -> 16.5 us
  Pallas kernels: 15.9 us -> 19 us
  local copies, waits for them, and re-layouts: 2.21 us -> 0.17 us
    all_to_all x3 -> x2, blocking collectives: 89.1 us -> 75.9 us  [exchange(): return lax.all_to_all(x, axis, split_axis=0, concat_axis=0, tiled=True)]
    all_to_all x0 -> x2, waiting for transfers between devices: none -> 8.2 us  [exchange(): return lax.all_to_all(x, axis, split_axis=0, concat_axis=0, tiled=True)]
    all_to_all x0 -> x2, starting transfers between devices: none -> 7.8 us  [exchange(): return lax.all_to_all(x, axis, split_axis=0, concat_axis=0, tiled=True)]
    ppermute x4, starting transfers between devices: 9.64 us -> 6.17 us  [local(): lax.ppermute(s, 'facet', [(f, f ^ 1) for f in range(n_facet)])]
    pallas_call x1 -> x2, Pallas kernels: 8.05 us -> 11.5 us  [the longest x1 6.95 us: grid_first(): pl.pallas_call(functools.partial(grid_first_kernel, n_rows // PIECE + n_p...]
    unnamed x9 -> x3, local copies, waits for them, and re-layouts: 2.14 us -> 0.1 us
  transfers between devices with their start and end apart: 7 -> 9, of which waited for: 1 -> 2; matrix products, arithmetic and copies ran while one was open for 0% -> 0% of each run, Pallas kernels for 0% -> 4%
where the time goes in v6:
time: 121 us; the launch traced here: 120 us
  blocking collectives  75.9 us (63%)
  Pallas kernels  19 us (16%)
  starting transfers between devices  16.5 us (14%)
  waiting for transfers between devices  8.22 us (7%)
    all_to_all x2, blocking collectives, exchange(): return lax.all_to_all(x, axis, split_axis=0, concat_axis=0, tiled=True)  75.9 us
    all_to_all x2, waiting for transfers between devices, exchange(): return lax.all_to_all(x, axis, split_axis=0, concat_axis=0, tiled=True)  8.2 us
    all_to_all x2, starting transfers between devices, exchange(): return lax.all_to_all(x, axis, split_axis=0, concat_axis=0, tiled=True)  7.8 us
    pallas_call x1, Pallas kernels, grid_first(): pl.pallas_call(functools.partial(grid_first_kernel, n_rows // PIECE + n_p...  6.95 us
    ppermute x4, starting transfers between devices, local(): lax.ppermute(s, 'facet', [(f, f ^ 1) for f in range(n_facet)])  6.17 us
    pallas_call x1, Pallas kernels, grid_second(): pl.pallas_call(functools.partial(grid_second_kernel, n_rows // PIECE + n_...  4.56 us
    pallas_call x1, Pallas kernels, send_order(): pl.pallas_call(functools.partial(send_kernel, n_planes, n_order, t_dev),...  3.57 us
    ppermute x3, starting transfers between devices, local(): lax.ppermute(own, 'facet', [(f, (f + 2 * dz) % n_facet) for f in range(n_...  2.56 us
  transfers between devices with their start and end apart: 9, of which 2 were waited for; matrix products, arithmetic and copies ran while one was open for 0% of the time, Pallas kernels for 4%

profile of v6, /device:TPU:1, one launch (start us, length us, event | category | flops | bytes accessed | tf_op | source)
XLA Modules:
  0.0 120.0 jit_solution(1767292717235890578)
XLA Ops:
  0.0 0.0 copy-start
  0.0 3.6 %send_order.1 = (bf16[128,2,64,128]{3,2,1,0:T(8,128)(2,1)S(1)}, f32[64,128]{1,0:T(8,128)S(1)}, s32[1,1024]{1,0:T(1,128)S(1)}, s32[1,1536]{1,0:T(1,128)S(1)}, s32[8,128]{1,0:T(8,128)S(1)}) custom-call(s32[2]{0:T(128)} %refs_0_.1, s32[2,512]{1,0:T(2,128)} %refs_1_.1, s32[2,512]{1,0:T(2,128)} %refs_2_.1, f32[16,64,128]{2,1,0:T(8,128)} %bitcast.3, ...), custom_call_target="tpu_custom_call" | custom-call | tf_op jit(solution)/shard_map/send_order/pallas_call | solution.py:151
  3.6 64.0 %all_to_all.20.vis_ref = bf16[128,2,64,128]{3,2,1,0:T(8,128)(2,1)S(1)} all-to-all(bf16[128,2,64,128]{3,2,1,0:T(8,128)(2,1)S(1)} %get-tuple-element.18), channel_id=1, replica_groups=mesh['facet'=8,'chan'=16] {'facet','chan'}, dimensions={0} | all-to-all | bytes 8388608 | tf_op jit(solution)/shard_map/all_to_all | solution.py:415
  67.5 1.7 %average.1 = bf16[16,2,64,128]{3,2,1,0:T(8,128)(2,1)S(1)} custom-call(f32[64,128]{1,0:T(8,128)S(1)} %get-tuple-element.17.delay_ref, bf16[128,2,64,128]{3,2,1,0:T(8,128)(2,1)S(1)} %all_to_all.20.vis_ref), custom_call_target="tpu_custom_call" | custom-call | tf_op jit(solution)/shard_map/average/pallas_call | solution.py:220
  69.3 11.9 %all_to_all.21.refs_3_ = bf16[16,2,64,128]{3,2,1,0:T(8,128)(2,1)S(1)} all-to-all(bf16[16,2,64,128]{3,2,1,0:T(8,128)(2,1)S(1)} %average.1), channel_id=1, replica_groups=mesh['facet'=8,'chan'=16] {'chan'}, dimensions={0} | all-to-all | bytes 1048576 | tf_op jit(solution)/shard_map/all_to_all | solution.py:415
  81.2 7.0 %grid_first.1 = (bf16[16,32,256]{2,1,0:T(8,128)(2,1)}, bf16[1568,256]{1,0:T(8,128)(2,1)S(1)}) custom-call(s32[8,128]{1,0:T(8,128)S(1)} %get-tuple-element.14.refs_0_, s32[1,1024]{1,0:T(1,128)S(1)} %get-tuple-element.15.refs_1_, s32[1,1536]{1,0:T(1,128)S(1)} %get-tuple-element.16.refs_2_.refs_1_, bf16[16,2,64,128]{3,2,1,0:T(8,128)(2,1)S(1)} %all_to_all.21.refs_3_, ...), custom_call_target="tpu_custom_call" | custom-call | tf_op jit(solution)/shard_map/grid_first/pallas_call | solution.py:316
  88.1 4.3 %all-to-all-start.2 = ((bf16[16,32,256]{2,1,0:T(8,128)(2,1)}), bf16[16,32,256]{2,1,0:T(8,128)(2,1)S(1)}, u32[]{:S(2)}, u32[]{:S(2)}) async-start(bf16[16,32,256]{2,1,0:T(8,128)(2,1)} %get-tuple-element.19), calls=%async_computation.2 | async-start | bytes 524288 | tf_op jit(solution)/shard_map/all_to_all | solution.py:415
  92.4 4.6 %grid_second.1 = bf16[16,32,256]{2,1,0:T(8,128)(2,1)} custom-call(s32[8,128]{1,0:T(8,128)S(1)} %get-tuple-element.14.refs_0_, s32[1,1536]{1,0:T(1,128)S(1)} %get-tuple-element.16.refs_2_.refs_1_, bf16[1568,256]{1,0:T(8,128)(2,1)S(1)} %get-tuple-element.20.refs_2_, bf16[32,256,512]{2,1,0:T(8,128)(2,1)} %refs_3_.1), custom_call_target="tpu_custom_call" | custom-call | tf_op jit(solution)/shard_map/grid_second/pallas_call | solution.py:333
  97.0 2.8 %all-to-all-done.2.main_ref.first_ref = bf16[16,32,256]{2,1,0:T(8,128)(2,1)S(1)} async-done(((bf16[16,32,256]{2,1,0:T(8,128)(2,1)}), bf16[16,32,256]{2,1,0:T(8,128)(2,1)S(1)}, u32[]{:S(2)}, u32[]{:S(2)}) %all-to-all-start.2) | async-done | bytes 262176 | tf_op jit(solution)/shard_map/all_to_all | solution.py:415
  99.7 0.1 strips.1.refs_0_
  99.8 0.4 collective-permute-start.2
  100.3 2.1 %collective-permute-start.1 = (bf16[16,32,128]{2,1,0:T(8,128)(2,1)S(1)}, bf16[16,32,128]{2,1,0:T(8,128)(2,1)S(1)}, u32[]{:S(2)}, u32[]{:S(2)}) collective-permute-start(bf16[16,32,128]{2,1,0:T(8,128)(2,1)S(1)} %strips.1.refs_0_), channel_id=1, source_target_pairs={{0,64},{16,80},{32,96},{48,112},{64,0},{80,16},{96,32},{112,48},{1... | collective-permute-start | bytes 393224 | tf_op jit(solution)/shard_map/ppermute | solution.py:447
  102.3 0.0 collective-permute-start
  102.4 0.0 copy-done
  102.4 0.1 constant_dynamic-slice_fusion
  102.5 0.1 copy.9
  102.6 3.9 %collective-permute-start.3 = (bf16[16,32,128]{2,1,0:T(8,128)(2,1)S(1)}, bf16[16,32,128]{2,1,0:T(8,128)(2,1)S(1)}, u32[]{:S(2)}, u32[]{:S(2)}) collective-permute-start(bf16[16,32,128]{2,1,0:T(8,128)(2,1)S(1)} %strips.1.refs_0_), channel_id=1, source_target_pairs={{0,16},{16,0},{32,48},{48,32},{64,80},{80,64},{96,112},{112,96},{1... | collective-permute-start | bytes 393224 | tf_op jit(solution)/shard_map/ppermute | solution.py:448
  106.5 3.5 %all-to-all-start.3 = ((bf16[16,32,256]{2,1,0:T(8,128)(2,1)}), bf16[16,32,256]{2,1,0:T(8,128)(2,1)S(1)}, u32[]{:S(2)}, u32[]{:S(2)}) async-start(bf16[16,32,256]{2,1,0:T(8,128)(2,1)} %grid_second.1), calls=%async_computation.3 | async-start | bytes 524288 | tf_op jit(solution)/shard_map/all_to_all | solution.py:415
  110.0 0.0 collective-permute-done.2.refs_3_
  110.0 0.2 collective-permute-start.6
  110.2 0.0 collective-permute-done.1.refs_2_
  110.2 0.6 collective-permute-start.5
  110.9 0.0 collective-permute-done.refs_1_
  110.9 1.4 %collective-permute-start.4 = (bf16[16,32,128]{2,1,0:T(8,128)(2,1)S(1)}, bf16[16,32,128]{2,1,0:T(8,128)(2,1)S(1)}, u32[]{:S(2)}, u32[]{:S(2)}) collective-permute-start(bf16[16,32,128]{2,1,0:T(8,128)(2,1)S(1)} %collective-permute-done.refs_1_), channel_id=1, source_target_pairs={{0,16},{16,0},{32,48},{48,32},{64,80},{80,64},{96,112},{112,96},{1... | collective-permute-start | bytes 393224 | tf_op jit(solution)/shard_map/ppermute | solution.py:448
  112.3 0.1 pad_add_fusion.nb_ref
  112.4 0.0 collective-permute-done.3.refs_4_
  112.4 5.4 %all-to-all-done.3.second_ref = bf16[16,32,256]{2,1,0:T(8,128)(2,1)S(1)} async-done(((bf16[16,32,256]{2,1,0:T(8,128)(2,1)}), bf16[16,32,256]{2,1,0:T(8,128)(2,1)S(1)}, u32[]{:S(2)}, u32[]{:S(2)}) %all-to-all-start.3) | async-done | bytes 262176 | tf_op jit(solution)/shard_map/all_to_all | solution.py:415
  117.8 0.0 collective-permute-done.6.refs_7_
  117.8 0.0 collective-permute-done.5.refs_6_
  117.8 0.0 collective-permute-done.4.refs_5_
  117.8 2.2 %join.1 = f32[16,2,16,512]{3,2,1,0:T(8,128)} custom-call(s32[2,8]{1,0:T(2,128)S(1)} %pad_add_fusion.nb_ref, bf16[16,32,256]{2,1,0:T(8,128)(2,1)S(1)} %all-to-all-done.2.main_ref.first_ref, bf16[16,32,256]{2,1,0:T(8,128)(2,1)S(1)} %all-to-all-done.3.second_ref, bf16[16,32,128]{2,1,0:T(8,128)(2,1)S(1)} %strips.1.refs_0_, ...), custom_call_target="tpu_custom_call" | custom-call | tf_op jit(solution)/shard_map/join/pallas_call | solution.py:403
  (1 shorter events, 0.0 us)
Async XLA Ops:
  0.0 102.4 %copy-start = (s32[16,4]{0,1:T(4,128)S(1)}, s32[16,4]{0,1:T(4,128)}, u32[]{:S(2)}) copy-start(s32[16,4]{0,1:T(4,128)} %param.13) | copy-start | bytes 772
  88.1 11.6 %all-to-all-start.2 = ((bf16[16,32,256]{2,1,0:T(8,128)(2,1)}), bf16[16,32,256]{2,1,0:T(8,128)(2,1)S(1)}, u32[]{:S(2)}, u32[]{:S(2)}) async-start(bf16[16,32,256]{2,1,0:T(8,128)(2,1)} %get-tuple-element.19), calls=%async_computation.2 | async-start | bytes 524288 | tf_op jit(solution)/shard_map/all_to_all | solution.py:415
  99.8 10.2 %collective-permute-start.2 = (bf16[16,32,128]{2,1,0:T(8,128)(2,1)S(1)}, bf16[16,32,128]{2,1,0:T(8,128)(2,1)S(1)}, u32[]{:S(2)}, u32[]{:S(2)}) collective-permute-start(bf16[16,32,128]{2,1,0:T(8,128)(2,1)S(1)} %strips.1.refs_0_), channel_id=1, source_target_pairs={{0,96},{16,112},{32,0},{48,16},{64,32},{80,48},{96,64},{112,80},{1... | collective-permute-start | bytes 393224 | tf_op jit(solution)/shard_map/ppermute | solution.py:447
  100.3 10.0 %collective-permute-start.1 = (bf16[16,32,128]{2,1,0:T(8,128)(2,1)S(1)}, bf16[16,32,128]{2,1,0:T(8,128)(2,1)S(1)}, u32[]{:S(2)}, u32[]{:S(2)}) collective-permute-start(bf16[16,32,128]{2,1,0:T(8,128)(2,1)S(1)} %strips.1.refs_0_), channel_id=1, source_target_pairs={{0,64},{16,80},{32,96},{48,112},{64,0},{80,16},{96,32},{112,48},{1... | collective-permute-start | bytes 393224 | tf_op jit(solution)/shard_map/ppermute | solution.py:447
  102.3 8.5 %collective-permute-start = (bf16[16,32,128]{2,1,0:T(8,128)(2,1)S(1)}, bf16[16,32,128]{2,1,0:T(8,128)(2,1)S(1)}, u32[]{:S(2)}, u32[]{:S(2)}) collective-permute-start(bf16[16,32,128]{2,1,0:T(8,128)(2,1)S(1)} %strips.1.refs_0_), channel_id=1, source_target_pairs={{0,32},{16,48},{32,64},{48,80},{64,96},{80,112},{96,0},{112,16},{1... | collective-permute-start | bytes 393224 | tf_op jit(solution)/shard_map/ppermute | solution.py:447
  102.6 9.8 %collective-permute-start.3 = (bf16[16,32,128]{2,1,0:T(8,128)(2,1)S(1)}, bf16[16,32,128]{2,1,0:T(8,128)(2,1)S(1)}, u32[]{:S(2)}, u32[]{:S(2)}) collective-permute-start(bf16[16,32,128]{2,1,0:T(8,128)(2,1)S(1)} %strips.1.refs_0_), channel_id=1, source_target_pairs={{0,16},{16,0},{32,48},{48,32},{64,80},{80,64},{96,112},{112,96},{1... | collective-permute-start | bytes 393224 | tf_op jit(solution)/shard_map/ppermute | solution.py:448
  106.5 11.4 %all-to-all-start.3 = ((bf16[16,32,256]{2,1,0:T(8,128)(2,1)}), bf16[16,32,256]{2,1,0:T(8,128)(2,1)S(1)}, u32[]{:S(2)}, u32[]{:S(2)}) async-start(bf16[16,32,256]{2,1,0:T(8,128)(2,1)} %grid_second.1), calls=%async_computation.3 | async-start | bytes 524288 | tf_op jit(solution)/shard_map/all_to_all | solution.py:415
  110.0 7.8 %collective-permute-start.6 = (bf16[16,32,128]{2,1,0:T(8,128)(2,1)S(1)}, bf16[16,32,128]{2,1,0:T(8,128)(2,1)S(1)}, u32[]{:S(2)}, u32[]{:S(2)}) collective-permute-start(bf16[16,32,128]{2,1,0:T(8,128)(2,1)S(1)} %collective-permute-done.2.refs_3_), channel_id=1, source_target_pairs={{0,16},{16,0},{32,48},{48,32},{64,80},{80,64},{96,112},{112,96},{1... | collective-permute-start | bytes 393224 | tf_op jit(solution)/shard_map/ppermute | solution.py:448
  110.2 7.6 %collective-permute-start.5 = (bf16[16,32,128]{2,1,0:T(8,128)(2,1)S(1)}, bf16[16,32,128]{2,1,0:T(8,128)(2,1)S(1)}, u32[]{:S(2)}, u32[]{:S(2)}) collective-permute-start(bf16[16,32,128]{2,1,0:T(8,128)(2,1)S(1)} %collective-permute-done.1.refs_2_), channel_id=1, source_target_pairs={{0,16},{16,0},{32,48},{48,32},{64,80},{80,64},{96,112},{112,96},{1... | collective-permute-start | bytes 393224 | tf_op jit(solution)/shard_map/ppermute | solution.py:448
  110.9 7.0 %collective-permute-start.4 = (bf16[16,32,128]{2,1,0:T(8,128)(2,1)S(1)}, bf16[16,32,128]{2,1,0:T(8,128)(2,1)S(1)}, u32[]{:S(2)}, u32[]{:S(2)}) collective-permute-start(bf16[16,32,128]{2,1,0:T(8,128)(2,1)S(1)} %collective-permute-done.refs_1_), channel_id=1, source_target_pairs={{0,16},{16,0},{32,48},{48,32},{64,80},{80,64},{96,112},{112,96},{1... | collective-permute-start | bytes 393224 | tf_op jit(solution)/shard_map/ppermute | solution.py:448

commit v7 on v5

v7 whole, which is shorter than its diff:
```python
import functools
import math

import jax
import jax.numpy as jnp
from jax import lax
from jax.experimental import pallas as pl
from jax.experimental.pallas import tpu as pltpu
from jax.sharding import PartitionSpec as P

AVG = 8
TS = 16
EDGE = 4
STRIP = EDGE * TS
GROUP = 16
PIECE = 64
STRETCH = 8
MIB = 1024 * 1024

SIN = (-1.0 / 6, 1.0 / 120, -1.0 / 5040, 1.0 / 362880, -1.0 / 39916800)
COS = (-1.0 / 2, 1.0 / 24, -1.0 / 720, 1.0 / 40320, -1.0 / 3628800, 1.0 / 479001600)


def series(turns):
    x = (2.0 * math.pi) * turns
    y = x * x
    s = jnp.full_like(x, SIN[-1])
    for k in SIN[-2::-1]:
        s = s * y + k
    c = jnp.full_like(x, COS[-1])
    for k in COS[-2::-1]:
        c = c * y + k
    return c * y + 1.0, (s * y + 1.0) * x


def turn_by(turns):
    half = jnp.round(2.0 * turns)
    c, s = series(turns - 0.5 * half)
    odd = (half - 2.0 * jnp.floor(0.5 * half)) > 0.5
    sign = jnp.where(odd, -1.0, 1.0)
    return c * sign, s * sign


def times(a, b):
    return a[0] * b[0] - a[1] * b[1], a[0] * b[1] + a[1] * b[0]


def vmem():
    return pl.BlockSpec(memory_space=pltpu.VMEM)


def to_bf16(mask):
    return mask.astype(jnp.float32).astype(jnp.bfloat16)


def iota(shape, dim):
    return lax.broadcasted_iota(jnp.int32, shape, dim)


def fill_tables(n_planes, n_order, t_dev, count_ref, plane_ref, tile_ref, order_ref, tiles_ref, piece_ref):
    f32 = jnp.float32
    slots, blocks = plane_ref.shape
    n_rows = slots * blocks
    planes, tiles = [], []
    for slot in range(slots):
        alive = iota((1, blocks), 1) < count_ref[slot]
        planes.append(jnp.where(alive, plane_ref[slot : slot + 1, :], -1))
        tiles.append(tile_ref[slot : slot + 1, :])
    plane = jnp.concatenate(planes, axis=1)
    tile = jnp.concatenate(tiles, axis=1)
    mine = plane == iota((n_planes, n_rows), 0)
    before = to_bf16(iota((n_rows, n_rows), 0) < iota((n_rows, n_rows), 1))
    rank = jnp.dot(to_bf16(mine), before, preferred_element_type=f32)
    count = jnp.sum(mine.astype(f32), axis=1, keepdims=True)
    groups = jnp.floor((count + (GROUP - 1)) * (1.0 / GROUP))
    pieces = jnp.floor((groups + (PIECE // GROUP - 1)) * (GROUP / PIECE))
    earlier = to_bf16(iota((n_planes, n_planes), 1) < iota((n_planes, n_planes), 0))
    both = jnp.concatenate(
        [jnp.broadcast_to(groups, (n_planes, 128)), jnp.broadcast_to(pieces, (n_planes, 128))], axis=1
    )
    both = jnp.dot(earlier, both.astype(jnp.bfloat16), preferred_element_type=f32)
    first_group = both[:, 0:1]
    first_piece = both[:, 128:129]
    place = jnp.sum(jnp.where(mine, rank + GROUP * first_group, 0.0), axis=0, keepdims=True)
    live = jnp.sum(mine.astype(f32), axis=0, keepdims=True)
    place = jnp.where(live > 0.5, place, -1.0).astype(jnp.int32)
    order = to_bf16(iota((n_order, n_rows), 0) == place)
    order_ref[...] = order

    row = iota((8, n_rows), 0)
    slot = (iota((8, n_rows), 1) >= n_rows // 2).astype(f32)
    values = jnp.where(row == 0, tile.astype(f32) + 1.0, jnp.where(row == 1, slot, 0.0))
    n_codes, n_used = tiles_ref.shape
    ordered = lax.dot_general(
        values.astype(jnp.bfloat16), order[:n_used], (((1,), (1,)), ((), ())), preferred_element_type=f32
    )
    tile = ordered[0:1].astype(jnp.int32) - 1
    slot = ordered[1:2].astype(jnp.int32)
    code = (tile // t_dev) * (2 * t_dev) + slot * t_dev + tile % t_dev
    code = jnp.where(tile < 0, -1, code)
    tiles_ref[...] = to_bf16(iota((n_codes, n_used), 0) == code)

    lower = jnp.sum(jnp.where(iota((n_planes, 1), 0) < n_planes // 2, pieces, 0.0))
    upper = jnp.sum(pieces) - lower
    lane = iota((n_planes, 128), 1)
    at = (lane % 64).astype(f32)
    is_upper = lane >= 64
    which = jnp.minimum(at, jnp.where(is_upper, upper, lower) - 1.0) + jnp.where(is_upper, lower, 0.0)
    taken = (which >= first_piece) & (which < first_piece + pieces)
    group = first_group + (PIECE // GROUP) * (which - first_piece)
    group = jnp.sum(jnp.where(taken, group, 0.0), axis=0, keepdims=True)
    owner = jnp.sum(jnp.where(taken, iota((n_planes, 128), 0).astype(f32), 0.0), axis=0, keepdims=True)
    owner = owner - jnp.where(iota((1, 128), 1) >= 64, float(n_planes // 2), 0.0)
    row = iota((8, 128), 0)
    totals = jnp.where(iota((8, 128), 1) >= 64, upper, lower)
    value = jnp.where(row == 0, group, jnp.where(row == 1, jnp.maximum(owner, 0.0), jnp.where(row == 2, totals, 0.0)))
    piece_ref[...] = value.astype(jnp.int32)


def sizes(n_rows, n_planes):
    used = n_rows + n_planes * (GROUP - 1)
    n_order = -(-(used - GROUP + PIECE) // 32) * 32
    n_used = -(-used // 256) * 256
    assert n_used <= n_order
    return n_order, n_used


def send_kernel(n_planes, n_order, t_dev, *refs):
    (count_hbm, plane_hbm, tile_hbm, delay_hbm, vis_hbm), refs = refs[:5], refs[5:]
    (out_ref, delay_ref, *tables), (count_ref, plane_ref, tile_ref, small_sem, sem) = refs[:-5], refs[-5:]
    smalls = [
        pltpu.make_async_copy(count_hbm, count_ref, small_sem.at[0]),
        pltpu.make_async_copy(plane_hbm, plane_ref, small_sem.at[1]),
        pltpu.make_async_copy(tile_hbm, tile_ref, small_sem.at[2]),
        pltpu.make_async_copy(delay_hbm.at[lax.axis_index("chan")], delay_ref, small_sem.at[3]),
    ]
    for copy in smalls:
        copy.start()
    halves, dests = vis_hbm.shape[:2]
    n = sem.shape[1]
    copies = []
    for i in range(n):
        at = pl.ds(i * (dests // n), dests // n)
        for h in range(halves):
            copies.append(pltpu.make_async_copy(vis_hbm.at[h, at], out_ref.at[at, h], sem.at[h, i]))
            copies[-1].start()
    for copy in smalls:
        copy.wait()
    fill_tables(n_planes, n_order, t_dev, count_ref, plane_ref, tile_ref, *tables)
    for copy in copies:
        copy.wait()


def send_order(counts, planes, tiles, delays, vis, n_planes, n_codes, t_dev):
    halves, dests, rows, bv = vis.shape
    n_rows = planes.shape[0] * planes.shape[1]
    n_order, n_used = sizes(n_rows, n_planes)
    args = [pltpu.with_memory_space_constraint(x, pltpu.HBM) for x in (counts, planes, tiles, delays, vis)]
    return pl.pallas_call(
        functools.partial(send_kernel, n_planes, n_order, t_dev),
        out_shape=[
            jax.ShapeDtypeStruct((dests, halves, rows, bv), vis.dtype),
            jax.ShapeDtypeStruct(delays.shape[1:], delays.dtype),
            jax.ShapeDtypeStruct((n_order, n_rows), jnp.bfloat16),
            jax.ShapeDtypeStruct((n_codes, n_used), jnp.bfloat16),
            jax.ShapeDtypeStruct((8, 128), jnp.int32),
        ],
        in_specs=[pl.BlockSpec(memory_space=pltpu.HBM)] * len(args),
        out_specs=[vmem()] * 5,
        scratch_shapes=[
            pltpu.SMEM(counts.shape, jnp.int32),
            pltpu.VMEM(planes.shape, jnp.int32),
            pltpu.VMEM(tiles.shape, jnp.int32),
            pltpu.SemaphoreType.DMA((4,)),
            pltpu.SemaphoreType.DMA((halves, 8)),
        ],
        compiler_params=pltpu.CompilerParams(vmem_limit_bytes=32 * MIB),
        name="send_order",
    )(*args)


def fill_turns(d, inner_ref, outer_ref):
    small = series(d * (1.0 / 256.0))
    table = [None, small]
    for j in range(2, AVG):
        table.append(times(table[j // 2], table[j - j // 2]))
    for j in range(1, AVG):
        inner_ref[j - 1, 0] = table[j][0]
        inner_ref[j - 1, 1] = table[j][1]
    c, s = turn_by(d)
    turn = (c * (1.0 / AVG), s * (1.0 / AVG))
    step = series(d * (1.0 / 32.0))
    for o in range(outer_ref.shape[0]):
        outer_ref[o, 0] = turn[0]
        outer_ref[o, 1] = turn[1]
        turn = times(turn, step)


def fetch_matrices(k_hbm, first, k_ref, sem):
    n_fetch = sem.shape[0]
    part = k_ref.shape[0] // n_fetch
    fetches = []
    for i in range(n_fetch):
        source = k_hbm.at[pl.ds(first + i * part, part)]
        fetches.append(pltpu.make_async_copy(source, k_ref.at[pl.ds(i * part, part)], sem.at[i]))
        fetches[-1].start()
    return fetches


def average_kernel(delay_ref, vis_ref, k_hbm, out_ref, k_ref, inner_ref, outer_ref, sem):
    fetches = fetch_matrices(k_hbm, 0, k_ref, sem)
    fill_turns(delay_ref[...], inner_ref, outer_ref)
    n_out, _, rows, _ = out_ref.shape
    for r in range(0, rows, 16):
        at = slice(r, r + 16)
        table = [(inner_ref[j, 0, at], inner_ref[j, 1, at]) for j in range(AVG - 1)]

        def one(o, carry, at=at, table=table):
            c = o * AVG
            re = vis_ref[c, 0, at].astype(jnp.float32)
            im = vis_ref[c, 1, at].astype(jnp.float32)
            for j in range(1, AVG):
                a = vis_ref[c + j, 0, at].astype(jnp.float32)
                b = vis_ref[c + j, 1, at].astype(jnp.float32)
                tc, ts = table[j - 1]
                re += a * tc - b * ts
                im += a * ts + b * tc
            tc = outer_ref[o, 0, at]
            ts = outer_ref[o, 1, at]
            out_ref[o, 0, at] = (re * tc - im * ts).astype(jnp.bfloat16)
            out_ref[o, 1, at] = (re * ts + im * tc).astype(jnp.bfloat16)
            return carry

        lax.fori_loop(0, n_out, one, 0, unroll=4)
    for fetch in fetches:
        fetch.wait()


def average(delay, vis, kernels):
    n_ch, halves, rows, bv = vis.shape
    n_out = n_ch // AVG
    n_planes, k_rows, cells = kernels.shape
    return pl.pallas_call(
        average_kernel,
        out_shape=[
            jax.ShapeDtypeStruct((n_out, halves, rows, bv), jnp.bfloat16),
            jax.ShapeDtypeStruct((n_planes // 2, k_rows, cells), kernels.dtype),
        ],
        in_specs=[vmem()] * 2 + [pl.BlockSpec(memory_space=pltpu.HBM)],
        out_specs=[vmem()] * 2,
        scratch_shapes=[
            pltpu.VMEM((AVG - 1, 2, rows, bv), jnp.float32),
            pltpu.VMEM((n_out, 2, rows, bv), jnp.float32),
            pltpu.SemaphoreType.DMA((4,)),
        ],
        compiler_params=pltpu.CompilerParams(vmem_limit_bytes=16 * MIB),
        name="average",
    )(delay, vis, pltpu.with_memory_space_constraint(kernels, pltpu.HBM))


def grid_kernel(n_pieces, *refs):
    piece_vmem, rows_ref, order_ref, tiles_ref, low_ref, k_hbm, out_ref, piece_ref, high_ref, x_ref, c_ref, sem, piece_sem = refs
    piece_copy = pltpu.make_async_copy(piece_vmem, piece_ref, piece_sem.at[0])
    piece_copy.start()
    fetches = fetch_matrices(k_hbm, low_ref.shape[0], high_ref, sem)
    n_src, _, per, bv = rows_ref.shape
    re = rows_ref[:, 0].reshape(n_src * per, bv)
    im = rows_ref[:, 1].reshape(n_src * per, bv)
    x = jnp.concatenate([re, im], axis=1)
    x_ref[...] = jnp.dot(order_ref[...], x, preferred_element_type=jnp.float32).astype(jnp.bfloat16)
    c_ref[...] = jnp.zeros_like(c_ref)
    piece_copy.wait()
    for lane, k_ref in ((0, low_ref), (64, high_ref)):
        if lane:
            for fetch in fetches:
                fetch.wait()
        for begin in range(0, n_pieces, STRETCH):

            @pl.when(begin < piece_ref[2, lane])
            def _(begin=begin, lane=lane, k_ref=k_ref):
                for i in range(lane + begin, lane + min(begin + STRETCH, n_pieces)):
                    at = pl.ds(pl.multiple_of(piece_ref[0, i] * GROUP, GROUP), PIECE)
                    product = jnp.dot(x_ref[at, :], k_ref[piece_ref[1, i]], preferred_element_type=jnp.float32)
                    c_ref[at, :] = product.astype(jnp.bfloat16)

    grid = jnp.dot(tiles_ref[...], c_ref[: tiles_ref.shape[1], :], preferred_element_type=jnp.float32)
    out_ref[...] = grid.astype(jnp.bfloat16).reshape(out_ref.shape)


def grid_rows(piece, rows, order, tiles, low, kernels):
    n_planes, k_rows, cells = kernels.shape
    n_order, n_rows = order.shape
    n_chan = rows.shape[0]
    n_pieces = n_rows // PIECE + n_planes // 2
    assert n_pieces <= 64
    return pl.pallas_call(
        functools.partial(grid_kernel, n_pieces),
        out_shape=jax.ShapeDtypeStruct((n_chan, tiles.shape[0] // n_chan, cells), jnp.bfloat16),
        in_specs=[vmem()] * 5 + [pl.BlockSpec(memory_space=pltpu.HBM)],
        out_specs=vmem(),
        scratch_shapes=[
            pltpu.SMEM(piece.shape, jnp.int32),
            pltpu.VMEM(low.shape, low.dtype),
            pltpu.VMEM((n_order, k_rows), jnp.bfloat16),
            pltpu.VMEM((n_order, cells), jnp.bfloat16),
            pltpu.SemaphoreType.DMA((4,)),
            pltpu.SemaphoreType.DMA((1,)),
        ],
        compiler_params=pltpu.CompilerParams(vmem_limit_bytes=24 * MIB),
        name="grid_rows",
    )(piece, rows, order, tiles, low, pltpu.with_memory_space_constraint(kernels, pltpu.HBM))


def strip_kernel(main_ref, out_ref):
    n_out, per, cells = main_ref.shape
    half = cells // 2
    low = main_ref[:, :, :128].reshape(n_out * per, 128).astype(jnp.float32)
    high = main_ref[:, :, half : half + 128].reshape(n_out * per, 128).astype(jnp.float32)
    lane = lax.broadcasted_iota(jnp.int32, low.shape, 1)
    strip = jnp.where(lane < STRIP, low, pltpu.roll(high, STRIP, 1)).astype(jnp.bfloat16)
    out_ref[...] = strip.reshape(out_ref.shape)


def strips_of(main):
    n_out, per, _ = main.shape
    return pl.pallas_call(
        strip_kernel,
        out_shape=jax.ShapeDtypeStruct((n_out, per, 2 * STRIP), jnp.bfloat16),
        in_specs=[vmem()],
        out_specs=vmem(),
        compiler_params=pltpu.CompilerParams(vmem_limit_bytes=8 * MIB),
        name="strips",
    )(main)


def placing(n_out, t_dev):
    n_rows = n_out * t_dev
    to = iota((n_rows, n_rows), 0)
    return (iota((n_rows, n_rows), 1) == (to % n_out) * t_dev + to // n_out).astype(jnp.float32)


def place_kernel(main_ref, out_hbm, rest_ref, done_ref, sem):
    n_out, per, cells = main_ref.shape
    t_dev = per // 2
    run = cells // 4
    place = placing(n_out, t_dev).astype(jnp.bfloat16)
    copies = []
    for slot in range(2):
        main = main_ref[:, slot * t_dev : (slot + 1) * t_dev, :].reshape(n_out * t_dev, cells)
        main = jnp.dot(place, main, preferred_element_type=jnp.float32)
        for i in range(2):
            at = slice(2 * i * run, (2 * i + 1) * run)
            done_ref[i, :, slot] = main[:, at].reshape(t_dev, n_out, run)
            rest_ref[i, :, slot] = main[:, at.stop : at.stop + run].reshape(t_dev, n_out, run)
    for i in range(2):
        copies.append(pltpu.make_async_copy(done_ref.at[i], out_hbm.at[:, :, :, pl.ds(2 * i * run, run)], sem.at[i]))
        copies[-1].start()
    for copy in copies:
        copy.wait()


def place_main(main):
    n_out, per, cells = main.shape
    part = (2, per // 2, 2, n_out, cells // 4)
    return pl.pallas_call(
        place_kernel,
        out_shape=[
            pltpu.HBM((per // 2, 2, n_out, cells), jnp.float32),
            jax.ShapeDtypeStruct(part, jnp.float32),
        ],
        in_specs=[vmem()],
        out_specs=[pl.BlockSpec(memory_space=pltpu.HBM), vmem()],
        scratch_shapes=[pltpu.VMEM(part, jnp.float32), pltpu.SemaphoreType.DMA((2,))],
        compiler_params=pltpu.CompilerParams(vmem_limit_bytes=8 * MIB),
        name="place",
    )(main)


def join_kernel(nb_ref, placed_hbm, rest_ref, *refs):
    strips, (out_hbm, strip_ref, done_ref, sem) = refs[:-4], refs[-4:]
    _, t_dev, _, n_out, run = rest_ref.shape
    n_rows = n_out * t_dev
    for i, ref in enumerate(strips):
        strip_ref[i] = ref[...].reshape(strip_ref.shape[1:])
    upper = iota((n_rows, 2 * STRIP), 1) >= STRIP
    quarter = (0.25 * placing(n_out, t_dev)).astype(jnp.bfloat16)
    n_nb = nb_ref.shape[1] // 2
    copies = []
    for slot in range(2):
        blend = jnp.zeros((n_rows, 2 * STRIP), jnp.float32)
        for k in range(n_nb):
            strip = strip_ref[nb_ref[slot, k], :, nb_ref[slot, n_nb + k]].reshape(n_rows, 2 * STRIP)
            blend += jnp.dot(quarter, strip, preferred_element_type=jnp.float32)
        for i, part in enumerate((pltpu.roll(blend, STRIP, 1), blend)):
            part = jnp.where(upper, part, 0.0).reshape(t_dev, n_out, run)
            done_ref[i, :, slot] = rest_ref[i, :, slot] + part
            target = out_hbm.at[:, slot, :, pl.ds((2 * i + 1) * run, run)]
            copies.append(pltpu.make_async_copy(done_ref.at[i, :, slot], target, sem.at[slot, i]))
            copies[-1].start()
    for copy in copies:
        copy.wait()


def join(sources, placed, rest, strips):
    _, t_dev, _, n_out, run = rest.shape
    assert run == 2 * STRIP
    return pl.pallas_call(
        join_kernel,
        out_shape=pltpu.HBM(placed.shape, placed.dtype),
        in_specs=[pl.BlockSpec(memory_space=pltpu.SMEM), pl.BlockSpec(memory_space=pltpu.HBM)]
        + [vmem()] * (1 + len(strips)),
        out_specs=pl.BlockSpec(memory_space=pltpu.HBM),
        scratch_shapes=[
            pltpu.VMEM((len(strips), n_out, 2, t_dev, 2 * STRIP), jnp.bfloat16),
            pltpu.VMEM(rest.shape, jnp.float32),
            pltpu.SemaphoreType.DMA((2, 2)),
        ],
        input_output_aliases={1: 0},
        compiler_params=pltpu.CompilerParams(vmem_limit_bytes=16 * MIB),
        name="join",
    )(sources, placed, rest, *strips)


def exchange(x, axis):
    return lax.all_to_all(x, axis, split_axis=0, concat_axis=0, tiled=True)


def local(visibilities, kernels, delays, tile_of, plane_of, counts, neighbours):
    n_facet = lax.axis_size("facet")
    n_chan = lax.axis_size("chan")
    facet_index = lax.axis_index("facet")
    halves, facets, blocks, _, bv = visibilities.shape
    fac_dev = facets // n_facet
    n_tiles = 16 * n_chan
    t_dev = n_tiles // n_chan
    n_rows = fac_dev * blocks
    per = n_rows // n_chan

    vis = visibilities.reshape(halves, n_facet * n_chan, per, bv)
    vis, delay, order, tiles, piece = send_order(
        counts,
        plane_of,
        tile_of,
        delays.reshape(n_chan, per, bv),
        vis,
        kernels.shape[0],
        fac_dev * n_tiles,
        t_dev,
    )
    vis = exchange(vis, ("facet", "chan"))

    rows, low = average(delay, vis, kernels)
    rows = exchange(rows, "chan")
    main = exchange(grid_rows(piece, rows, order, tiles, low, kernels), "chan")

    own = strips_of(main)
    chips = n_facet // 2
    strips = [own]
    for dz in range(1, chips):
        strips.append(lax.ppermute(own, "facet", [(f, (f + 2 * dz) % n_facet) for f in range(n_facet)]))
    strips += [lax.ppermute(s, "facet", [(f, f ^ 1) for f in range(n_facet)]) for s in strips]
    mine = lax.dynamic_slice_in_dim(neighbours, facet_index * fac_dev, fac_dev, 0)
    group = mine // fac_dev
    source = (facet_index // 2 - group // 2) % chips + chips * ((group + facet_index) % 2)
    sources = jnp.concatenate([source, mine % fac_dev], axis=1).astype(jnp.int32)
    placed, rest = place_main(main)
    return join(sources, placed, rest, strips)


def solution(mesh):
    return jax.shard_map(
        local,
        mesh=mesh,
        in_specs=(
            P(None, None, None, ("facet", "chan"), None),
            P(),
            P("facet", None, None),
            P("facet", None),
            P("facet", None),
            P("facet"),
            P(),
        ),
        out_specs=P("chan", "facet", None, None),
        check_vma=False,
    )
```

time: 121 us -> 117 us (0.967)
  local copies, waits for them, and re-layouts: 2.21 us -> 0.17 us
    pallas_call x3 -> x4, Pallas kernels: 12.7 us -> 10.5 us  [the longest x1 5.03 us: grid_rows(): pl.pallas_call(functools.partial(grid_kernel, n_pieces), out_shape=jax.Sh...]
    unnamed x9 -> x3, local copies, waits for them, and re-layouts: 2.14 us -> 0.1 us
    pallas_call x1, Pallas kernels: 3.13 us -> 4.7 us  [send_order(): pl.pallas_call(functools.partial(send_kernel, n_planes, n_order, t_dev),...]
  transfers between devices with their start and end apart: 7 -> 7, of which waited for: 1 -> 0; matrix products, arithmetic and copies ran while one was open for 0% -> 0% of each run, Pallas kernels for 0% -> 1%
where the time goes in v7:
time: 117 us
  blocking collectives  89.1 us (76%)
  Pallas kernels  15.3 us (13%)
  starting transfers between devices  12.3 us (11%)
    all_to_all x3, blocking collectives, exchange(): return lax.all_to_all(x, axis, split_axis=0, concat_axis=0, tiled=True)  89.1 us
    ppermute x4, starting transfers between devices, local(): lax.ppermute(s, 'facet', [(f, f ^ 1) for f in range(n_facet)])  9.64 us
    pallas_call x1, Pallas kernels, grid_rows(): pl.pallas_call(functools.partial(grid_kernel, n_pieces), out_shape=jax.Sh...  5.03 us
    pallas_call x1, Pallas kernels, send_order(): pl.pallas_call(functools.partial(send_kernel, n_planes, n_order, t_dev),...  4.7 us
    ppermute x3, starting transfers between devices, local(): lax.ppermute(own, 'facet', [(f, (f + 2 * dz) % n_facet) for f in range(n_...  2.68 us
  transfers between devices with their start and end apart: 7, of which 0 were waited for; matrix products, arithmetic and copies ran while one was open for 0% of the time, Pallas kernels for 1%

profile of v7, /device:TPU:1, one launch (start us, length us, event | category | flops | bytes accessed | tf_op | source)
XLA Modules:
  0.0 117.1 jit_solution(920742074499058019)
XLA Ops:
  0.0 0.0 copy-start
  0.0 4.7 %send_order.1 = (bf16[128,2,64,128]{3,2,1,0:T(8,128)(2,1)S(1)}, f32[64,128]{1,0:T(8,128)S(1)}, bf16[1568,1024]{1,0:T(8,128)(2,1)S(1)}, bf16[512,1536]{1,0:T(8,128)(2,1)S(1)}, s32[8,128]{1,0:T(8,128)S(1)}) custom-call(s32[2]{0:T(128)} %refs_0_.1, s32[2,512]{1,0:T(2,128)} %refs_1_.1, s32[2,512]{1,0:T(2,128)} %refs_2_.1, f32[16,64,128]{2,1,0:T(8,128)} %bitcast.3, ...), custom_call_target="tpu_custom_call" | custom-call | tf_op jit(solution)/shard_map/send_order/pallas_call | solution.py:159
  4.7 64.0 %all_to_all.15.vis_ref = bf16[128,2,64,128]{3,2,1,0:T(8,128)(2,1)S(1)} all-to-all(bf16[128,2,64,128]{3,2,1,0:T(8,128)(2,1)S(1)} %get-tuple-element.16), channel_id=1, replica_groups=mesh['facet'=8,'chan'=16] {'facet','chan'}, dimensions={0} | all-to-all | bytes 8388608 | tf_op jit(solution)/shard_map/all_to_all | solution.py:425
  68.7 2.2 %average.1 = (bf16[16,2,64,128]{3,2,1,0:T(8,128)(2,1)S(1)}, bf16[16,256,512]{2,1,0:T(8,128)(2,1)S(1)}) custom-call(f32[64,128]{1,0:T(8,128)S(1)} %get-tuple-element.15.delay_ref, bf16[128,2,64,128]{3,2,1,0:T(8,128)(2,1)S(1)} %all_to_all.15.vis_ref, bf16[32,256,512]{2,1,0:T(8,128)(2,1)} %refs_5_.1), custom_call_target="tpu_custom_call" | custom-call | tf_op jit(solution)/shard_map/average/pallas_call | solution.py:243
  70.9 11.9 %all_to_all.16.refs_1_ = bf16[16,2,64,128]{3,2,1,0:T(8,128)(2,1)S(1)} all-to-all(bf16[16,2,64,128]{3,2,1,0:T(8,128)(2,1)S(1)} %get-tuple-element.17), channel_id=1, replica_groups=mesh['facet'=8,'chan'=16] {'chan'}, dimensions={0} | all-to-all | bytes 1048576 | tf_op jit(solution)/shard_map/all_to_all | solution.py:425
  82.8 5.0 %grid_rows.1 = bf16[16,32,512]{2,1,0:T(8,128)(2,1)S(1)} custom-call(s32[8,128]{1,0:T(8,128)S(1)} %get-tuple-element.14.refs_0_, bf16[16,2,64,128]{3,2,1,0:T(8,128)(2,1)S(1)} %all_to_all.16.refs_1_, bf16[1568,1024]{1,0:T(8,128)(2,1)S(1)} %get-tuple-element.18.refs_2_, bf16[512,1536]{1,0:T(8,128)(2,1)S(1)} %get-tuple-element.19.refs_3_, ...), custom_call_target="tpu_custom_call" | custom-call | tf_op jit(solution)/shard_map/grid_rows/pallas_call | solution.py:296
  87.8 13.2 %all_to_all.17.main_ref = bf16[16,32,512]{2,1,0:T(8,128)(2,1)S(1)} all-to-all(bf16[16,32,512]{2,1,0:T(8,128)(2,1)S(1)} %grid_rows.1), channel_id=1, replica_groups=mesh['facet'=8,'chan'=16] {'chan'}, dimensions={0} | all-to-all | bytes 1048576 | tf_op jit(solution)/shard_map/all_to_all | solution.py:425
  101.0 0.1 strips.1.refs_0_
  101.1 0.5 collective-permute-start.2
  101.6 2.1 %collective-permute-start.1 = (bf16[16,32,128]{2,1,0:T(8,128)(2,1)S(1)}, bf16[16,32,128]{2,1,0:T(8,128)(2,1)S(1)}, u32[]{:S(2)}, u32[]{:S(2)}) collective-permute-start(bf16[16,32,128]{2,1,0:T(8,128)(2,1)S(1)} %strips.1.refs_0_), channel_id=1, source_target_pairs={{0,64},{16,80},{32,96},{48,112},{64,0},{80,16},{96,32},{112,48},{1... | collective-permute-start | bytes 393224 | tf_op jit(solution)/shard_map/ppermute | solution.py:460
  103.7 0.2 collective-permute-start
  103.8 0.0 copy-done
  103.8 0.1 constant_dynamic-slice_fusion
  103.9 0.1 copy.10
  104.0 4.0 %collective-permute-start.3 = (bf16[16,32,128]{2,1,0:T(8,128)(2,1)S(1)}, bf16[16,32,128]{2,1,0:T(8,128)(2,1)S(1)}, u32[]{:S(2)}, u32[]{:S(2)}) collective-permute-start(bf16[16,32,128]{2,1,0:T(8,128)(2,1)S(1)} %strips.1.refs_0_), channel_id=1, source_target_pairs={{0,16},{16,0},{32,48},{48,32},{64,80},{80,64},{96,112},{112,96},{1... | collective-permute-start | bytes 393224 | tf_op jit(solution)/shard_map/ppermute | solution.py:461
  108.0 0.0 collective-permute-done.2.refs_3_
  108.0 1.8 %collective-permute-start.6 = (bf16[16,32,128]{2,1,0:T(8,128)(2,1)S(1)}, bf16[16,32,128]{2,1,0:T(8,128)(2,1)S(1)}, u32[]{:S(2)}, u32[]{:S(2)}) collective-permute-start(bf16[16,32,128]{2,1,0:T(8,128)(2,1)S(1)} %collective-permute-done.2.refs_3_), channel_id=1, source_target_pairs={{0,16},{16,0},{32,48},{48,32},{64,80},{80,64},{96,112},{112,96},{1... | collective-permute-start | bytes 393224 | tf_op jit(solution)/shard_map/ppermute | solution.py:461
  109.8 0.0 collective-permute-done.1.refs_2_
  109.8 2.1 %collective-permute-start.5 = (bf16[16,32,128]{2,1,0:T(8,128)(2,1)S(1)}, bf16[16,32,128]{2,1,0:T(8,128)(2,1)S(1)}, u32[]{:S(2)}, u32[]{:S(2)}) collective-permute-start(bf16[16,32,128]{2,1,0:T(8,128)(2,1)S(1)} %collective-permute-done.1.refs_2_), channel_id=1, source_target_pairs={{0,16},{16,0},{32,48},{48,32},{64,80},{80,64},{96,112},{112,96},{1... | collective-permute-start | bytes 393224 | tf_op jit(solution)/shard_map/ppermute | solution.py:461
  111.9 0.0 collective-permute-done.refs_1_
  111.9 1.7 %collective-permute-start.4 = (bf16[16,32,128]{2,1,0:T(8,128)(2,1)S(1)}, bf16[16,32,128]{2,1,0:T(8,128)(2,1)S(1)}, u32[]{:S(2)}, u32[]{:S(2)}) collective-permute-start(bf16[16,32,128]{2,1,0:T(8,128)(2,1)S(1)} %collective-permute-done.refs_1_), channel_id=1, source_target_pairs={{0,16},{16,0},{32,48},{48,32},{64,80},{80,64},{96,112},{112,96},{1... | collective-permute-start | bytes 393224 | tf_op jit(solution)/shard_map/ppermute | solution.py:461
  113.7 0.1 pad_add_fusion.nb_ref
  113.7 1.1 place.1
  114.9 0.0 collective-permute-done.3.refs_4_
  114.9 0.0 collective-permute-done.6.refs_7_
  114.9 0.0 collective-permute-done.5.refs_6_
  114.9 0.0 collective-permute-done.4.refs_5_
  114.9 2.2 %join.1 = f32[16,2,16,512]{3,2,1,0:T(8,128)} custom-call(s32[2,8]{1,0:T(2,128)S(1)} %pad_add_fusion.nb_ref, f32[16,2,16,512]{3,2,1,0:T(8,128)} %get-tuple-element.21.placed_hbm, f32[2,16,2,16,128]{4,3,2,1,0:T(8,128)S(1)} %get-tuple-element.22.rest_ref, bf16[16,32,128]{2,1,0:T(8,128)(2,1)S(1)} %strips.1.refs_0_, ...), custom_call_target="tpu_custom_call", output_to_operand_aliasing={{}: (1, {})} | custom-call | tf_op jit(solution)/shard_map/join/pallas_call | solution.py:407
  (1 shorter events, 0.0 us)
Async XLA Ops:
  0.0 103.8 %copy-start = (s32[16,4]{0,1:T(4,128)S(1)}, s32[16,4]{0,1:T(4,128)}, u32[]{:S(2)}) copy-start(s32[16,4]{0,1:T(4,128)} %param.13) | copy-start | bytes 772
  101.1 6.9 %collective-permute-start.2 = (bf16[16,32,128]{2,1,0:T(8,128)(2,1)S(1)}, bf16[16,32,128]{2,1,0:T(8,128)(2,1)S(1)}, u32[]{:S(2)}, u32[]{:S(2)}) collective-permute-start(bf16[16,32,128]{2,1,0:T(8,128)(2,1)S(1)} %strips.1.refs_0_), channel_id=1, source_target_pairs={{0,96},{16,112},{32,0},{48,16},{64,32},{80,48},{96,64},{112,80},{1... | collective-permute-start | bytes 393224 | tf_op jit(solution)/shard_map/ppermute | solution.py:460
  101.6 8.2 %collective-permute-start.1 = (bf16[16,32,128]{2,1,0:T(8,128)(2,1)S(1)}, bf16[16,32,128]{2,1,0:T(8,128)(2,1)S(1)}, u32[]{:S(2)}, u32[]{:S(2)}) collective-permute-start(bf16[16,32,128]{2,1,0:T(8,128)(2,1)S(1)} %strips.1.refs_0_), channel_id=1, source_target_pairs={{0,64},{16,80},{32,96},{48,112},{64,0},{80,16},{96,32},{112,48},{1... | collective-permute-start | bytes 393224 | tf_op jit(solution)/shard_map/ppermute | solution.py:460
  103.7 8.3 %collective-permute-start = (bf16[16,32,128]{2,1,0:T(8,128)(2,1)S(1)}, bf16[16,32,128]{2,1,0:T(8,128)(2,1)S(1)}, u32[]{:S(2)}, u32[]{:S(2)}) collective-permute-start(bf16[16,32,128]{2,1,0:T(8,128)(2,1)S(1)} %strips.1.refs_0_), channel_id=1, source_target_pairs={{0,32},{16,48},{32,64},{48,80},{64,96},{80,112},{96,0},{112,16},{1... | collective-permute-start | bytes 393224 | tf_op jit(solution)/shard_map/ppermute | solution.py:460
  104.0 10.9 %collective-permute-start.3 = (bf16[16,32,128]{2,1,0:T(8,128)(2,1)S(1)}, bf16[16,32,128]{2,1,0:T(8,128)(2,1)S(1)}, u32[]{:S(2)}, u32[]{:S(2)}) collective-permute-start(bf16[16,32,128]{2,1,0:T(8,128)(2,1)S(1)} %strips.1.refs_0_), channel_id=1, source_target_pairs={{0,16},{16,0},{32,48},{48,32},{64,80},{80,64},{96,112},{112,96},{1... | collective-permute-start | bytes 393224 | tf_op jit(solution)/shard_map/ppermute | solution.py:461
  108.0 6.8 %collective-permute-start.6 = (bf16[16,32,128]{2,1,0:T(8,128)(2,1)S(1)}, bf16[16,32,128]{2,1,0:T(8,128)(2,1)S(1)}, u32[]{:S(2)}, u32[]{:S(2)}) collective-permute-start(bf16[16,32,128]{2,1,0:T(8,128)(2,1)S(1)} %collective-permute-done.2.refs_3_), channel_id=1, source_target_pairs={{0,16},{16,0},{32,48},{48,32},{64,80},{80,64},{96,112},{112,96},{1... | collective-permute-start | bytes 393224 | tf_op jit(solution)/shard_map/ppermute | solution.py:461
  109.8 5.1 %collective-permute-start.5 = (bf16[16,32,128]{2,1,0:T(8,128)(2,1)S(1)}, bf16[16,32,128]{2,1,0:T(8,128)(2,1)S(1)}, u32[]{:S(2)}, u32[]{:S(2)}) collective-permute-start(bf16[16,32,128]{2,1,0:T(8,128)(2,1)S(1)} %collective-permute-done.1.refs_2_), channel_id=1, source_target_pairs={{0,16},{16,0},{32,48},{48,32},{64,80},{80,64},{96,112},{112,96},{1... | collective-permute-start | bytes 393224 | tf_op jit(solution)/shard_map/ppermute | solution.py:461
  111.9 3.0 %collective-permute-start.4 = (bf16[16,32,128]{2,1,0:T(8,128)(2,1)S(1)}, bf16[16,32,128]{2,1,0:T(8,128)(2,1)S(1)}, u32[]{:S(2)}, u32[]{:S(2)}) collective-permute-start(bf16[16,32,128]{2,1,0:T(8,128)(2,1)S(1)} %collective-permute-done.refs_1_), channel_id=1, source_target_pairs={{0,16},{16,0},{32,48},{48,32},{64,80},{80,64},{96,112},{112,96},{1... | collective-permute-start | bytes 393224 | tf_op jit(solution)/shard_map/ppermute | solution.py:461

commit v8 on v7

--- a/solution.py
+++ b/solution.py
@@ -57,7 +57,7 @@
     return lax.broadcasted_iota(jnp.int32, shape, dim)
 
 
-def fill_tables(n_planes, n_order, t_dev, count_ref, plane_ref, tile_ref, order_ref, tiles_ref, piece_ref):
+def fill_tables(n_planes, t_dev, count_ref, plane_ref, tile_ref, place_ref, code_ref, piece_ref):
     f32 = jnp.float32
     slots, blocks = plane_ref.shape
     n_rows = slots * blocks
@@ -84,21 +84,20 @@
     place = jnp.sum(jnp.where(mine, rank + GROUP * first_group, 0.0), axis=0, keepdims=True)
     live = jnp.sum(mine.astype(f32), axis=0, keepdims=True)
     place = jnp.where(live > 0.5, place, -1.0).astype(jnp.int32)
-    order = to_bf16(iota((n_order, n_rows), 0) == place)
-    order_ref[...] = order
+    place_ref[...] = place
+    n_used = code_ref.shape[1]
+    order = to_bf16(iota((n_used, n_rows), 0) == place)
 
     row = iota((8, n_rows), 0)
     slot = (iota((8, n_rows), 1) >= n_rows // 2).astype(f32)
     values = jnp.where(row == 0, tile.astype(f32) + 1.0, jnp.where(row == 1, slot, 0.0))
-    n_codes, n_used = tiles_ref.shape
     ordered = lax.dot_general(
-        values.astype(jnp.bfloat16), order[:n_used], (((1,), (1,)), ((), ())), preferred_element_type=f32
+        values.astype(jnp.bfloat16), order, (((1,), (1,)), ((), ())), preferred_element_type=f32
     )
     tile = ordered[0:1].astype(jnp.int32) - 1
     slot = ordered[1:2].astype(jnp.int32)
     code = (tile // t_dev) * (2 * t_dev) + slot * t_dev + tile % t_dev
-    code = jnp.where(tile < 0, -1, code)
-    tiles_ref[...] = to_bf16(iota((n_codes, n_used), 0) == code)
+    code_ref[...] = jnp.where(tile < 0, -1, code)
 
     lower = jnp.sum(jnp.where(iota((n_planes, 1), 0) < n_planes // 2, pieces, 0.0))
     upper = jnp.sum(pieces) - lower
@@ -125,7 +124,7 @@
     return n_order, n_used
 
 
-def send_kernel(n_planes, n_order, t_dev, *refs):
+def send_kernel(n_planes, t_dev, *refs):
     (count_hbm, plane_hbm, tile_hbm, delay_hbm, vis_hbm), refs = refs[:5], refs[5:]
     (out_ref, delay_ref, *tables), (count_ref, plane_ref, tile_ref, small_sem, sem) = refs[:-5], refs[-5:]
     smalls = [
@@ -146,23 +145,23 @@
             copies[-1].start()
     for copy in smalls:
         copy.wait()
-    fill_tables(n_planes, n_order, t_dev, count_ref, plane_ref, tile_ref, *tables)
+    fill_tables(n_planes, t_dev, count_ref, plane_ref, tile_ref, *tables)
     for copy in copies:
         copy.wait()
 
 
-def send_order(counts, planes, tiles, delays, vis, n_planes, n_codes, t_dev):
+def send_order(counts, planes, tiles, delays, vis, n_planes, t_dev):
     halves, dests, rows, bv = vis.shape
     n_rows = planes.shape[0] * planes.shape[1]
     n_order, n_used = sizes(n_rows, n_planes)
     args = [pltpu.with_memory_space_constraint(x, pltpu.HBM) for x in (counts, planes, tiles, delays, vis)]
     return pl.pallas_call(
-        functools.partial(send_kernel, n_planes, n_order, t_dev),
+        functools.partial(send_kernel, n_planes, t_dev),
         out_shape=[
             jax.ShapeDtypeStruct((dests, halves, rows, bv), vis.dtype),
             jax.ShapeDtypeStruct(delays.shape[1:], delays.dtype),
-            jax.ShapeDtypeStruct((n_order, n_rows), jnp.bfloat16),
-            jax.ShapeDtypeStruct((n_codes, n_used), jnp.bfloat16),
+            jax.ShapeDtypeStruct((1, n_rows), jnp.int32),
+            jax.ShapeDtypeStruct((1, n_used), jnp.int32),
             jax.ShapeDtypeStruct((8, 128), jnp.int32),
         ],
         in_specs=[pl.BlockSpec(memory_space=pltpu.HBM)] * len(args),
@@ -259,7 +258,7 @@
 
 
 def grid_kernel(n_pieces, *refs):
-    piece_vmem, rows_ref, order_ref, tiles_ref, low_ref, k_hbm, out_ref, piece_ref, high_ref, x_ref, c_ref, sem, piece_sem = refs
+    piece_vmem, rows_ref, place_ref, code_ref, low_ref, k_hbm, out_ref, piece_ref, high_ref, x_ref, c_ref, sem, piece_sem = refs
     piece_copy = pltpu.make_async_copy(piece_vmem, piece_ref, piece_sem.at[0])
     piece_copy.start()
     fetches = fetch_matrices(k_hbm, low_ref.shape[0], high_ref, sem)
@@ -267,7 +266,8 @@
     re = rows_ref[:, 0].reshape(n_src * per, bv)
     im = rows_ref[:, 1].reshape(n_src * per, bv)
     x = jnp.concatenate([re, im], axis=1)
-    x_ref[...] = jnp.dot(order_ref[...], x, preferred_element_type=jnp.float32).astype(jnp.bfloat16)
+    order = to_bf16(iota((x_ref.shape[0], n_src * per), 0) == place_ref[...])
+    x_ref[...] = jnp.dot(order, x, preferred_element_type=jnp.float32).astype(jnp.bfloat16)
     c_ref[...] = jnp.zeros_like(c_ref)
     piece_copy.wait()
     for lane, k_ref in ((0, low_ref), (64, high_ref)):
@@ -283,19 +283,22 @@
                     product = jnp.dot(x_ref[at, :], k_ref[piece_ref[1, i]], preferred_element_type=jnp.float32)
                     c_ref[at, :] = product.astype(jnp.bfloat16)
 
-    grid = jnp.dot(tiles_ref[...], c_ref[: tiles_ref.shape[1], :], preferred_element_type=jnp.float32)
+    n_used = code_ref.shape[1]
+    tiles = to_bf16(iota((out_ref.shape[0] * out_ref.shape[1], n_used), 0) == code_ref[...])
+    grid = jnp.dot(tiles, c_ref[:n_used, :], preferred_element_type=jnp.float32)
     out_ref[...] = grid.astype(jnp.bfloat16).reshape(out_ref.shape)
 
 
-def grid_rows(piece, rows, order, tiles, low, kernels):
+def grid_rows(piece, rows, place, code, low, kernels, n_codes):
     n_planes, k_rows, cells = kernels.shape
-    n_order, n_rows = order.shape
+    n_rows = place.shape[1]
+    n_order, _ = sizes(n_rows, n_planes)
     n_chan = rows.shape[0]
     n_pieces = n_rows // PIECE + n_planes // 2
     assert n_pieces <= 64
     return pl.pallas_call(
         functools.partial(grid_kernel, n_pieces),
-        out_shape=jax.ShapeDtypeStruct((n_chan, tiles.shape[0] // n_chan, cells), jnp.bfloat16),
+        out_shape=jax.ShapeDtypeStruct((n_chan, n_codes // n_chan, cells), jnp.bfloat16),
         in_specs=[vmem()] * 5 + [pl.BlockSpec(memory_space=pltpu.HBM)],
         out_specs=vmem(),
         scratch_shapes=[
@@ -308,7 +311,7 @@
         ],
         compiler_params=pltpu.CompilerParams(vmem_limit_bytes=24 * MIB),
         name="grid_rows",
-    )(piece, rows, order, tiles, low, pltpu.with_memory_space_constraint(kernels, pltpu.HBM))
+    )(piece, rows, place, code, low, pltpu.with_memory_space_constraint(kernels, pltpu.HBM))
 
 
 def strip_kernel(main_ref, out_ref):
@@ -372,12 +375,15 @@
         out_specs=[pl.BlockSpec(memory_space=pltpu.HBM), vmem()],
         scratch_shapes=[pltpu.VMEM(part, jnp.float32), pltpu.SemaphoreType.DMA((2,))],
         compiler_params=pltpu.CompilerParams(vmem_limit_bytes=8 * MIB),
+        cost_estimate=pl.CostEstimate(flops=2 * n_out * per * n_out * per // 2 * cells, transcendentals=0, bytes_accessed=3 * MIB // 2),
         name="place",
     )(main)
 
 
-def join_kernel(nb_ref, placed_hbm, rest_ref, *refs):
-    strips, (out_hbm, strip_ref, done_ref, sem) = refs[:-4], refs[-4:]
+def join_kernel(nb_vmem, placed_hbm, rest_ref, *refs):
+    strips, (out_hbm, nb_ref, strip_ref, done_ref, sem, nb_sem) = refs[:-6], refs[-6:]
+    nb_copy = pltpu.make_async_copy(nb_vmem, nb_ref, nb_sem.at[0])
+    nb_copy.start()
     _, t_dev, _, n_out, run = rest_ref.shape
     n_rows = n_out * t_dev
     for i, ref in enumerate(strips):
@@ -385,6 +391,7 @@
     upper = iota((n_rows, 2 * STRIP), 1) >= STRIP
     quarter = (0.25 * placing(n_out, t_dev)).astype(jnp.bfloat16)
     n_nb = nb_ref.shape[1] // 2
+    nb_copy.wait()
     copies = []
     for slot in range(2):
         blend = jnp.zeros((n_rows, 2 * STRIP), jnp.float32)
@@ -407,13 +414,14 @@
     return pl.pallas_call(
         join_kernel,
         out_shape=pltpu.HBM(placed.shape, placed.dtype),
-        in_specs=[pl.BlockSpec(memory_space=pltpu.SMEM), pl.BlockSpec(memory_space=pltpu.HBM)]
-        + [vmem()] * (1 + len(strips)),
+        in_specs=[vmem(), pl.BlockSpec(memory_space=pltpu.HBM)] + [vmem()] * (1 + len(strips)),
         out_specs=pl.BlockSpec(memory_space=pltpu.HBM),
         scratch_shapes=[
+            pltpu.SMEM(sources.shape, jnp.int32),
             pltpu.VMEM((len(strips), n_out, 2, t_dev, 2 * STRIP), jnp.bfloat16),
             pltpu.VMEM(rest.shape, jnp.float32),
             pltpu.SemaphoreType.DMA((2, 2)),
+            pltpu.SemaphoreType.DMA((1,)),
         ],
         input_output_aliases={1: 0},
         compiler_params=pltpu.CompilerParams(vmem_limit_bytes=16 * MIB),
@@ -437,33 +445,29 @@
     per = n_rows // n_chan
 
     vis = visibilities.reshape(halves, n_facet * n_chan, per, bv)
-    vis, delay, order, tiles, piece = send_order(
-        counts,
-        plane_of,
-        tile_of,
-        delays.reshape(n_chan, per, bv),
-        vis,
-        kernels.shape[0],
-        fac_dev * n_tiles,
-        t_dev,
+    vis, delay, place, code, piece = send_order(
+        counts, plane_of, tile_of, delays.reshape(n_chan, per, bv), vis, kernels.shape[0], t_dev
     )
     vis = exchange(vis, ("facet", "chan"))
 
     rows, low = average(delay, vis, kernels)
     rows = exchange(rows, "chan")
-    main = exchange(grid_rows(piece, rows, order, tiles, low, kernels), "chan")
+    main = exchange(grid_rows(piece, rows, place, code, low, kernels, fac_dev * n_tiles), "chan")
 
     own = strips_of(main)
     chips = n_facet // 2
-    strips = [own]
-    for dz in range(1, chips):
-        strips.append(lax.ppermute(own, "facet", [(f, (f + 2 * dz) % n_facet) for f in range(n_facet)]))
-    strips += [lax.ppermute(s, "facet", [(f, f ^ 1) for f in range(n_facet)]) for s in strips]
+    along = lambda x, dz: lax.ppermute(x, "facet", [(f, (f + 2 * dz) % n_facet) for f in range(n_facet)])
+    across = lambda x: lax.ppermute(x, "facet", [(f, f ^ 1) for f in range(n_facet)])
+    arrived = {dz: along(own, dz) for dz in range(1, chips - 1)}
+    placed, rest = place_main(main)
+    own, rest = lax.optimization_barrier((own, rest))
+    arrived[chips - 1] = along(own, chips - 1)
+    strips = [own] + [arrived[dz] for dz in range(1, chips)]
+    strips += [across(s) for s in strips]
     mine = lax.dynamic_slice_in_dim(neighbours, facet_index * fac_dev, fac_dev, 0)
     group = mine // fac_dev
     source = (facet_index // 2 - group // 2) % chips + chips * ((group + facet_index) % 2)
     sources = jnp.concatenate([source, mine % fac_dev], axis=1).astype(jnp.int32)
-    placed, rest = place_main(main)
     return join(sources, placed, rest, strips)
 
 

time: 117 us -> 115 us (0.983)
  Pallas kernels: 15.3 us -> 14 us
  starting transfers between devices: 12.3 us -> 11 us
    ppermute x7, starting transfers between devices: 12.3 us -> 11 us  [the longest x4 6.38 us: local(): lax.ppermute(x, 'facet', [(f, f ^ 1) for f in range(n_facet)])]
  transfers between devices with their start and end apart: 7 -> 7, of which waited for: 0 -> 2; matrix products, arithmetic and copies ran while one was open for 0% -> 0% of each run, Pallas kernels for 1% -> 1%
where the time goes in v8:
time: 115 us
  blocking collectives  89.1 us (77%)
  Pallas kernels  14 us (12%)
  starting transfers between devices  11 us (10%)
    all_to_all x3, blocking collectives, exchange(): return lax.all_to_all(x, axis, split_axis=0, concat_axis=0, tiled=True)  89.1 us
    ppermute x4, starting transfers between devices, local(): lax.ppermute(x, 'facet', [(f, f ^ 1) for f in range(n_facet)])  6.38 us
    pallas_call x1, Pallas kernels, grid_rows(): pl.pallas_call(functools.partial(grid_kernel, n_pieces), out_shape=jax.Sh...  5.01 us
    ppermute x3, starting transfers between devices, local(): lax.ppermute(x, 'facet', [(f, (f + 2 * dz) % n_facet) for f in range(n_fa...  4.58 us
    pallas_call x1, Pallas kernels, send_order(): pl.pallas_call(functools.partial(send_kernel, n_planes, t_dev), out_shape...  3.57 us
  transfers between devices with their start and end apart: 7, of which 2 were waited for; matrix products, arithmetic and copies ran while one was open for 0% of the time, Pallas kernels for 1%

profile of v8, /device:TPU:1, one launch (start us, length us, event | category | flops | bytes accessed | tf_op | source)
XLA Modules:
  0.0 115.2 jit_solution(15113040311244070227)
XLA Ops:
  0.0 0.0 copy-start
  0.0 3.6 %send_order.1 = (bf16[128,2,64,128]{3,2,1,0:T(8,128)(2,1)S(1)}, f32[64,128]{1,0:T(8,128)S(1)}, s32[1,1024]{1,0:T(1,128)S(1)}, s32[1,1536]{1,0:T(1,128)S(1)}, s32[8,128]{1,0:T(8,128)S(1)}) custom-call(s32[2]{0:T(128)} %refs_0_.1, s32[2,512]{1,0:T(2,128)} %refs_1_.1, s32[2,512]{1,0:T(2,128)} %refs_2_.1, f32[16,64,128]{2,1,0:T(8,128)} %bitcast.3, ...), custom_call_target="tpu_custom_call" | custom-call | tf_op jit(solution)/shard_map/send_order/pallas_call | solution.py:158
  3.6 64.0 %all_to_all.15.vis_ref = bf16[128,2,64,128]{3,2,1,0:T(8,128)(2,1)S(1)} all-to-all(bf16[128,2,64,128]{3,2,1,0:T(8,128)(2,1)S(1)} %get-tuple-element.18), channel_id=1, replica_groups=mesh['facet'=8,'chan'=16] {'facet','chan'}, dimensions={0} | all-to-all | bytes 8388608 | tf_op jit(solution)/shard_map/all_to_all | solution.py:433
  67.5 2.2 %average.1 = (bf16[16,2,64,128]{3,2,1,0:T(8,128)(2,1)S(1)}, bf16[16,256,512]{2,1,0:T(8,128)(2,1)S(1)}) custom-call(f32[64,128]{1,0:T(8,128)S(1)} %get-tuple-element.17.delay_ref, bf16[128,2,64,128]{3,2,1,0:T(8,128)(2,1)S(1)} %all_to_all.15.vis_ref, bf16[32,256,512]{2,1,0:T(8,128)(2,1)} %refs_5_.1), custom_call_target="tpu_custom_call" | custom-call | tf_op jit(solution)/shard_map/average/pallas_call | solution.py:242
  69.8 11.9 %all_to_all.16.refs_1_ = bf16[16,2,64,128]{3,2,1,0:T(8,128)(2,1)S(1)} all-to-all(bf16[16,2,64,128]{3,2,1,0:T(8,128)(2,1)S(1)} %get-tuple-element.19), channel_id=1, replica_groups=mesh['facet'=8,'chan'=16] {'chan'}, dimensions={0} | all-to-all | bytes 1048576 | tf_op jit(solution)/shard_map/all_to_all | solution.py:433
  81.7 5.0 %grid_rows.1 = bf16[16,32,512]{2,1,0:T(8,128)(2,1)S(1)} custom-call(s32[8,128]{1,0:T(8,128)S(1)} %get-tuple-element.16.refs_0_, bf16[16,2,64,128]{3,2,1,0:T(8,128)(2,1)S(1)} %all_to_all.16.refs_1_, s32[1,1024]{1,0:T(1,128)S(1)} %get-tuple-element.20.refs_2_, s32[1,1536]{1,0:T(1,128)S(1)} %get-tuple-element.21.refs_3_, ...), custom_call_target="tpu_custom_call" | custom-call | tf_op jit(solution)/shard_map/grid_rows/pallas_call | solution.py:299
  86.7 13.2 %all_to_all.17.main_ref = bf16[16,32,512]{2,1,0:T(8,128)(2,1)S(1)} all-to-all(bf16[16,32,512]{2,1,0:T(8,128)(2,1)S(1)} %grid_rows.1), channel_id=1, replica_groups=mesh['facet'=8,'chan'=16] {'chan'}, dimensions={0} | all-to-all | bytes 1048576 | tf_op jit(solution)/shard_map/all_to_all | solution.py:433
  99.9 0.1 strips.1.refs_0_
  100.0 1.8 %collective-permute-start.1 = (bf16[16,32,128]{2,1,0:T(8,128)(2,1)S(1)}, bf16[16,32,128]{2,1,0:T(8,128)(2,1)S(1)}, u32[]{:S(2)}, u32[]{:S(2)}) collective-permute-start(bf16[16,32,128]{2,1,0:T(8,128)(2,1)S(1)} %strips.1.refs_0_), channel_id=1, source_target_pairs={{0,64},{16,80},{32,96},{48,112},{64,0},{80,16},{96,32},{112,48},{1... | collective-permute-start | bytes 393224 | tf_op jit(solution)/shard_map/ppermute | solution.py:459
  101.8 0.0 collective-permute-start
  101.8 1.1 place.1
  102.9 2.7 %collective-permute-start.2 = (bf16[16,32,128]{2,1,0:T(8,128)(2,1)S(1)}, bf16[16,32,128]{2,1,0:T(8,128)(2,1)S(1)}, u32[]{:S(2)}, u32[]{:S(2)}) collective-permute-start(bf16[16,32,128]{2,1,0:T(8,128)(2,1)S(1)} %strips.1.refs_0_), channel_id=1, source_target_pairs={{0,96},{16,112},{32,0},{48,16},{64,32},{80,48},{96,64},{112,80},{1... | collective-permute-start | bytes 393224 | tf_op jit(solution)/shard_map/ppermute | solution.py:459
  105.7 0.0 copy-done
  105.7 0.1 constant_dynamic-slice_fusion
  105.7 0.1 copy.10
  105.8 4.0 %collective-permute-start.3 = (bf16[16,32,128]{2,1,0:T(8,128)(2,1)S(1)}, bf16[16,32,128]{2,1,0:T(8,128)(2,1)S(1)}, u32[]{:S(2)}, u32[]{:S(2)}) collective-permute-start(bf16[16,32,128]{2,1,0:T(8,128)(2,1)S(1)} %strips.1.refs_0_), channel_id=1, source_target_pairs={{0,16},{16,0},{32,48},{48,32},{64,80},{80,64},{96,112},{112,96},{1... | collective-permute-start | bytes 393224 | tf_op jit(solution)/shard_map/ppermute | solution.py:460
  109.9 0.0 collective-permute-done.1.refs_2_
  109.9 0.3 collective-permute-start.5
  110.2 0.0 collective-permute-done.refs_1_
  110.2 1.4 %collective-permute-start.4 = (bf16[16,32,128]{2,1,0:T(8,128)(2,1)S(1)}, bf16[16,32,128]{2,1,0:T(8,128)(2,1)S(1)}, u32[]{:S(2)}, u32[]{:S(2)}) collective-permute-start(bf16[16,32,128]{2,1,0:T(8,128)(2,1)S(1)} %collective-permute-done.refs_1_), channel_id=1, source_target_pairs={{0,16},{16,0},{32,48},{48,32},{64,80},{80,64},{96,112},{112,96},{1... | collective-permute-start | bytes 393224 | tf_op jit(solution)/shard_map/ppermute | solution.py:460
  111.6 0.0 collective-permute-done.2.refs_3_
  111.6 0.6 collective-permute-start.6
  112.3 0.1 pad_add_fusion.nb_vmem
  112.3 0.0 collective-permute-done.3.refs_4_
  112.3 0.0 collective-permute-done.5.refs_6_
  112.3 0.2 collective-permute-done.4.refs_5_
  112.6 0.6 collective-permute-done.6.refs_7_
  113.2 2.0 %join.1 = f32[16,2,16,512]{3,2,1,0:T(8,128)} custom-call(s32[2,8]{1,0:T(2,128)S(1)} %pad_add_fusion.nb_vmem, f32[16,2,16,512]{3,2,1,0:T(8,128)} %get-tuple-element.23.placed_hbm, f32[2,16,2,16,128]{4,3,2,1,0:T(8,128)S(1)} %get-tuple-element.25.rest_ref, bf16[16,32,128]{2,1,0:T(8,128)(2,1)S(1)} %strips.1.refs_0_, ...), custom_call_target="tpu_custom_call", output_to_operand_aliasing={{}: (1, {})} | custom-call | tf_op jit(solution)/shard_map/join/pallas_call | solution.py:414
  (1 shorter events, 0.0 us)
Async XLA Ops:
  0.0 105.7 %copy-start = (s32[16,4]{0,1:T(4,128)S(1)}, s32[16,4]{0,1:T(4,128)}, u32[]{:S(2)}) copy-start(s32[16,4]{0,1:T(4,128)} %param.13) | copy-start | bytes 772
  100.0 9.9 %collective-permute-start.1 = (bf16[16,32,128]{2,1,0:T(8,128)(2,1)S(1)}, bf16[16,32,128]{2,1,0:T(8,128)(2,1)S(1)}, u32[]{:S(2)}, u32[]{:S(2)}) collective-permute-start(bf16[16,32,128]{2,1,0:T(8,128)(2,1)S(1)} %strips.1.refs_0_), channel_id=1, source_target_pairs={{0,64},{16,80},{32,96},{48,112},{64,0},{80,16},{96,32},{112,48},{1... | collective-permute-start | bytes 393224 | tf_op jit(solution)/shard_map/ppermute | solution.py:459
  101.8 8.4 %collective-permute-start = (bf16[16,32,128]{2,1,0:T(8,128)(2,1)S(1)}, bf16[16,32,128]{2,1,0:T(8,128)(2,1)S(1)}, u32[]{:S(2)}, u32[]{:S(2)}) collective-permute-start(bf16[16,32,128]{2,1,0:T(8,128)(2,1)S(1)} %strips.1.refs_0_), channel_id=1, source_target_pairs={{0,32},{16,48},{32,64},{48,80},{64,96},{80,112},{96,0},{112,16},{1... | collective-permute-start | bytes 393224 | tf_op jit(solution)/shard_map/ppermute | solution.py:459
  102.9 8.7 %collective-permute-start.2 = (bf16[16,32,128]{2,1,0:T(8,128)(2,1)S(1)}, bf16[16,32,128]{2,1,0:T(8,128)(2,1)S(1)}, u32[]{:S(2)}, u32[]{:S(2)}) collective-permute-start(bf16[16,32,128]{2,1,0:T(8,128)(2,1)S(1)} %strips.1.refs_0_), channel_id=1, source_target_pairs={{0,96},{16,112},{32,0},{48,16},{64,32},{80,48},{96,64},{112,80},{1... | collective-permute-start | bytes 393224 | tf_op jit(solution)/shard_map/ppermute | solution.py:459
  105.8 6.5 %collective-permute-start.3 = (bf16[16,32,128]{2,1,0:T(8,128)(2,1)S(1)}, bf16[16,32,128]{2,1,0:T(8,128)(2,1)S(1)}, u32[]{:S(2)}, u32[]{:S(2)}) collective-permute-start(bf16[16,32,128]{2,1,0:T(8,128)(2,1)S(1)} %strips.1.refs_0_), channel_id=1, source_target_pairs={{0,16},{16,0},{32,48},{48,32},{64,80},{80,64},{96,112},{112,96},{1... | collective-permute-start | bytes 393224 | tf_op jit(solution)/shard_map/ppermute | solution.py:460
  109.9 2.5 %collective-permute-start.5 = (bf16[16,32,128]{2,1,0:T(8,128)(2,1)S(1)}, bf16[16,32,128]{2,1,0:T(8,128)(2,1)S(1)}, u32[]{:S(2)}, u32[]{:S(2)}) collective-permute-start(bf16[16,32,128]{2,1,0:T(8,128)(2,1)S(1)} %collective-permute-done.1.refs_2_), channel_id=1, source_target_pairs={{0,16},{16,0},{32,48},{48,32},{64,80},{80,64},{96,112},{112,96},{1... | collective-permute-start | bytes 393224 | tf_op jit(solution)/shard_map/ppermute | solution.py:460
  110.2 2.4 %collective-permute-start.4 = (bf16[16,32,128]{2,1,0:T(8,128)(2,1)S(1)}, bf16[16,32,128]{2,1,0:T(8,128)(2,1)S(1)}, u32[]{:S(2)}, u32[]{:S(2)}) collective-permute-start(bf16[16,32,128]{2,1,0:T(8,128)(2,1)S(1)} %collective-permute-done.refs_1_), channel_id=1, source_target_pairs={{0,16},{16,0},{32,48},{48,32},{64,80},{80,64},{96,112},{112,96},{1... | collective-permute-start | bytes 393224 | tf_op jit(solution)/shard_map/ppermute | solution.py:460
  111.6 1.6 %collective-permute-start.6 = (bf16[16,32,128]{2,1,0:T(8,128)(2,1)S(1)}, bf16[16,32,128]{2,1,0:T(8,128)(2,1)S(1)}, u32[]{:S(2)}, u32[]{:S(2)}) collective-permute-start(bf16[16,32,128]{2,1,0:T(8,128)(2,1)S(1)} %collective-permute-done.2.refs_3_), channel_id=1, source_target_pairs={{0,16},{16,0},{32,48},{48,32},{64,80},{80,64},{96,112},{112,96},{1... | collective-permute-start | bytes 393224 | tf_op jit(solution)/shard_map/ppermute | solution.py:460

commit v9 on v8

--- a/solution.py
+++ b/solution.py
@@ -135,6 +135,8 @@
     ]
     for copy in smalls:
         copy.start()
+    for copy in smalls:
+        copy.wait()
     halves, dests = vis_hbm.shape[:2]
     n = sem.shape[1]
     copies = []
@@ -143,8 +145,6 @@
         for h in range(halves):
             copies.append(pltpu.make_async_copy(vis_hbm.at[h, at], out_ref.at[at, h], sem.at[h, i]))
             copies[-1].start()
-    for copy in smalls:
-        copy.wait()
     fill_tables(n_planes, t_dev, count_ref, plane_ref, tile_ref, *tables)
     for copy in copies:
         copy.wait()
@@ -195,19 +195,7 @@
         turn = times(turn, step)
 
 
-def fetch_matrices(k_hbm, first, k_ref, sem):
-    n_fetch = sem.shape[0]
-    part = k_ref.shape[0] // n_fetch
-    fetches = []
-    for i in range(n_fetch):
-        source = k_hbm.at[pl.ds(first + i * part, part)]
-        fetches.append(pltpu.make_async_copy(source, k_ref.at[pl.ds(i * part, part)], sem.at[i]))
-        fetches[-1].start()
-    return fetches
-
-
-def average_kernel(delay_ref, vis_ref, k_hbm, out_ref, k_ref, inner_ref, outer_ref, sem):
-    fetches = fetch_matrices(k_hbm, 0, k_ref, sem)
+def average_kernel(delay_ref, vis_ref, out_ref, inner_ref, outer_ref):
     fill_turns(delay_ref[...], inner_ref, outer_ref)
     n_out, _, rows, _ = out_ref.shape
     for r in range(0, rows, 16):
@@ -231,37 +219,29 @@
             return carry
 
         lax.fori_loop(0, n_out, one, 0, unroll=4)
-    for fetch in fetches:
-        fetch.wait()
-
-
-def average(delay, vis, kernels):
+
+
+def average(delay, vis):
     n_ch, halves, rows, bv = vis.shape
     n_out = n_ch // AVG
-    n_planes, k_rows, cells = kernels.shape
     return pl.pallas_call(
         average_kernel,
-        out_shape=[
-            jax.ShapeDtypeStruct((n_out, halves, rows, bv), jnp.bfloat16),
-            jax.ShapeDtypeStruct((n_planes // 2, k_rows, cells), kernels.dtype),
-        ],
-        in_specs=[vmem()] * 2 + [pl.BlockSpec(memory_space=pltpu.HBM)],
-        out_specs=[vmem()] * 2,
+        out_shape=jax.ShapeDtypeStruct((n_out, halves, rows, bv), jnp.bfloat16),
+        in_specs=[vmem()] * 2,
+        out_specs=vmem(),
         scratch_shapes=[
             pltpu.VMEM((AVG - 1, 2, rows, bv), jnp.float32),
             pltpu.VMEM((n_out, 2, rows, bv), jnp.float32),
-            pltpu.SemaphoreType.DMA((4,)),
-        ],
-        compiler_params=pltpu.CompilerParams(vmem_limit_bytes=16 * MIB),
+        ],
+        compiler_params=pltpu.CompilerParams(vmem_limit_bytes=8 * MIB),
         name="average",
-    )(delay, vis, pltpu.with_memory_space_constraint(kernels, pltpu.HBM))
+    )(delay, vis)
 
 
 def grid_kernel(n_pieces, *refs):
-    piece_vmem, rows_ref, place_ref, code_ref, low_ref, k_hbm, out_ref, piece_ref, high_ref, x_ref, c_ref, sem, piece_sem = refs
+    piece_vmem, rows_ref, place_ref, code_ref, k_ref, out_ref, piece_ref, x_ref, c_ref, piece_sem = refs
     piece_copy = pltpu.make_async_copy(piece_vmem, piece_ref, piece_sem.at[0])
     piece_copy.start()
-    fetches = fetch_matrices(k_hbm, low_ref.shape[0], high_ref, sem)
     n_src, _, per, bv = rows_ref.shape
     re = rows_ref[:, 0].reshape(n_src * per, bv)
     im = rows_ref[:, 1].reshape(n_src * per, bv)
@@ -270,17 +250,14 @@
     x_ref[...] = jnp.dot(order, x, preferred_element_type=jnp.float32).astype(jnp.bfloat16)
     c_ref[...] = jnp.zeros_like(c_ref)
     piece_copy.wait()
-    for lane, k_ref in ((0, low_ref), (64, high_ref)):
-        if lane:
-            for fetch in fetches:
-                fetch.wait()
+    for lane, first in ((0, 0), (64, k_ref.shape[0] // 2)):
         for begin in range(0, n_pieces, STRETCH):
 
             @pl.when(begin < piece_ref[2, lane])
-            def _(begin=begin, lane=lane, k_ref=k_ref):
+            def _(begin=begin, lane=lane, first=first):
                 for i in range(lane + begin, lane + min(begin + STRETCH, n_pieces)):
                     at = pl.ds(pl.multiple_of(piece_ref[0, i] * GROUP, GROUP), PIECE)
-                    product = jnp.dot(x_ref[at, :], k_ref[piece_ref[1, i]], preferred_element_type=jnp.float32)
+                    product = jnp.dot(x_ref[at, :], k_ref[first + piece_ref[1, i]], preferred_element_type=jnp.float32)
                     c_ref[at, :] = product.astype(jnp.bfloat16)
 
     n_used = code_ref.shape[1]
@@ -289,7 +266,7 @@
     out_ref[...] = grid.astype(jnp.bfloat16).reshape(out_ref.shape)
 
 
-def grid_rows(piece, rows, place, code, low, kernels, n_codes):
+def grid_rows(piece, rows, place, code, kernels, n_codes):
     n_planes, k_rows, cells = kernels.shape
     n_rows = place.shape[1]
     n_order, _ = sizes(n_rows, n_planes)
@@ -299,19 +276,17 @@
     return pl.pallas_call(
         functools.partial(grid_kernel, n_pieces),
         out_shape=jax.ShapeDtypeStruct((n_chan, n_codes // n_chan, cells), jnp.bfloat16),
-        in_specs=[vmem()] * 5 + [pl.BlockSpec(memory_space=pltpu.HBM)],
+        in_specs=[vmem()] * 5,
         out_specs=vmem(),
         scratch_shapes=[
             pltpu.SMEM(piece.shape, jnp.int32),
-            pltpu.VMEM(low.shape, low.dtype),
             pltpu.VMEM((n_order, k_rows), jnp.bfloat16),
             pltpu.VMEM((n_order, cells), jnp.bfloat16),
-            pltpu.SemaphoreType.DMA((4,)),
             pltpu.SemaphoreType.DMA((1,)),
         ],
-        compiler_params=pltpu.CompilerParams(vmem_limit_bytes=24 * MIB),
+        compiler_params=pltpu.CompilerParams(vmem_limit_bytes=20 * MIB),
         name="grid_rows",
-    )(piece, rows, place, code, low, pltpu.with_memory_space_constraint(kernels, pltpu.HBM))
+    )(piece, rows, place, code, kernels)
 
 
 def strip_kernel(main_ref, out_ref):
@@ -450,9 +425,8 @@
     )
     vis = exchange(vis, ("facet", "chan"))
 
-    rows, low = average(delay, vis, kernels)
-    rows = exchange(rows, "chan")
-    main = exchange(grid_rows(piece, rows, place, code, low, kernels, fac_dev * n_tiles), "chan")
+    rows = exchange(average(delay, vis), "chan")
+    main = exchange(grid_rows(piece, rows, place, code, kernels, fac_dev * n_tiles), "chan")
 
     own = strips_of(main)
     chips = n_facet // 2

time: 115 us -> 114 us (level)
  Pallas kernels: 14 us -> 12.6 us
where the time goes in v9:
time: 114 us
  blocking collectives  89.1 us (78%)
  Pallas kernels  12.6 us (11%)
  starting transfers between devices  11 us (10%)
    all_to_all x3, blocking collectives, exchange(): return lax.all_to_all(x, axis, split_axis=0, concat_axis=0, tiled=True)  89.1 us
    ppermute x4, starting transfers between devices, local(): lax.ppermute(x, 'facet', [(f, f ^ 1) for f in range(n_facet)])  6.38 us
    ppermute x3, starting transfers between devices, local(): lax.ppermute(x, 'facet', [(f, (f + 2 * dz) % n_facet) for f in range(n_fa...  4.57 us
    pallas_call x1, Pallas kernels, grid_rows(): pl.pallas_call(functools.partial(grid_kernel, n_pieces), out_shape=jax.Sh...  4 us
    pallas_call x1, Pallas kernels, send_order(): pl.pallas_call(functools.partial(send_kernel, n_planes, t_dev), out_shape...  3.68 us
  transfers between devices with their start and end apart: 7, of which 2 were waited for; matrix products, arithmetic and copies ran while one was open for 0% of the time, Pallas kernels for 1%

profile of v9, /device:TPU:1, one launch (start us, length us, event | category | flops | bytes accessed | tf_op | source)
XLA Modules:
  0.0 113.8 jit_solution(10321344785312859548)
XLA Ops:
  0.0 0.0 copy-start
  0.0 0.0 slice-start
  0.0 3.7 %send_order.1 = (bf16[128,2,64,128]{3,2,1,0:T(8,128)(2,1)S(1)}, f32[64,128]{1,0:T(8,128)S(1)}, s32[1,1024]{1,0:T(1,128)S(1)}, s32[1,1536]{1,0:T(1,128)S(1)}, s32[8,128]{1,0:T(8,128)S(1)}) custom-call(s32[2]{0:T(128)} %refs_0_.1, s32[2,512]{1,0:T(2,128)} %refs_1_.1, s32[2,512]{1,0:T(2,128)} %refs_2_.1, f32[16,64,128]{2,1,0:T(8,128)} %bitcast.5, ...), custom_call_target="tpu_custom_call" | custom-call | tf_op jit(solution)/shard_map/send_order/pallas_call | solution.py:158
  3.7 0.0 slice-start.1
  3.7 64.0 %all_to_all.15.vis_ref = bf16[128,2,64,128]{3,2,1,0:T(8,128)(2,1)S(1)} all-to-all(bf16[128,2,64,128]{3,2,1,0:T(8,128)(2,1)S(1)} %get-tuple-element.16), channel_id=1, replica_groups=mesh['facet'=8,'chan'=16] {'facet','chan'}, dimensions={0} | all-to-all | bytes 8388608 | tf_op jit(solution)/shard_map/all_to_all | solution.py:408
  67.7 1.7 %average.1 = bf16[16,2,64,128]{3,2,1,0:T(8,128)(2,1)S(1)} custom-call(f32[64,128]{1,0:T(8,128)S(1)} %get-tuple-element.15.delay_ref, bf16[128,2,64,128]{3,2,1,0:T(8,128)(2,1)S(1)} %all_to_all.15.vis_ref), custom_call_target="tpu_custom_call" | custom-call | tf_op jit(solution)/shard_map/average/pallas_call | solution.py:227
  69.4 11.9 %all_to_all.16.refs_1_ = bf16[16,2,64,128]{3,2,1,0:T(8,128)(2,1)S(1)} all-to-all(bf16[16,2,64,128]{3,2,1,0:T(8,128)(2,1)S(1)} %average.1), channel_id=1, replica_groups=mesh['facet'=8,'chan'=16] {'chan'}, dimensions={0} | all-to-all | bytes 1048576 | tf_op jit(solution)/shard_map/all_to_all | solution.py:408
  81.3 0.0 slice-done
  81.3 0.0 slice-done.1
  81.3 4.0 %grid_rows.1 = bf16[16,32,512]{2,1,0:T(8,128)(2,1)S(1)} custom-call(s32[8,128]{1,0:T(8,128)S(1)} %get-tuple-element.14.refs_0_, bf16[16,2,64,128]{3,2,1,0:T(8,128)(2,1)S(1)} %all_to_all.16.refs_1_, s32[1,1024]{1,0:T(1,128)S(1)} %get-tuple-element.17.refs_2_, s32[1,1536]{1,0:T(1,128)S(1)} %get-tuple-element.18.refs_3_, bf16[32,256,512]{2,1,0:T(8,128)(2,1)S(1)} %bitcast.3), custom_call_target="tpu_custom_call" | custom-call | tf_op jit(solution)/shard_map/grid_rows/pallas_call | solution.py:276
  85.3 13.2 %all_to_all.17.main_ref = bf16[16,32,512]{2,1,0:T(8,128)(2,1)S(1)} all-to-all(bf16[16,32,512]{2,1,0:T(8,128)(2,1)S(1)} %grid_rows.1), channel_id=1, replica_groups=mesh['facet'=8,'chan'=16] {'chan'}, dimensions={0} | all-to-all | bytes 1048576 | tf_op jit(solution)/shard_map/all_to_all | solution.py:408
  98.5 0.1 strips.1.refs_0_
  98.6 1.8 %collective-permute-start.1 = (bf16[16,32,128]{2,1,0:T(8,128)(2,1)S(1)}, bf16[16,32,128]{2,1,0:T(8,128)(2,1)S(1)}, u32[]{:S(2)}, u32[]{:S(2)}) collective-permute-start(bf16[16,32,128]{2,1,0:T(8,128)(2,1)S(1)} %strips.1.refs_0_), channel_id=1, source_target_pairs={{0,64},{16,80},{32,96},{48,112},{64,0},{80,16},{96,32},{112,48},{1... | collective-permute-start | bytes 393224 | tf_op jit(solution)/shard_map/ppermute | solution.py:433
  100.4 0.0 collective-permute-start
  100.4 1.1 place.1
  101.5 2.7 %collective-permute-start.2 = (bf16[16,32,128]{2,1,0:T(8,128)(2,1)S(1)}, bf16[16,32,128]{2,1,0:T(8,128)(2,1)S(1)}, u32[]{:S(2)}, u32[]{:S(2)}) collective-permute-start(bf16[16,32,128]{2,1,0:T(8,128)(2,1)S(1)} %strips.1.refs_0_), channel_id=1, source_target_pairs={{0,96},{16,112},{32,0},{48,16},{64,32},{80,48},{96,64},{112,80},{1... | collective-permute-start | bytes 393224 | tf_op jit(solution)/shard_map/ppermute | solution.py:433
  104.3 0.0 copy-done
  104.3 0.1 constant_dynamic-slice_fusion
  104.4 0.1 copy.10
  104.4 4.0 %collective-permute-start.3 = (bf16[16,32,128]{2,1,0:T(8,128)(2,1)S(1)}, bf16[16,32,128]{2,1,0:T(8,128)(2,1)S(1)}, u32[]{:S(2)}, u32[]{:S(2)}) collective-permute-start(bf16[16,32,128]{2,1,0:T(8,128)(2,1)S(1)} %strips.1.refs_0_), channel_id=1, source_target_pairs={{0,16},{16,0},{32,48},{48,32},{64,80},{80,64},{96,112},{112,96},{1... | collective-permute-start | bytes 393224 | tf_op jit(solution)/shard_map/ppermute | solution.py:434
  108.5 0.0 collective-permute-done.1.refs_2_
  108.5 0.3 collective-permute-start.5
  108.8 0.0 collective-permute-done.refs_1_
  108.8 1.4 %collective-permute-start.4 = (bf16[16,32,128]{2,1,0:T(8,128)(2,1)S(1)}, bf16[16,32,128]{2,1,0:T(8,128)(2,1)S(1)}, u32[]{:S(2)}, u32[]{:S(2)}) collective-permute-start(bf16[16,32,128]{2,1,0:T(8,128)(2,1)S(1)} %collective-permute-done.refs_1_), channel_id=1, source_target_pairs={{0,16},{16,0},{32,48},{48,32},{64,80},{80,64},{96,112},{112,96},{1... | collective-permute-start | bytes 393224 | tf_op jit(solution)/shard_map/ppermute | solution.py:434
  110.2 0.0 collective-permute-done.2.refs_3_
  110.2 0.6 collective-permute-start.6
  110.9 0.1 pad_add_fusion.nb_vmem
  110.9 0.0 collective-permute-done.3.refs_4_
  110.9 0.0 collective-permute-done.5.refs_6_
  111.0 0.2 collective-permute-done.4.refs_5_
  111.2 0.6 collective-permute-done.6.refs_7_
  111.8 2.0 %join.1 = f32[16,2,16,512]{3,2,1,0:T(8,128)} custom-call(s32[2,8]{1,0:T(2,128)S(1)} %pad_add_fusion.nb_vmem, f32[16,2,16,512]{3,2,1,0:T(8,128)} %get-tuple-element.19.placed_hbm, f32[2,16,2,16,128]{4,3,2,1,0:T(8,128)S(1)} %get-tuple-element.21.rest_ref, bf16[16,32,128]{2,1,0:T(8,128)(2,1)S(1)} %strips.1.refs_0_, ...), custom_call_target="tpu_custom_call", output_to_operand_aliasing={{}: (1, {})} | custom-call | tf_op jit(solution)/shard_map/join/pallas_call | solution.py:389
  (2 shorter events, 0.0 us)
Async XLA Ops:
  0.0 104.3 %copy-start = (s32[16,4]{0,1:T(4,128)S(1)}, s32[16,4]{0,1:T(4,128)}, u32[]{:S(2)}) copy-start(s32[16,4]{0,1:T(4,128)} %param.13) | copy-start | bytes 772
  0.0 81.3 %slice-start = ((s8[8388608]{0:T(1024)(128)(4,1)}), s8[4194304]{0:T(1024)(128)(4,1)S(1)}, s32[]{:S(2)}) async-start(s8[8388608]{0:T(1024)(128)(4,1)} %bitcast.2), calls=%async_computation.3 | async-start | bytes 8388608
  3.7 77.6 %slice-start.1 = ((s8[8388608]{0:T(1024)(128)(4,1)}), s8[4194304]{0:T(1024)(128)(4,1)S(1)}, s32[]{:S(2)}) async-start(s8[8388608]{0:T(1024)(128)(4,1)} %bitcast.2), calls=%async_computation.4 | async-start | bytes 8388608
  98.6 9.9 %collective-permute-start.1 = (bf16[16,32,128]{2,1,0:T(8,128)(2,1)S(1)}, bf16[16,32,128]{2,1,0:T(8,128)(2,1)S(1)}, u32[]{:S(2)}, u32[]{:S(2)}) collective-permute-start(bf16[16,32,128]{2,1,0:T(8,128)(2,1)S(1)} %strips.1.refs_0_), channel_id=1, source_target_pairs={{0,64},{16,80},{32,96},{48,112},{64,0},{80,16},{96,32},{112,48},{1... | collective-permute-start | bytes 393224 | tf_op jit(solution)/shard_map/ppermute | solution.py:433
  100.4 8.4 %collective-permute-start = (bf16[16,32,128]{2,1,0:T(8,128)(2,1)S(1)}, bf16[16,32,128]{2,1,0:T(8,128)(2,1)S(1)}, u32[]{:S(2)}, u32[]{:S(2)}) collective-permute-start(bf16[16,32,128]{2,1,0:T(8,128)(2,1)S(1)} %strips.1.refs_0_), channel_id=1, source_target_pairs={{0,32},{16,48},{32,64},{48,80},{64,96},{80,112},{96,0},{112,16},{1... | collective-permute-start | bytes 393224 | tf_op jit(solution)/shard_map/ppermute | solution.py:433
  101.5 8.7 %collective-permute-start.2 = (bf16[16,32,128]{2,1,0:T(8,128)(2,1)S(1)}, bf16[16,32,128]{2,1,0:T(8,128)(2,1)S(1)}, u32[]{:S(2)}, u32[]{:S(2)}) collective-permute-start(bf16[16,32,128]{2,1,0:T(8,128)(2,1)S(1)} %strips.1.refs_0_), channel_id=1, source_target_pairs={{0,96},{16,112},{32,0},{48,16},{64,32},{80,48},{96,64},{112,80},{1... | collective-permute-start | bytes 393224 | tf_op jit(solution)/shard_map/ppermute | solution.py:433
  104.4 6.5 %collective-permute-start.3 = (bf16[16,32,128]{2,1,0:T(8,128)(2,1)S(1)}, bf16[16,32,128]{2,1,0:T(8,128)(2,1)S(1)}, u32[]{:S(2)}, u32[]{:S(2)}) collective-permute-start(bf16[16,32,128]{2,1,0:T(8,128)(2,1)S(1)} %strips.1.refs_0_), channel_id=1, source_target_pairs={{0,16},{16,0},{32,48},{48,32},{64,80},{80,64},{96,112},{112,96},{1... | collective-permute-start | bytes 393224 | tf_op jit(solution)/shard_map/ppermute | solution.py:434
  108.5 2.5 %collective-permute-start.5 = (bf16[16,32,128]{2,1,0:T(8,128)(2,1)S(1)}, bf16[16,32,128]{2,1,0:T(8,128)(2,1)S(1)}, u32[]{:S(2)}, u32[]{:S(2)}) collective-permute-start(bf16[16,32,128]{2,1,0:T(8,128)(2,1)S(1)} %collective-permute-done.1.refs_2_), channel_id=1, source_target_pairs={{0,16},{16,0},{32,48},{48,32},{64,80},{80,64},{96,112},{112,96},{1... | collective-permute-start | bytes 393224 | tf_op jit(solution)/shard_map/ppermute | solution.py:434
  108.8 2.4 %collective-permute-start.4 = (bf16[16,32,128]{2,1,0:T(8,128)(2,1)S(1)}, bf16[16,32,128]{2,1,0:T(8,128)(2,1)S(1)}, u32[]{:S(2)}, u32[]{:S(2)}) collective-permute-start(bf16[16,32,128]{2,1,0:T(8,128)(2,1)S(1)} %collective-permute-done.refs_1_), channel_id=1, source_target_pairs={{0,16},{16,0},{32,48},{48,32},{64,80},{80,64},{96,112},{112,96},{1... | collective-permute-start | bytes 393224 | tf_op jit(solution)/shard_map/ppermute | solution.py:434
  110.2 1.6 %collective-permute-start.6 = (bf16[16,32,128]{2,1,0:T(8,128)(2,1)S(1)}, bf16[16,32,128]{2,1,0:T(8,128)(2,1)S(1)}, u32[]{:S(2)}, u32[]{:S(2)}) collective-permute-start(bf16[16,32,128]{2,1,0:T(8,128)(2,1)S(1)} %collective-permute-done.2.refs_3_), channel_id=1, source_target_pairs={{0,16},{16,0},{32,48},{48,32},{64,80},{80,64},{96,112},{112,96},{1... | collective-permute-start | bytes 393224 | tf_op jit(solution)/shard_map/ppermute | solution.py:434

commit v10 on v9

--- a/solution.py
+++ b/solution.py
@@ -145,7 +145,11 @@
         for h in range(halves):
             copies.append(pltpu.make_async_copy(vis_hbm.at[h, at], out_ref.at[at, h], sem.at[h, i]))
             copies[-1].start()
-    fill_tables(n_planes, t_dev, count_ref, plane_ref, tile_ref, *tables)
+
+    @pl.when(count_ref[0] >= 0)
+    def _():
+        fill_tables(n_planes, t_dev, count_ref, plane_ref, tile_ref, *tables)
+
     for copy in copies:
         copy.wait()
 
@@ -171,7 +175,7 @@
             pltpu.VMEM(planes.shape, jnp.int32),
             pltpu.VMEM(tiles.shape, jnp.int32),
             pltpu.SemaphoreType.DMA((4,)),
-            pltpu.SemaphoreType.DMA((halves, 8)),
+            pltpu.SemaphoreType.DMA((halves, 2)),
         ],
         compiler_params=pltpu.CompilerParams(vmem_limit_bytes=32 * MIB),
         name="send_order",
@@ -234,6 +238,7 @@
             pltpu.VMEM((n_out, 2, rows, bv), jnp.float32),
         ],
         compiler_params=pltpu.CompilerParams(vmem_limit_bytes=8 * MIB),
+        cost_estimate=pl.CostEstimate(flops=300 * 9 * n_ch * halves * rows * bv, transcendentals=0, bytes_accessed=300 * 5 * MIB),
         name="average",
     )(delay, vis)
 

time: 114 us -> 114 us (level)
  no operation moved by 1% of the time
where the time goes in v10:
time: 114 us; the launch traced here: 113 us
  blocking collectives  89.2 us (78%)
  Pallas kernels  12 us (11%)
  starting transfers between devices  10.9 us (10%)
    all_to_all x3, blocking collectives, exchange(): return lax.all_to_all(x, axis, split_axis=0, concat_axis=0, tiled=True)  89.2 us
    ppermute x4, starting transfers between devices, local(): lax.ppermute(x, 'facet', [(f, f ^ 1) for f in range(n_facet)])  6.38 us
    ppermute x3, starting transfers between devices, local(): lax.ppermute(x, 'facet', [(f, (f + 2 * dz) % n_facet) for f in range(n_fa...  4.56 us
    pallas_call x1, Pallas kernels, grid_rows(): pl.pallas_call(functools.partial(grid_kernel, n_pieces), out_shape=jax.Sh...  4 us
    pallas_call x1, Pallas kernels, send_order(): pl.pallas_call(functools.partial(send_kernel, n_planes, t_dev), out_shape...  3.04 us
  transfers between devices with their start and end apart: 7, of which 2 were waited for; matrix products, arithmetic and copies ran while one was open for 0% of the time, Pallas kernels for 1%

profile of v10, /device:TPU:1, one launch (start us, length us, event | category | flops | bytes accessed | tf_op | source)
XLA Modules:
  0.0 113.3 jit_solution(11199596858446797784)
XLA Ops:
  0.0 0.0 copy-start
  0.0 3.0 %send_order.1 = (bf16[128,2,64,128]{3,2,1,0:T(8,128)(2,1)S(1)}, f32[64,128]{1,0:T(8,128)S(1)}, s32[1,1024]{1,0:T(1,128)S(1)}, s32[1,1536]{1,0:T(1,128)S(1)}, s32[8,128]{1,0:T(8,128)S(1)}) custom-call(s32[2]{0:T(128)} %refs_0_.1, s32[2,512]{1,0:T(2,128)} %refs_1_.1, s32[2,512]{1,0:T(2,128)} %refs_2_.1, f32[16,64,128]{2,1,0:T(8,128)} %bitcast.5, ...), custom_call_target="tpu_custom_call" | custom-call | tf_op jit(solution)/shard_map/send_order/pallas_call | solution.py:162
  3.1 64.0 %all_to_all.15.vis_ref = bf16[128,2,64,128]{3,2,1,0:T(8,128)(2,1)S(1)} all-to-all(bf16[128,2,64,128]{3,2,1,0:T(8,128)(2,1)S(1)} %get-tuple-element.16), channel_id=1, replica_groups=mesh['facet'=8,'chan'=16] {'facet','chan'}, dimensions={0} | all-to-all | bytes 8388608 | tf_op jit(solution)/shard_map/all_to_all | solution.py:413
  67.0 0.0 slice-start
  67.0 0.0 slice-start.1
  67.0 1.7 %average.1 = bf16[16,2,64,128]{3,2,1,0:T(8,128)(2,1)S(1)} custom-call(f32[64,128]{1,0:T(8,128)S(1)} %get-tuple-element.15.delay_ref, bf16[128,2,64,128]{3,2,1,0:T(8,128)(2,1)S(1)} %all_to_all.15.vis_ref), custom_call_target="tpu_custom_call" | custom-call | flops 5662310400 | bytes 1572864000 | tf_op jit(solution)/shard_map/average/pallas_call | solution.py:231
  68.7 12.0 %all_to_all.16.refs_1_ = bf16[16,2,64,128]{3,2,1,0:T(8,128)(2,1)S(1)} all-to-all(bf16[16,2,64,128]{3,2,1,0:T(8,128)(2,1)S(1)} %average.1), channel_id=1, replica_groups=mesh['facet'=8,'chan'=16] {'chan'}, dimensions={0} | all-to-all | bytes 1048576 | tf_op jit(solution)/shard_map/all_to_all | solution.py:413
  80.8 0.0 slice-done
  80.8 0.0 slice-done.1
  80.8 4.0 %grid_rows.1 = bf16[16,32,512]{2,1,0:T(8,128)(2,1)S(1)} custom-call(s32[8,128]{1,0:T(8,128)S(1)} %get-tuple-element.14.refs_0_, bf16[16,2,64,128]{3,2,1,0:T(8,128)(2,1)S(1)} %all_to_all.16.refs_1_, s32[1,1024]{1,0:T(1,128)S(1)} %get-tuple-element.17.refs_2_, s32[1,1536]{1,0:T(1,128)S(1)} %get-tuple-element.18.refs_3_, bf16[32,256,512]{2,1,0:T(8,128)(2,1)S(1)} %bitcast.3), custom_call_target="tpu_custom_call" | custom-call | tf_op jit(solution)/shard_map/grid_rows/pallas_call | solution.py:281
  84.8 13.2 %all_to_all.17.main_ref = bf16[16,32,512]{2,1,0:T(8,128)(2,1)S(1)} all-to-all(bf16[16,32,512]{2,1,0:T(8,128)(2,1)S(1)} %grid_rows.1), channel_id=1, replica_groups=mesh['facet'=8,'chan'=16] {'chan'}, dimensions={0} | all-to-all | bytes 1048576 | tf_op jit(solution)/shard_map/all_to_all | solution.py:413
  98.0 0.1 strips.1.refs_0_
  98.1 1.8 %collective-permute-start.1 = (bf16[16,32,128]{2,1,0:T(8,128)(2,1)S(1)}, bf16[16,32,128]{2,1,0:T(8,128)(2,1)S(1)}, u32[]{:S(2)}, u32[]{:S(2)}) collective-permute-start(bf16[16,32,128]{2,1,0:T(8,128)(2,1)S(1)} %strips.1.refs_0_), channel_id=1, source_target_pairs={{0,64},{16,80},{32,96},{48,112},{64,0},{80,16},{96,32},{112,48},{1... | collective-permute-start | bytes 393224 | tf_op jit(solution)/shard_map/ppermute | solution.py:438
  99.9 0.0 collective-permute-start
  99.9 1.1 place.1
  101.0 2.7 %collective-permute-start.2 = (bf16[16,32,128]{2,1,0:T(8,128)(2,1)S(1)}, bf16[16,32,128]{2,1,0:T(8,128)(2,1)S(1)}, u32[]{:S(2)}, u32[]{:S(2)}) collective-permute-start(bf16[16,32,128]{2,1,0:T(8,128)(2,1)S(1)} %strips.1.refs_0_), channel_id=1, source_target_pairs={{0,96},{16,112},{32,0},{48,16},{64,32},{80,48},{96,64},{112,80},{1... | collective-permute-start | bytes 393224 | tf_op jit(solution)/shard_map/ppermute | solution.py:438
  103.8 0.0 copy-done
  103.8 0.1 constant_dynamic-slice_fusion
  103.8 0.1 copy.10
  103.9 4.0 %collective-permute-start.3 = (bf16[16,32,128]{2,1,0:T(8,128)(2,1)S(1)}, bf16[16,32,128]{2,1,0:T(8,128)(2,1)S(1)}, u32[]{:S(2)}, u32[]{:S(2)}) collective-permute-start(bf16[16,32,128]{2,1,0:T(8,128)(2,1)S(1)} %strips.1.refs_0_), channel_id=1, source_target_pairs={{0,16},{16,0},{32,48},{48,32},{64,80},{80,64},{96,112},{112,96},{1... | collective-permute-start | bytes 393224 | tf_op jit(solution)/shard_map/ppermute | solution.py:439
  108.0 0.0 collective-permute-done.1.refs_2_
  108.0 0.3 collective-permute-start.5
  108.3 0.0 collective-permute-done.refs_1_
  108.3 1.4 %collective-permute-start.4 = (bf16[16,32,128]{2,1,0:T(8,128)(2,1)S(1)}, bf16[16,32,128]{2,1,0:T(8,128)(2,1)S(1)}, u32[]{:S(2)}, u32[]{:S(2)}) collective-permute-start(bf16[16,32,128]{2,1,0:T(8,128)(2,1)S(1)} %collective-permute-done.refs_1_), channel_id=1, source_target_pairs={{0,16},{16,0},{32,48},{48,32},{64,80},{80,64},{96,112},{112,96},{1... | collective-permute-start | bytes 393224 | tf_op jit(solution)/shard_map/ppermute | solution.py:439
  109.7 0.0 collective-permute-done.2.refs_3_
  109.7 0.6 collective-permute-start.6
  110.4 0.1 pad_add_fusion.nb_vmem
  110.4 0.0 collective-permute-done.3.refs_4_
  110.4 0.0 collective-permute-done.5.refs_6_
  110.4 0.2 collective-permute-done.4.refs_5_
  110.7 0.7 collective-permute-done.6.refs_7_
  111.3 2.0 %join.1 = f32[16,2,16,512]{3,2,1,0:T(8,128)} custom-call(s32[2,8]{1,0:T(2,128)S(1)} %pad_add_fusion.nb_vmem, f32[16,2,16,512]{3,2,1,0:T(8,128)} %get-tuple-element.19.placed_hbm, f32[2,16,2,16,128]{4,3,2,1,0:T(8,128)S(1)} %get-tuple-element.21.rest_ref, bf16[16,32,128]{2,1,0:T(8,128)(2,1)S(1)} %strips.1.refs_0_, ...), custom_call_target="tpu_custom_call", output_to_operand_aliasing={{}: (1, {})} | custom-call | tf_op jit(solution)/shard_map/join/pallas_call | solution.py:394
  (2 shorter events, 0.0 us)
Async XLA Ops:
  0.0 103.8 %copy-start = (s32[16,4]{0,1:T(4,128)S(1)}, s32[16,4]{0,1:T(4,128)}, u32[]{:S(2)}) copy-start(s32[16,4]{0,1:T(4,128)} %param.13) | copy-start | bytes 772
  67.0 13.7 %slice-start = ((s8[8388608]{0:T(1024)(128)(4,1)}), s8[4194304]{0:T(1024)(128)(4,1)S(1)}, s32[]{:S(2)}) async-start(s8[8388608]{0:T(1024)(128)(4,1)} %bitcast.2), calls=%async_computation.3 | async-start | bytes 8388608
  67.0 13.7 %slice-start.1 = ((s8[8388608]{0:T(1024)(128)(4,1)}), s8[4194304]{0:T(1024)(128)(4,1)S(1)}, s32[]{:S(2)}) async-start(s8[8388608]{0:T(1024)(128)(4,1)} %bitcast.2), calls=%async_computation.4 | async-start | bytes 8388608
  98.1 9.9 %collective-permute-start.1 = (bf16[16,32,128]{2,1,0:T(8,128)(2,1)S(1)}, bf16[16,32,128]{2,1,0:T(8,128)(2,1)S(1)}, u32[]{:S(2)}, u32[]{:S(2)}) collective-permute-start(bf16[16,32,128]{2,1,0:T(8,128)(2,1)S(1)} %strips.1.refs_0_), channel_id=1, source_target_pairs={{0,64},{16,80},{32,96},{48,112},{64,0},{80,16},{96,32},{112,48},{1... | collective-permute-start | bytes 393224 | tf_op jit(solution)/shard_map/ppermute | solution.py:438
  99.9 8.4 %collective-permute-start = (bf16[16,32,128]{2,1,0:T(8,128)(2,1)S(1)}, bf16[16,32,128]{2,1,0:T(8,128)(2,1)S(1)}, u32[]{:S(2)}, u32[]{:S(2)}) collective-permute-start(bf16[16,32,128]{2,1,0:T(8,128)(2,1)S(1)} %strips.1.refs_0_), channel_id=1, source_target_pairs={{0,32},{16,48},{32,64},{48,80},{64,96},{80,112},{96,0},{112,16},{1... | collective-permute-start | bytes 393224 | tf_op jit(solution)/shard_map/ppermute | solution.py:438
  101.0 8.7 %collective-permute-start.2 = (bf16[16,32,128]{2,1,0:T(8,128)(2,1)S(1)}, bf16[16,32,128]{2,1,0:T(8,128)(2,1)S(1)}, u32[]{:S(2)}, u32[]{:S(2)}) collective-permute-start(bf16[16,32,128]{2,1,0:T(8,128)(2,1)S(1)} %strips.1.refs_0_), channel_id=1, source_target_pairs={{0,96},{16,112},{32,0},{48,16},{64,32},{80,48},{96,64},{112,80},{1... | collective-permute-start | bytes 393224 | tf_op jit(solution)/shard_map/ppermute | solution.py:438
  103.9 6.5 %collective-permute-start.3 = (bf16[16,32,128]{2,1,0:T(8,128)(2,1)S(1)}, bf16[16,32,128]{2,1,0:T(8,128)(2,1)S(1)}, u32[]{:S(2)}, u32[]{:S(2)}) collective-permute-start(bf16[16,32,128]{2,1,0:T(8,128)(2,1)S(1)} %strips.1.refs_0_), channel_id=1, source_target_pairs={{0,16},{16,0},{32,48},{48,32},{64,80},{80,64},{96,112},{112,96},{1... | collective-permute-start | bytes 393224 | tf_op jit(solution)/shard_map/ppermute | solution.py:439
  108.0 2.5 %collective-permute-start.5 = (bf16[16,32,128]{2,1,0:T(8,128)(2,1)S(1)}, bf16[16,32,128]{2,1,0:T(8,128)(2,1)S(1)}, u32[]{:S(2)}, u32[]{:S(2)}) collective-permute-start(bf16[16,32,128]{2,1,0:T(8,128)(2,1)S(1)} %collective-permute-done.1.refs_2_), channel_id=1, source_target_pairs={{0,16},{16,0},{32,48},{48,32},{64,80},{80,64},{96,112},{112,96},{1... | collective-permute-start | bytes 393224 | tf_op jit(solution)/shard_map/ppermute | solution.py:439
  108.3 2.4 %collective-permute-start.4 = (bf16[16,32,128]{2,1,0:T(8,128)(2,1)S(1)}, bf16[16,32,128]{2,1,0:T(8,128)(2,1)S(1)}, u32[]{:S(2)}, u32[]{:S(2)}) collective-permute-start(bf16[16,32,128]{2,1,0:T(8,128)(2,1)S(1)} %collective-permute-done.refs_1_), channel_id=1, source_target_pairs={{0,16},{16,0},{32,48},{48,32},{64,80},{80,64},{96,112},{112,96},{1... | collective-permute-start | bytes 393224 | tf_op jit(solution)/shard_map/ppermute | solution.py:439
  109.7 1.6 %collective-permute-start.6 = (bf16[16,32,128]{2,1,0:T(8,128)(2,1)S(1)}, bf16[16,32,128]{2,1,0:T(8,128)(2,1)S(1)}, u32[]{:S(2)}, u32[]{:S(2)}) collective-permute-start(bf16[16,32,128]{2,1,0:T(8,128)(2,1)S(1)} %collective-permute-done.2.refs_3_), channel_id=1, source_target_pairs={{0,16},{16,0},{32,48},{48,32},{64,80},{80,64},{96,112},{112,96},{1... | collective-permute-start | bytes 393224 | tf_op jit(solution)/shard_map/ppermute | solution.py:439

commit v11 on v10

--- a/solution.py
+++ b/solution.py
@@ -126,7 +126,8 @@
 
 def send_kernel(n_planes, t_dev, *refs):
     (count_hbm, plane_hbm, tile_hbm, delay_hbm, vis_hbm), refs = refs[:5], refs[5:]
-    (out_ref, delay_ref, *tables), (count_ref, plane_ref, tile_ref, small_sem, sem) = refs[:-5], refs[-5:]
+    (out_ref, inner_ref, outer_ref, *tables), scratch = refs[:-6], refs[-6:]
+    delay_ref, count_ref, plane_ref, tile_ref, small_sem, sem = scratch
     smalls = [
         pltpu.make_async_copy(count_hbm, count_ref, small_sem.at[0]),
         pltpu.make_async_copy(plane_hbm, plane_ref, small_sem.at[1]),
@@ -148,13 +149,14 @@
 
     @pl.when(count_ref[0] >= 0)
     def _():
+        fill_turns(delay_ref[...], inner_ref, outer_ref)
         fill_tables(n_planes, t_dev, count_ref, plane_ref, tile_ref, *tables)
 
     for copy in copies:
         copy.wait()
 
 
-def send_order(counts, planes, tiles, delays, vis, n_planes, t_dev):
+def send_order(counts, planes, tiles, delays, vis, n_planes, n_out, t_dev):
     halves, dests, rows, bv = vis.shape
     n_rows = planes.shape[0] * planes.shape[1]
     n_order, n_used = sizes(n_rows, n_planes)
@@ -163,14 +165,16 @@
         functools.partial(send_kernel, n_planes, t_dev),
         out_shape=[
             jax.ShapeDtypeStruct((dests, halves, rows, bv), vis.dtype),
-            jax.ShapeDtypeStruct(delays.shape[1:], delays.dtype),
+            jax.ShapeDtypeStruct((AVG - 1, 2, rows, bv), jnp.float32),
+            jax.ShapeDtypeStruct((n_out, 2, rows, bv), jnp.float32),
             jax.ShapeDtypeStruct((1, n_rows), jnp.int32),
             jax.ShapeDtypeStruct((1, n_used), jnp.int32),
             jax.ShapeDtypeStruct((8, 128), jnp.int32),
         ],
         in_specs=[pl.BlockSpec(memory_space=pltpu.HBM)] * len(args),
-        out_specs=[vmem()] * 5,
+        out_specs=[vmem()] * 6,
         scratch_shapes=[
+            pltpu.VMEM((rows, bv), jnp.float32),
             pltpu.SMEM(counts.shape, jnp.int32),
             pltpu.VMEM(planes.shape, jnp.int32),
             pltpu.VMEM(tiles.shape, jnp.int32),
@@ -199,8 +203,7 @@
         turn = times(turn, step)
 
 
-def average_kernel(delay_ref, vis_ref, out_ref, inner_ref, outer_ref):
-    fill_turns(delay_ref[...], inner_ref, outer_ref)
+def average_kernel(inner_ref, outer_ref, vis_ref, out_ref):
     n_out, _, rows, _ = out_ref.shape
     for r in range(0, rows, 16):
         at = slice(r, r + 16)
@@ -225,22 +228,18 @@
         lax.fori_loop(0, n_out, one, 0, unroll=4)
 
 
-def average(delay, vis):
+def average(inner, outer, vis):
     n_ch, halves, rows, bv = vis.shape
     n_out = n_ch // AVG
     return pl.pallas_call(
         average_kernel,
         out_shape=jax.ShapeDtypeStruct((n_out, halves, rows, bv), jnp.bfloat16),
-        in_specs=[vmem()] * 2,
+        in_specs=[vmem()] * 3,
         out_specs=vmem(),
-        scratch_shapes=[
-            pltpu.VMEM((AVG - 1, 2, rows, bv), jnp.float32),
-            pltpu.VMEM((n_out, 2, rows, bv), jnp.float32),
-        ],
         compiler_params=pltpu.CompilerParams(vmem_limit_bytes=8 * MIB),
         cost_estimate=pl.CostEstimate(flops=300 * 9 * n_ch * halves * rows * bv, transcendentals=0, bytes_accessed=300 * 5 * MIB),
         name="average",
-    )(delay, vis)
+    )(inner, outer, vis)
 
 
 def grid_kernel(n_pieces, *refs):
@@ -425,12 +424,12 @@
     per = n_rows // n_chan
 
     vis = visibilities.reshape(halves, n_facet * n_chan, per, bv)
-    vis, delay, place, code, piece = send_order(
-        counts, plane_of, tile_of, delays.reshape(n_chan, per, bv), vis, kernels.shape[0], t_dev
+    vis, inner, outer, place, code, piece = send_order(
+        counts, plane_of, tile_of, delays.reshape(n_chan, per, bv), vis, kernels.shape[0], n_chan, t_dev
     )
     vis = exchange(vis, ("facet", "chan"))
 
-    rows = exchange(average(delay, vis), "chan")
+    rows = exchange(average(inner, outer, vis), "chan")
     main = exchange(grid_rows(piece, rows, place, code, kernels, fac_dev * n_tiles), "chan")
 
     own = strips_of(main)

time: 114 us -> 113 us (level)
  no operation moved by 1% of the time
where the time goes in v11:
time: 113 us
  blocking collectives  89.3 us (79%)
  Pallas kernels  11.7 us (10%)
  starting transfers between devices  10.9 us (10%)
    all_to_all x3, blocking collectives, exchange(): return lax.all_to_all(x, axis, split_axis=0, concat_axis=0, tiled=True)  89.3 us
    ppermute x4, starting transfers between devices, local(): lax.ppermute(x, 'facet', [(f, f ^ 1) for f in range(n_facet)])  6.38 us
    ppermute x3, starting transfers between devices, local(): lax.ppermute(x, 'facet', [(f, (f + 2 * dz) % n_facet) for f in range(n_fa...  4.56 us
    pallas_call x1, Pallas kernels, grid_rows(): pl.pallas_call(functools.partial(grid_kernel, n_pieces), out_shape=jax.Sh...  4 us
    pallas_call x1, Pallas kernels, send_order(): pl.pallas_call(functools.partial(send_kernel, n_planes, t_dev), out_shape...  3.04 us
  transfers between devices with their start and end apart: 7, of which 2 were waited for; matrix products, arithmetic and copies ran while one was open for 0% of the time, Pallas kernels for 1%

profile of v11, /device:TPU:1, one launch (start us, length us, event | category | flops | bytes accessed | tf_op | source)
XLA Modules:
  0.0 113.2 jit_solution(17609534911285097440)
XLA Ops:
  0.0 0.0 copy-start
  0.0 3.0 %send_order.1 = (bf16[128,2,64,128]{3,2,1,0:T(8,128)(2,1)S(1)}, f32[7,2,64,128]{3,2,1,0:T(8,128)S(1)}, f32[16,2,64,128]{3,2,1,0:T(8,128)S(1)}, s32[1,1024]{1,0:T...) custom-call(s32[2]{0:T(128)} %refs_0_.1, s32[2,512]{1,0:T(2,128)} %refs_1_.1, s32[2,512]{1,0:T(2,128)} %refs_2_.1, ...), custom_call_target="tpu_custom_call" | custom-call | tf_op jit(solution)/shard_map/send_order/pallas_call | solution.py:164
  3.1 64.0 %all_to_all.15.vis_ref = bf16[128,2,64,128]{3,2,1,0:T(8,128)(2,1)S(1)} all-to-all(bf16[128,2,64,128]{3,2,1,0:T(8,128)(2,1)S(1)} %get-tuple-element.18), channel_id=1, replica_groups=mesh['facet'=8,'chan'=16] {'facet','chan'}, dimensions={0} | all-to-all | bytes 8388608 | tf_op jit(solution)/shard_map/all_to_all | solution.py:412
  67.0 0.0 slice-start
  67.0 0.0 slice-start.1
  67.0 1.4 %average.1 = bf16[16,2,64,128]{3,2,1,0:T(8,128)(2,1)S(1)} custom-call(f32[7,2,64,128]{3,2,1,0:T(8,128)S(1)} %get-tuple-element.16.inner_ref, f32[16,2,64,128]{3,2,1,0:T(8,128)S(1)} %get-tuple-element.17.outer_ref, bf16[128,2,64,128]{3,2,1,0:T(8,128)(2,1)S(1)} %all_to_all.15.vis_ref), custom_call_target="tpu_custom_call" | custom-call | flops 5662310400 | bytes 1572864000 | tf_op jit(solution)/shard_map/average/pallas_call | solution.py:234
  68.5 12.2 %all_to_all.16.refs_1_ = bf16[16,2,64,128]{3,2,1,0:T(8,128)(2,1)S(1)} all-to-all(bf16[16,2,64,128]{3,2,1,0:T(8,128)(2,1)S(1)} %average.1), channel_id=1, replica_groups=mesh['facet'=8,'chan'=16] {'chan'}, dimensions={0} | all-to-all | bytes 1048576 | tf_op jit(solution)/shard_map/all_to_all | solution.py:412
  80.6 0.0 slice-done
  80.6 0.0 slice-done.1
  80.6 4.0 %grid_rows.1 = bf16[16,32,512]{2,1,0:T(8,128)(2,1)S(1)} custom-call(s32[8,128]{1,0:T(8,128)S(1)} %get-tuple-element.15.refs_0_, bf16[16,2,64,128]{3,2,1,0:T(8,128)(2,1)S(1)} %all_to_all.16.refs_1_, s32[1,1024]{1,0:T(1,128)S(1)} %get-tuple-element.19.refs_2_, s32[1,1536]{1,0:T(1,128)S(1)} %get-tuple-element.20.refs_3_, bf16[32,256,512]{2,1,0:T(8,128)(2,1)S(1)} %bitcast.3), custom_call_target="tpu_custom_call" | custom-call | tf_op jit(solution)/shard_map/grid_rows/pallas_call | solution.py:280
  84.6 13.2 %all_to_all.17.main_ref = bf16[16,32,512]{2,1,0:T(8,128)(2,1)S(1)} all-to-all(bf16[16,32,512]{2,1,0:T(8,128)(2,1)S(1)} %grid_rows.1), channel_id=1, replica_groups=mesh['facet'=8,'chan'=16] {'chan'}, dimensions={0} | all-to-all | bytes 1048576 | tf_op jit(solution)/shard_map/all_to_all | solution.py:412
  97.8 0.1 strips.1.refs_0_
  98.0 1.8 %collective-permute-start.1 = (bf16[16,32,128]{2,1,0:T(8,128)(2,1)S(1)}, bf16[16,32,128]{2,1,0:T(8,128)(2,1)S(1)}, u32[]{:S(2)}, u32[]{:S(2)}) collective-permute-start(bf16[16,32,128]{2,1,0:T(8,128)(2,1)S(1)} %strips.1.refs_0_), channel_id=1, source_target_pairs={{0,64},{16,80},{32,96},{48,112},{64,0},{80,16},{96,32},{112,48},{1... | collective-permute-start | bytes 393224 | tf_op jit(solution)/shard_map/ppermute | solution.py:437
  99.8 0.0 collective-permute-start
  99.8 1.1 place.1
  100.9 2.7 %collective-permute-start.2 = (bf16[16,32,128]{2,1,0:T(8,128)(2,1)S(1)}, bf16[16,32,128]{2,1,0:T(8,128)(2,1)S(1)}, u32[]{:S(2)}, u32[]{:S(2)}) collective-permute-start(bf16[16,32,128]{2,1,0:T(8,128)(2,1)S(1)} %strips.1.refs_0_), channel_id=1, source_target_pairs={{0,96},{16,112},{32,0},{48,16},{64,32},{80,48},{96,64},{112,80},{1... | collective-permute-start | bytes 393224 | tf_op jit(solution)/shard_map/ppermute | solution.py:437
  103.6 0.0 copy-done
  103.6 0.1 constant_dynamic-slice_fusion
  103.7 0.1 copy.10
  103.8 4.0 %collective-permute-start.3 = (bf16[16,32,128]{2,1,0:T(8,128)(2,1)S(1)}, bf16[16,32,128]{2,1,0:T(8,128)(2,1)S(1)}, u32[]{:S(2)}, u32[]{:S(2)}) collective-permute-start(bf16[16,32,128]{2,1,0:T(8,128)(2,1)S(1)} %strips.1.refs_0_), channel_id=1, source_target_pairs={{0,16},{16,0},{32,48},{48,32},{64,80},{80,64},{96,112},{112,96},{1... | collective-permute-start | bytes 393224 | tf_op jit(solution)/shard_map/ppermute | solution.py:438
  107.8 0.0 collective-permute-done.1.refs_2_
  107.8 0.3 collective-permute-start.5
  108.2 0.0 collective-permute-done.refs_1_
  108.2 1.4 %collective-permute-start.4 = (bf16[16,32,128]{2,1,0:T(8,128)(2,1)S(1)}, bf16[16,32,128]{2,1,0:T(8,128)(2,1)S(1)}, u32[]{:S(2)}, u32[]{:S(2)}) collective-permute-start(bf16[16,32,128]{2,1,0:T(8,128)(2,1)S(1)} %collective-permute-done.refs_1_), channel_id=1, source_target_pairs={{0,16},{16,0},{32,48},{48,32},{64,80},{80,64},{96,112},{112,96},{1... | collective-permute-start | bytes 393224 | tf_op jit(solution)/shard_map/ppermute | solution.py:438
  109.5 0.0 collective-permute-done.2.refs_3_
  109.5 0.6 collective-permute-start.6
  110.2 0.1 pad_add_fusion.nb_vmem
  110.3 0.0 collective-permute-done.3.refs_4_
  110.3 0.0 collective-permute-done.5.refs_6_
  110.3 0.2 collective-permute-done.4.refs_5_
  110.5 0.6 collective-permute-done.6.refs_7_
  111.2 2.0 %join.1 = f32[16,2,16,512]{3,2,1,0:T(8,128)} custom-call(s32[2,8]{1,0:T(2,128)S(1)} %pad_add_fusion.nb_vmem, f32[16,2,16,512]{3,2,1,0:T(8,128)} %get-tuple-element.21.placed_hbm, f32[2,16,2,16,128]{4,3,2,1,0:T(8,128)S(1)} %get-tuple-element.23.rest_ref, bf16[16,32,128]{2,1,0:T(8,128)(2,1)S(1)} %strips.1.refs_0_, ...), custom_call_target="tpu_custom_call", output_to_operand_aliasing={{}: (1, {})} | custom-call | tf_op jit(solution)/shard_map/join/pallas_call | solution.py:393
  (2 shorter events, 0.0 us)
Async XLA Ops:
  0.0 103.6 %copy-start = (s32[16,4]{0,1:T(4,128)S(1)}, s32[16,4]{0,1:T(4,128)}, u32[]{:S(2)}) copy-start(s32[16,4]{0,1:T(4,128)} %param.13) | copy-start | bytes 772
  67.0 13.6 %slice-start = ((s8[8388608]{0:T(1024)(128)(4,1)}), s8[4194304]{0:T(1024)(128)(4,1)S(1)}, s32[]{:S(2)}) async-start(s8[8388608]{0:T(1024)(128)(4,1)} %bitcast.2), calls=%async_computation.3 | async-start | bytes 8388608
  67.0 13.6 %slice-start.1 = ((s8[8388608]{0:T(1024)(128)(4,1)}), s8[4194304]{0:T(1024)(128)(4,1)S(1)}, s32[]{:S(2)}) async-start(s8[8388608]{0:T(1024)(128)(4,1)} %bitcast.2), calls=%async_computation.4 | async-start | bytes 8388608
  98.0 9.9 %collective-permute-start.1 = (bf16[16,32,128]{2,1,0:T(8,128)(2,1)S(1)}, bf16[16,32,128]{2,1,0:T(8,128)(2,1)S(1)}, u32[]{:S(2)}, u32[]{:S(2)}) collective-permute-start(bf16[16,32,128]{2,1,0:T(8,128)(2,1)S(1)} %strips.1.refs_0_), channel_id=1, source_target_pairs={{0,64},{16,80},{32,96},{48,112},{64,0},{80,16},{96,32},{112,48},{1... | collective-permute-start | bytes 393224 | tf_op jit(solution)/shard_map/ppermute | solution.py:437
  99.8 8.4 %collective-permute-start = (bf16[16,32,128]{2,1,0:T(8,128)(2,1)S(1)}, bf16[16,32,128]{2,1,0:T(8,128)(2,1)S(1)}, u32[]{:S(2)}, u32[]{:S(2)}) collective-permute-start(bf16[16,32,128]{2,1,0:T(8,128)(2,1)S(1)} %strips.1.refs_0_), channel_id=1, source_target_pairs={{0,32},{16,48},{32,64},{48,80},{64,96},{80,112},{96,0},{112,16},{1... | collective-permute-start | bytes 393224 | tf_op jit(solution)/shard_map/ppermute | solution.py:437
  100.9 8.7 %collective-permute-start.2 = (bf16[16,32,128]{2,1,0:T(8,128)(2,1)S(1)}, bf16[16,32,128]{2,1,0:T(8,128)(2,1)S(1)}, u32[]{:S(2)}, u32[]{:S(2)}) collective-permute-start(bf16[16,32,128]{2,1,0:T(8,128)(2,1)S(1)} %strips.1.refs_0_), channel_id=1, source_target_pairs={{0,96},{16,112},{32,0},{48,16},{64,32},{80,48},{96,64},{112,80},{1... | collective-permute-start | bytes 393224 | tf_op jit(solution)/shard_map/ppermute | solution.py:437
  103.8 6.5 %collective-permute-start.3 = (bf16[16,32,128]{2,1,0:T(8,128)(2,1)S(1)}, bf16[16,32,128]{2,1,0:T(8,128)(2,1)S(1)}, u32[]{:S(2)}, u32[]{:S(2)}) collective-permute-start(bf16[16,32,128]{2,1,0:T(8,128)(2,1)S(1)} %strips.1.refs_0_), channel_id=1, source_target_pairs={{0,16},{16,0},{32,48},{48,32},{64,80},{80,64},{96,112},{112,96},{1... | collective-permute-start | bytes 393224 | tf_op jit(solution)/shard_map/ppermute | solution.py:438
  107.8 2.5 %collective-permute-start.5 = (bf16[16,32,128]{2,1,0:T(8,128)(2,1)S(1)}, bf16[16,32,128]{2,1,0:T(8,128)(2,1)S(1)}, u32[]{:S(2)}, u32[]{:S(2)}) collective-permute-start(bf16[16,32,128]{2,1,0:T(8,128)(2,1)S(1)} %collective-permute-done.1.refs_2_), channel_id=1, source_target_pairs={{0,16},{16,0},{32,48},{48,32},{64,80},{80,64},{96,112},{112,96},{1... | collective-permute-start | bytes 393224 | tf_op jit(solution)/shard_map/ppermute | solution.py:438
  108.2 2.4 %collective-permute-start.4 = (bf16[16,32,128]{2,1,0:T(8,128)(2,1)S(1)}, bf16[16,32,128]{2,1,0:T(8,128)(2,1)S(1)}, u32[]{:S(2)}, u32[]{:S(2)}) collective-permute-start(bf16[16,32,128]{2,1,0:T(8,128)(2,1)S(1)} %collective-permute-done.refs_1_), channel_id=1, source_target_pairs={{0,16},{16,0},{32,48},{48,32},{64,80},{80,64},{96,112},{112,96},{1... | collective-permute-start | bytes 393224 | tf_op jit(solution)/shard_map/ppermute | solution.py:438
  109.5 1.6 %collective-permute-start.6 = (bf16[16,32,128]{2,1,0:T(8,128)(2,1)S(1)}, bf16[16,32,128]{2,1,0:T(8,128)(2,1)S(1)}, u32[]{:S(2)}, u32[]{:S(2)}) collective-permute-start(bf16[16,32,128]{2,1,0:T(8,128)(2,1)S(1)} %collective-permute-done.2.refs_3_), channel_id=1, source_target_pairs={{0,16},{16,0},{32,48},{48,32},{64,80},{80,64},{96,112},{112,96},{1... | collective-permute-start | bytes 393224 | tf_op jit(solution)/shard_map/ppermute | solution.py:438

commit v12 on v11

--- a/solution.py
+++ b/solution.py
@@ -360,22 +360,22 @@
 
 
 def join_kernel(nb_vmem, placed_hbm, rest_ref, *refs):
-    strips, (out_hbm, nb_ref, strip_ref, done_ref, sem, nb_sem) = refs[:-6], refs[-6:]
-    nb_copy = pltpu.make_async_copy(nb_vmem, nb_ref, nb_sem.at[0])
-    nb_copy.start()
+    strips, (out_hbm, strip_ref, done_ref, sem) = refs[:-4], refs[-4:]
+    nb = nb_vmem[...].astype(jnp.float32)
+    at = iota(nb.shape, 0) * nb.shape[1] + iota(nb.shape, 1)
+    number = lambda slot, k: jnp.sum(jnp.where(at == slot * nb.shape[1] + k, nb, 0.0)).astype(jnp.int32)
     _, t_dev, _, n_out, run = rest_ref.shape
     n_rows = n_out * t_dev
     for i, ref in enumerate(strips):
         strip_ref[i] = ref[...].reshape(strip_ref.shape[1:])
     upper = iota((n_rows, 2 * STRIP), 1) >= STRIP
     quarter = (0.25 * placing(n_out, t_dev)).astype(jnp.bfloat16)
-    n_nb = nb_ref.shape[1] // 2
-    nb_copy.wait()
+    n_nb = nb.shape[1] // 2
     copies = []
     for slot in range(2):
         blend = jnp.zeros((n_rows, 2 * STRIP), jnp.float32)
         for k in range(n_nb):
-            strip = strip_ref[nb_ref[slot, k], :, nb_ref[slot, n_nb + k]].reshape(n_rows, 2 * STRIP)
+            strip = strip_ref[number(slot, k), :, number(slot, n_nb + k)].reshape(n_rows, 2 * STRIP)
             blend += jnp.dot(quarter, strip, preferred_element_type=jnp.float32)
         for i, part in enumerate((pltpu.roll(blend, STRIP, 1), blend)):
             part = jnp.where(upper, part, 0.0).reshape(t_dev, n_out, run)
@@ -396,11 +396,9 @@
         in_specs=[vmem(), pl.BlockSpec(memory_space=pltpu.HBM)] + [vmem()] * (1 + len(strips)),
         out_specs=pl.BlockSpec(memory_space=pltpu.HBM),
         scratch_shapes=[
-            pltpu.SMEM(sources.shape, jnp.int32),
             pltpu.VMEM((len(strips), n_out, 2, t_dev, 2 * STRIP), jnp.bfloat16),
             pltpu.VMEM(rest.shape, jnp.float32),
             pltpu.SemaphoreType.DMA((2, 2)),
-            pltpu.SemaphoreType.DMA((1,)),
         ],
         input_output_aliases={1: 0},
         compiler_params=pltpu.CompilerParams(vmem_limit_bytes=16 * MIB),

time: 113 us -> 113 us (level)
  no operation moved by 1% of the time
where the time goes in v12:
time: 113 us
  blocking collectives  89.3 us (79%)
  Pallas kernels  11.4 us (10%)
  starting transfers between devices  10.9 us (10%)
    all_to_all x3, blocking collectives, exchange(): return lax.all_to_all(x, axis, split_axis=0, concat_axis=0, tiled=True)  89.3 us
    ppermute x4, starting transfers between devices, local(): lax.ppermute(x, 'facet', [(f, f ^ 1) for f in range(n_facet)])  6.38 us
    ppermute x3, starting transfers between devices, local(): lax.ppermute(x, 'facet', [(f, (f + 2 * dz) % n_facet) for f in range(n_fa...  4.56 us
    pallas_call x1, Pallas kernels, grid_rows(): pl.pallas_call(functools.partial(grid_kernel, n_pieces), out_shape=jax.Sh...  4 us
    pallas_call x1, Pallas kernels, send_order(): pl.pallas_call(functools.partial(send_kernel, n_planes, t_dev), out_shape...  3.04 us
  transfers between devices with their start and end apart: 7, of which 2 were waited for; matrix products, arithmetic and copies ran while one was open for 0% of the time, Pallas kernels for 1%

profile of v12, /device:TPU:1, one launch (start us, length us, event | category | flops | bytes accessed | tf_op | source)
XLA Modules:
  0.0 112.9 jit_solution(12110633917995378047)
XLA Ops:
  0.0 0.0 copy-start
  0.0 3.0 %send_order.1 = (bf16[128,2,64,128]{3,2,1,0:T(8,128)(2,1)S(1)}, f32[7,2,64,128]{3,2,1,0:T(8,128)S(1)}, f32[16,2,64,128]{3,2,1,0:T(8,128)S(1)}, s32[1,1024]{1,0:T...) custom-call(s32[2]{0:T(128)} %refs_0_.1, s32[2,512]{1,0:T(2,128)} %refs_1_.1, s32[2,512]{1,0:T(2,128)} %refs_2_.1, ...), custom_call_target="tpu_custom_call" | custom-call | tf_op jit(solution)/shard_map/send_order/pallas_call | solution.py:164
  3.1 64.0 %all_to_all.15.vis_ref = bf16[128,2,64,128]{3,2,1,0:T(8,128)(2,1)S(1)} all-to-all(bf16[128,2,64,128]{3,2,1,0:T(8,128)(2,1)S(1)} %get-tuple-element.18), channel_id=1, replica_groups=mesh['facet'=8,'chan'=16] {'facet','chan'}, dimensions={0} | all-to-all | bytes 8388608 | tf_op jit(solution)/shard_map/all_to_all | solution.py:410
  67.0 0.0 slice-start
  67.0 0.0 slice-start.1
  67.0 1.4 %average.1 = bf16[16,2,64,128]{3,2,1,0:T(8,128)(2,1)S(1)} custom-call(f32[7,2,64,128]{3,2,1,0:T(8,128)S(1)} %get-tuple-element.16.inner_ref, f32[16,2,64,128]{3,2,1,0:T(8,128)S(1)} %get-tuple-element.17.outer_ref, bf16[128,2,64,128]{3,2,1,0:T(8,128)(2,1)S(1)} %all_to_all.15.vis_ref), custom_call_target="tpu_custom_call" | custom-call | flops 5662310400 | bytes 1572864000 | tf_op jit(solution)/shard_map/average/pallas_call | solution.py:234
  68.5 12.2 %all_to_all.16.refs_1_ = bf16[16,2,64,128]{3,2,1,0:T(8,128)(2,1)S(1)} all-to-all(bf16[16,2,64,128]{3,2,1,0:T(8,128)(2,1)S(1)} %average.1), channel_id=1, replica_groups=mesh['facet'=8,'chan'=16] {'chan'}, dimensions={0} | all-to-all | bytes 1048576 | tf_op jit(solution)/shard_map/all_to_all | solution.py:410
  80.6 0.0 slice-done
  80.6 0.0 slice-done.1
  80.6 4.0 %grid_rows.1 = bf16[16,32,512]{2,1,0:T(8,128)(2,1)S(1)} custom-call(s32[8,128]{1,0:T(8,128)S(1)} %get-tuple-element.15.refs_0_, bf16[16,2,64,128]{3,2,1,0:T(8,128)(2,1)S(1)} %all_to_all.16.refs_1_, s32[1,1024]{1,0:T(1,128)S(1)} %get-tuple-element.19.refs_2_, s32[1,1536]{1,0:T(1,128)S(1)} %get-tuple-element.20.refs_3_, bf16[32,256,512]{2,1,0:T(8,128)(2,1)S(1)} %bitcast.3), custom_call_target="tpu_custom_call" | custom-call | tf_op jit(solution)/shard_map/grid_rows/pallas_call | solution.py:280
  84.6 13.2 %all_to_all.17.main_ref = bf16[16,32,512]{2,1,0:T(8,128)(2,1)S(1)} all-to-all(bf16[16,32,512]{2,1,0:T(8,128)(2,1)S(1)} %grid_rows.1), channel_id=1, replica_groups=mesh['facet'=8,'chan'=16] {'chan'}, dimensions={0} | all-to-all | bytes 1048576 | tf_op jit(solution)/shard_map/all_to_all | solution.py:410
  97.8 0.1 strips.1.refs_0_
  98.0 1.8 %collective-permute-start.1 = (bf16[16,32,128]{2,1,0:T(8,128)(2,1)S(1)}, bf16[16,32,128]{2,1,0:T(8,128)(2,1)S(1)}, u32[]{:S(2)}, u32[]{:S(2)}) collective-permute-start(bf16[16,32,128]{2,1,0:T(8,128)(2,1)S(1)} %strips.1.refs_0_), channel_id=1, source_target_pairs={{0,64},{16,80},{32,96},{48,112},{64,0},{80,16},{96,32},{112,48},{1... | collective-permute-start | bytes 393224 | tf_op jit(solution)/shard_map/ppermute | solution.py:435
  99.8 0.0 collective-permute-start
  99.8 1.1 place.1
  100.9 2.7 %collective-permute-start.2 = (bf16[16,32,128]{2,1,0:T(8,128)(2,1)S(1)}, bf16[16,32,128]{2,1,0:T(8,128)(2,1)S(1)}, u32[]{:S(2)}, u32[]{:S(2)}) collective-permute-start(bf16[16,32,128]{2,1,0:T(8,128)(2,1)S(1)} %strips.1.refs_0_), channel_id=1, source_target_pairs={{0,96},{16,112},{32,0},{48,16},{64,32},{80,48},{96,64},{112,80},{1... | collective-permute-start | bytes 393224 | tf_op jit(solution)/shard_map/ppermute | solution.py:435
  103.6 0.0 copy-done
  103.6 0.1 constant_dynamic-slice_fusion
  103.7 0.1 copy.10
  103.8 4.0 %collective-permute-start.3 = (bf16[16,32,128]{2,1,0:T(8,128)(2,1)S(1)}, bf16[16,32,128]{2,1,0:T(8,128)(2,1)S(1)}, u32[]{:S(2)}, u32[]{:S(2)}) collective-permute-start(bf16[16,32,128]{2,1,0:T(8,128)(2,1)S(1)} %strips.1.refs_0_), channel_id=1, source_target_pairs={{0,16},{16,0},{32,48},{48,32},{64,80},{80,64},{96,112},{112,96},{1... | collective-permute-start | bytes 393224 | tf_op jit(solution)/shard_map/ppermute | solution.py:436
  107.8 0.0 collective-permute-done.1.refs_2_
  107.8 0.3 collective-permute-start.5
  108.2 0.0 collective-permute-done.refs_1_
  108.2 1.4 %collective-permute-start.4 = (bf16[16,32,128]{2,1,0:T(8,128)(2,1)S(1)}, bf16[16,32,128]{2,1,0:T(8,128)(2,1)S(1)}, u32[]{:S(2)}, u32[]{:S(2)}) collective-permute-start(bf16[16,32,128]{2,1,0:T(8,128)(2,1)S(1)} %collective-permute-done.refs_1_), channel_id=1, source_target_pairs={{0,16},{16,0},{32,48},{48,32},{64,80},{80,64},{96,112},{112,96},{1... | collective-permute-start | bytes 393224 | tf_op jit(solution)/shard_map/ppermute | solution.py:436
  109.5 0.0 collective-permute-done.2.refs_3_
  109.5 0.6 collective-permute-start.6
  110.2 0.1 pad_add_fusion.nb_vmem
  110.3 0.0 collective-permute-done.3.refs_4_
  110.3 0.0 collective-permute-done.5.refs_6_
  110.3 0.2 collective-permute-done.4.refs_5_
  110.5 0.6 collective-permute-done.6.refs_7_
  111.2 1.7 %join.1 = f32[16,2,16,512]{3,2,1,0:T(8,128)} custom-call(s32[2,8]{1,0:T(2,128)S(1)} %pad_add_fusion.nb_vmem, f32[16,2,16,512]{3,2,1,0:T(8,128)} %get-tuple-element.21.placed_hbm, f32[2,16,2,16,128]{4,3,2,1,0:T(8,128)S(1)} %get-tuple-element.23.rest_ref, bf16[16,32,128]{2,1,0:T(8,128)(2,1)S(1)} %strips.1.refs_0_, ...), custom_call_target="tpu_custom_call", output_to_operand_aliasing={{}: (1, {})} | custom-call | tf_op jit(solution)/shard_map/join/pallas_call | solution.py:393
  (2 shorter events, 0.0 us)
Async XLA Ops:
  0.0 103.6 %copy-start = (s32[16,4]{0,1:T(4,128)S(1)}, s32[16,4]{0,1:T(4,128)}, u32[]{:S(2)}) copy-start(s32[16,4]{0,1:T(4,128)} %param.13) | copy-start | bytes 772
  67.0 13.6 %slice-start = ((s8[8388608]{0:T(1024)(128)(4,1)}), s8[4194304]{0:T(1024)(128)(4,1)S(1)}, s32[]{:S(2)}) async-start(s8[8388608]{0:T(1024)(128)(4,1)} %bitcast.2), calls=%async_computation.3 | async-start | bytes 8388608
  67.0 13.6 %slice-start.1 = ((s8[8388608]{0:T(1024)(128)(4,1)}), s8[4194304]{0:T(1024)(128)(4,1)S(1)}, s32[]{:S(2)}) async-start(s8[8388608]{0:T(1024)(128)(4,1)} %bitcast.2), calls=%async_computation.4 | async-start | bytes 8388608
  98.0 9.9 %collective-permute-start.1 = (bf16[16,32,128]{2,1,0:T(8,128)(2,1)S(1)}, bf16[16,32,128]{2,1,0:T(8,128)(2,1)S(1)}, u32[]{:S(2)}, u32[]{:S(2)}) collective-permute-start(bf16[16,32,128]{2,1,0:T(8,128)(2,1)S(1)} %strips.1.refs_0_), channel_id=1, source_target_pairs={{0,64},{16,80},{32,96},{48,112},{64,0},{80,16},{96,32},{112,48},{1... | collective-permute-start | bytes 393224 | tf_op jit(solution)/shard_map/ppermute | solution.py:435
  99.8 8.4 %collective-permute-start = (bf16[16,32,128]{2,1,0:T(8,128)(2,1)S(1)}, bf16[16,32,128]{2,1,0:T(8,128)(2,1)S(1)}, u32[]{:S(2)}, u32[]{:S(2)}) collective-permute-start(bf16[16,32,128]{2,1,0:T(8,128)(2,1)S(1)} %strips.1.refs_0_), channel_id=1, source_target_pairs={{0,32},{16,48},{32,64},{48,80},{64,96},{80,112},{96,0},{112,16},{1... | collective-permute-start | bytes 393224 | tf_op jit(solution)/shard_map/ppermute | solution.py:435
  100.9 8.7 %collective-permute-start.2 = (bf16[16,32,128]{2,1,0:T(8,128)(2,1)S(1)}, bf16[16,32,128]{2,1,0:T(8,128)(2,1)S(1)}, u32[]{:S(2)}, u32[]{:S(2)}) collective-permute-start(bf16[16,32,128]{2,1,0:T(8,128)(2,1)S(1)} %strips.1.refs_0_), channel_id=1, source_target_pairs={{0,96},{16,112},{32,0},{48,16},{64,32},{80,48},{96,64},{112,80},{1... | collective-permute-start | bytes 393224 | tf_op jit(solution)/shard_map/ppermute | solution.py:435
  103.8 6.5 %collective-permute-start.3 = (bf16[16,32,128]{2,1,0:T(8,128)(2,1)S(1)}, bf16[16,32,128]{2,1,0:T(8,128)(2,1)S(1)}, u32[]{:S(2)}, u32[]{:S(2)}) collective-permute-start(bf16[16,32,128]{2,1,0:T(8,128)(2,1)S(1)} %strips.1.refs_0_), channel_id=1, source_target_pairs={{0,16},{16,0},{32,48},{48,32},{64,80},{80,64},{96,112},{112,96},{1... | collective-permute-start | bytes 393224 | tf_op jit(solution)/shard_map/ppermute | solution.py:436
  107.8 2.5 %collective-permute-start.5 = (bf16[16,32,128]{2,1,0:T(8,128)(2,1)S(1)}, bf16[16,32,128]{2,1,0:T(8,128)(2,1)S(1)}, u32[]{:S(2)}, u32[]{:S(2)}) collective-permute-start(bf16[16,32,128]{2,1,0:T(8,128)(2,1)S(1)} %collective-permute-done.1.refs_2_), channel_id=1, source_target_pairs={{0,16},{16,0},{32,48},{48,32},{64,80},{80,64},{96,112},{112,96},{1... | collective-permute-start | bytes 393224 | tf_op jit(solution)/shard_map/ppermute | solution.py:436
  108.2 2.4 %collective-permute-start.4 = (bf16[16,32,128]{2,1,0:T(8,128)(2,1)S(1)}, bf16[16,32,128]{2,1,0:T(8,128)(2,1)S(1)}, u32[]{:S(2)}, u32[]{:S(2)}) collective-permute-start(bf16[16,32,128]{2,1,0:T(8,128)(2,1)S(1)} %collective-permute-done.refs_1_), channel_id=1, source_target_pairs={{0,16},{16,0},{32,48},{48,32},{64,80},{80,64},{96,112},{112,96},{1... | collective-permute-start | bytes 393224 | tf_op jit(solution)/shard_map/ppermute | solution.py:436
  109.5 1.6 %collective-permute-start.6 = (bf16[16,32,128]{2,1,0:T(8,128)(2,1)S(1)}, bf16[16,32,128]{2,1,0:T(8,128)(2,1)S(1)}, u32[]{:S(2)}, u32[]{:S(2)}) collective-permute-start(bf16[16,32,128]{2,1,0:T(8,128)(2,1)S(1)} %collective-permute-done.2.refs_3_), channel_id=1, source_target_pairs={{0,16},{16,0},{32,48},{48,32},{64,80},{80,64},{96,112},{112,96},{1... | collective-permute-start | bytes 393224 | tf_op jit(solution)/shard_map/ppermute | solution.py:436

commit v13 on v12

--- a/solution.py
+++ b/solution.py
@@ -434,10 +434,10 @@
     chips = n_facet // 2
     along = lambda x, dz: lax.ppermute(x, "facet", [(f, (f + 2 * dz) % n_facet) for f in range(n_facet)])
     across = lambda x: lax.ppermute(x, "facet", [(f, f ^ 1) for f in range(n_facet)])
-    arrived = {dz: along(own, dz) for dz in range(1, chips - 1)}
+    arrived = {dz: along(own, dz) for dz in range(2, chips)}
     placed, rest = place_main(main)
     own, rest = lax.optimization_barrier((own, rest))
-    arrived[chips - 1] = along(own, chips - 1)
+    arrived[1] = along(own, 1)
     strips = [own] + [arrived[dz] for dz in range(1, chips)]
     strips += [across(s) for s in strips]
     mine = lax.dynamic_slice_in_dim(neighbours, facet_index * fac_dev, fac_dev, 0)

time: 113 us -> 115 us (1.018)
  starting transfers between devices: 10.9 us -> 12.4 us
    ppermute x4, starting transfers between devices: 6.38 us -> 9.65 us  [local(): lax.ppermute(x, 'facet', [(f, f ^ 1) for f in range(n_facet)])]
    ppermute x3, starting transfers between devices: 4.56 us -> 2.74 us  [local(): lax.ppermute(x, 'facet', [(f, (f + 2 * dz) % n_facet) for f in range(n_fa...]
  transfers between devices with their start and end apart: 7 -> 7, of which waited for: 2 -> 1; matrix products, arithmetic and copies ran while one was open for 0% -> 0% of each run, Pallas kernels for 1% -> 1%
where the time goes in v13:
time: 115 us; the launch traced here: 114 us
  blocking collectives  89.3 us (78%)
  starting transfers between devices  12.4 us (11%)
  Pallas kernels  11.4 us (10%)
    all_to_all x3, blocking collectives, exchange(): return lax.all_to_all(x, axis, split_axis=0, concat_axis=0, tiled=True)  89.3 us
    ppermute x4, starting transfers between devices, local(): lax.ppermute(x, 'facet', [(f, f ^ 1) for f in range(n_facet)])  9.65 us
    pallas_call x1, Pallas kernels, grid_rows(): pl.pallas_call(functools.partial(grid_kernel, n_pieces), out_shape=jax.Sh...  4 us
    pallas_call x1, Pallas kernels, send_order(): pl.pallas_call(functools.partial(send_kernel, n_planes, t_dev), out_shape...  3.04 us
    ppermute x3, starting transfers between devices, local(): lax.ppermute(x, 'facet', [(f, (f + 2 * dz) % n_facet) for f in range(n_fa...  2.74 us
  transfers between devices with their start and end apart: 7, of which 1 were waited for; matrix products, arithmetic and copies ran while one was open for 0% of the time, Pallas kernels for 1%

profile of v13, /device:TPU:1, one launch (start us, length us, event | category | flops | bytes accessed | tf_op | source)
XLA Modules:
  0.0 114.3 jit_solution(5546719967351775737)
XLA Ops:
  0.0 0.0 copy-start
  0.0 3.0 %send_order.1 = (bf16[128,2,64,128]{3,2,1,0:T(8,128)(2,1)S(1)}, f32[7,2,64,128]{3,2,1,0:T(8,128)S(1)}, f32[16,2,64,128]{3,2,1,0:T(8,128)S(1)}, s32[1,1024]{1,0:T...) custom-call(s32[2]{0:T(128)} %refs_0_.1, s32[2,512]{1,0:T(2,128)} %refs_1_.1, s32[2,512]{1,0:T(2,128)} %refs_2_.1, ...), custom_call_target="tpu_custom_call" | custom-call | tf_op jit(solution)/shard_map/send_order/pallas_call | solution.py:164
  3.1 64.0 %all_to_all.15.vis_ref = bf16[128,2,64,128]{3,2,1,0:T(8,128)(2,1)S(1)} all-to-all(bf16[128,2,64,128]{3,2,1,0:T(8,128)(2,1)S(1)} %get-tuple-element.18), channel_id=1, replica_groups=mesh['facet'=8,'chan'=16] {'facet','chan'}, dimensions={0} | all-to-all | bytes 8388608 | tf_op jit(solution)/shard_map/all_to_all | solution.py:410
  67.0 0.0 slice-start
  67.0 0.0 slice-start.1
  67.0 1.4 %average.1 = bf16[16,2,64,128]{3,2,1,0:T(8,128)(2,1)S(1)} custom-call(f32[7,2,64,128]{3,2,1,0:T(8,128)S(1)} %get-tuple-element.16.inner_ref, f32[16,2,64,128]{3,2,1,0:T(8,128)S(1)} %get-tuple-element.17.outer_ref, bf16[128,2,64,128]{3,2,1,0:T(8,128)(2,1)S(1)} %all_to_all.15.vis_ref), custom_call_target="tpu_custom_call" | custom-call | flops 5662310400 | bytes 1572864000 | tf_op jit(solution)/shard_map/average/pallas_call | solution.py:234
  68.5 12.2 %all_to_all.16.refs_1_ = bf16[16,2,64,128]{3,2,1,0:T(8,128)(2,1)S(1)} all-to-all(bf16[16,2,64,128]{3,2,1,0:T(8,128)(2,1)S(1)} %average.1), channel_id=1, replica_groups=mesh['facet'=8,'chan'=16] {'chan'}, dimensions={0} | all-to-all | bytes 1048576 | tf_op jit(solution)/shard_map/all_to_all | solution.py:410
  80.6 0.0 slice-done
  80.6 0.0 slice-done.1
  80.6 4.0 %grid_rows.1 = bf16[16,32,512]{2,1,0:T(8,128)(2,1)S(1)} custom-call(s32[8,128]{1,0:T(8,128)S(1)} %get-tuple-element.15.refs_0_, bf16[16,2,64,128]{3,2,1,0:T(8,128)(2,1)S(1)} %all_to_all.16.refs_1_, s32[1,1024]{1,0:T(1,128)S(1)} %get-tuple-element.19.refs_2_, s32[1,1536]{1,0:T(1,128)S(1)} %get-tuple-element.20.refs_3_, bf16[32,256,512]{2,1,0:T(8,128)(2,1)S(1)} %bitcast.3), custom_call_target="tpu_custom_call" | custom-call | tf_op jit(solution)/shard_map/grid_rows/pallas_call | solution.py:280
  84.6 13.2 %all_to_all.17.main_ref = bf16[16,32,512]{2,1,0:T(8,128)(2,1)S(1)} all-to-all(bf16[16,32,512]{2,1,0:T(8,128)(2,1)S(1)} %grid_rows.1), channel_id=1, replica_groups=mesh['facet'=8,'chan'=16] {'chan'}, dimensions={0} | all-to-all | bytes 1048576 | tf_op jit(solution)/shard_map/all_to_all | solution.py:410
  97.8 0.1 strips.1.refs_0_
  98.0 0.5 collective-permute-start.2
  98.4 2.1 %collective-permute-start.1 = (bf16[16,32,128]{2,1,0:T(8,128)(2,1)S(1)}, bf16[16,32,128]{2,1,0:T(8,128)(2,1)S(1)}, u32[]{:S(2)}, u32[]{:S(2)}) collective-permute-start(bf16[16,32,128]{2,1,0:T(8,128)(2,1)S(1)} %strips.1.refs_0_), channel_id=1, source_target_pairs={{0,64},{16,80},{32,96},{48,112},{64,0},{80,16},{96,32},{112,48},{1... | collective-permute-start | bytes 393224 | tf_op jit(solution)/shard_map/ppermute | solution.py:435
  100.5 1.1 place.1
  101.6 0.2 collective-permute-start
  101.8 0.0 copy-done
  101.8 0.1 constant_dynamic-slice_fusion
  101.9 0.1 copy.10
  102.0 4.0 %collective-permute-start.3 = (bf16[16,32,128]{2,1,0:T(8,128)(2,1)S(1)}, bf16[16,32,128]{2,1,0:T(8,128)(2,1)S(1)}, u32[]{:S(2)}, u32[]{:S(2)}) collective-permute-start(bf16[16,32,128]{2,1,0:T(8,128)(2,1)S(1)} %strips.1.refs_0_), channel_id=1, source_target_pairs={{0,16},{16,0},{32,48},{48,32},{64,80},{80,64},{96,112},{112,96},{1... | collective-permute-start | bytes 393224 | tf_op jit(solution)/shard_map/ppermute | solution.py:436
  106.0 0.0 collective-permute-done.2.refs_3_
  106.0 0.6 collective-permute-start.6
  106.6 0.0 collective-permute-done.1.refs_2_
  106.6 2.1 %collective-permute-start.5 = (bf16[16,32,128]{2,1,0:T(8,128)(2,1)S(1)}, bf16[16,32,128]{2,1,0:T(8,128)(2,1)S(1)}, u32[]{:S(2)}, u32[]{:S(2)}) collective-permute-start(bf16[16,32,128]{2,1,0:T(8,128)(2,1)S(1)} %collective-permute-done.1.refs_2_), channel_id=1, source_target_pairs={{0,16},{16,0},{32,48},{48,32},{64,80},{80,64},{96,112},{112,96},{1... | collective-permute-start | bytes 393224 | tf_op jit(solution)/shard_map/ppermute | solution.py:436
  108.8 0.0 collective-permute-done.refs_1_
  108.8 2.9 %collective-permute-start.4 = (bf16[16,32,128]{2,1,0:T(8,128)(2,1)S(1)}, bf16[16,32,128]{2,1,0:T(8,128)(2,1)S(1)}, u32[]{:S(2)}, u32[]{:S(2)}) collective-permute-start(bf16[16,32,128]{2,1,0:T(8,128)(2,1)S(1)} %collective-permute-done.refs_1_), channel_id=1, source_target_pairs={{0,16},{16,0},{32,48},{48,32},{64,80},{80,64},{96,112},{112,96},{1... | collective-permute-start | bytes 393224 | tf_op jit(solution)/shard_map/ppermute | solution.py:436
  111.7 0.1 pad_add_fusion.nb_vmem
  111.7 0.0 collective-permute-done.3.refs_4_
  111.7 0.0 collective-permute-done.6.refs_7_
  111.7 0.0 collective-permute-done.5.refs_6_
  111.8 0.9 collective-permute-done.4.refs_5_
  112.6 1.7 %join.1 = f32[16,2,16,512]{3,2,1,0:T(8,128)} custom-call(s32[2,8]{1,0:T(2,128)S(1)} %pad_add_fusion.nb_vmem, f32[16,2,16,512]{3,2,1,0:T(8,128)} %get-tuple-element.21.placed_hbm, f32[2,16,2,16,128]{4,3,2,1,0:T(8,128)S(1)} %get-tuple-element.23.rest_ref, bf16[16,32,128]{2,1,0:T(8,128)(2,1)S(1)} %strips.1.refs_0_, ...), custom_call_target="tpu_custom_call", output_to_operand_aliasing={{}: (1, {})} | custom-call | tf_op jit(solution)/shard_map/join/pallas_call | solution.py:393
  (2 shorter events, 0.0 us)
Async XLA Ops:
  0.0 101.8 %copy-start = (s32[16,4]{0,1:T(4,128)S(1)}, s32[16,4]{0,1:T(4,128)}, u32[]{:S(2)}) copy-start(s32[16,4]{0,1:T(4,128)} %param.13) | copy-start | bytes 772
  67.0 13.6 %slice-start = ((s8[8388608]{0:T(1024)(128)(4,1)}), s8[4194304]{0:T(1024)(128)(4,1)S(1)}, s32[]{:S(2)}) async-start(s8[8388608]{0:T(1024)(128)(4,1)} %bitcast.2), calls=%async_computation.3 | async-start | bytes 8388608
  67.0 13.6 %slice-start.1 = ((s8[8388608]{0:T(1024)(128)(4,1)}), s8[4194304]{0:T(1024)(128)(4,1)S(1)}, s32[]{:S(2)}) async-start(s8[8388608]{0:T(1024)(128)(4,1)} %bitcast.2), calls=%async_computation.4 | async-start | bytes 8388608
  98.0 8.1 %collective-permute-start.2 = (bf16[16,32,128]{2,1,0:T(8,128)(2,1)S(1)}, bf16[16,32,128]{2,1,0:T(8,128)(2,1)S(1)}, u32[]{:S(2)}, u32[]{:S(2)}) collective-permute-start(bf16[16,32,128]{2,1,0:T(8,128)(2,1)S(1)} %strips.1.refs_0_), channel_id=1, source_target_pairs={{0,96},{16,112},{32,0},{48,16},{64,32},{80,48},{96,64},{112,80},{1... | collective-permute-start | bytes 393224 | tf_op jit(solution)/shard_map/ppermute | solution.py:435
  98.4 8.2 %collective-permute-start.1 = (bf16[16,32,128]{2,1,0:T(8,128)(2,1)S(1)}, bf16[16,32,128]{2,1,0:T(8,128)(2,1)S(1)}, u32[]{:S(2)}, u32[]{:S(2)}) collective-permute-start(bf16[16,32,128]{2,1,0:T(8,128)(2,1)S(1)} %strips.1.refs_0_), channel_id=1, source_target_pairs={{0,64},{16,80},{32,96},{48,112},{64,0},{80,16},{96,32},{112,48},{1... | collective-permute-start | bytes 393224 | tf_op jit(solution)/shard_map/ppermute | solution.py:435
  101.6 7.2 %collective-permute-start = (bf16[16,32,128]{2,1,0:T(8,128)(2,1)S(1)}, bf16[16,32,128]{2,1,0:T(8,128)(2,1)S(1)}, u32[]{:S(2)}, u32[]{:S(2)}) collective-permute-start(bf16[16,32,128]{2,1,0:T(8,128)(2,1)S(1)} %strips.1.refs_0_), channel_id=1, source_target_pairs={{0,32},{16,48},{32,64},{48,80},{64,96},{80,112},{96,0},{112,16},{1... | collective-permute-start | bytes 393224 | tf_op jit(solution)/shard_map/ppermute | solution.py:435
  102.0 9.8 %collective-permute-start.3 = (bf16[16,32,128]{2,1,0:T(8,128)(2,1)S(1)}, bf16[16,32,128]{2,1,0:T(8,128)(2,1)S(1)}, u32[]{:S(2)}, u32[]{:S(2)}) collective-permute-start(bf16[16,32,128]{2,1,0:T(8,128)(2,1)S(1)} %strips.1.refs_0_), channel_id=1, source_target_pairs={{0,16},{16,0},{32,48},{48,32},{64,80},{80,64},{96,112},{112,96},{1... | collective-permute-start | bytes 393224 | tf_op jit(solution)/shard_map/ppermute | solution.py:436
  106.0 5.7 %collective-permute-start.6 = (bf16[16,32,128]{2,1,0:T(8,128)(2,1)S(1)}, bf16[16,32,128]{2,1,0:T(8,128)(2,1)S(1)}, u32[]{:S(2)}, u32[]{:S(2)}) collective-permute-start(bf16[16,32,128]{2,1,0:T(8,128)(2,1)S(1)} %collective-permute-done.2.refs_3_), channel_id=1, source_target_pairs={{0,16},{16,0},{32,48},{48,32},{64,80},{80,64},{96,112},{112,96},{1... | collective-permute-start | bytes 393224 | tf_op jit(solution)/shard_map/ppermute | solution.py:436
  106.6 5.1 %collective-permute-start.5 = (bf16[16,32,128]{2,1,0:T(8,128)(2,1)S(1)}, bf16[16,32,128]{2,1,0:T(8,128)(2,1)S(1)}, u32[]{:S(2)}, u32[]{:S(2)}) collective-permute-start(bf16[16,32,128]{2,1,0:T(8,128)(2,1)S(1)} %collective-permute-done.1.refs_2_), channel_id=1, source_target_pairs={{0,16},{16,0},{32,48},{48,32},{64,80},{80,64},{96,112},{112,96},{1... | collective-permute-start | bytes 393224 | tf_op jit(solution)/shard_map/ppermute | solution.py:436
  108.8 3.8 %collective-permute-start.4 = (bf16[16,32,128]{2,1,0:T(8,128)(2,1)S(1)}, bf16[16,32,128]{2,1,0:T(8,128)(2,1)S(1)}, u32[]{:S(2)}, u32[]{:S(2)}) collective-permute-start(bf16[16,32,128]{2,1,0:T(8,128)(2,1)S(1)} %collective-permute-done.refs_1_), channel_id=1, source_target_pairs={{0,16},{16,0},{32,48},{48,32},{64,80},{80,64},{96,112},{112,96},{1... | collective-permute-start | bytes 393224 | tf_op jit(solution)/shard_map/ppermute | solution.py:436
